TPU v7x, 32 devices: a whole 2x2x4 slice. The times are simulated.
32 devices in a mesh: fsdp: 4 (over z), heads: 2 (over core), tensor: 4 (over y, x).
Axes of the slice: x: 2, y: 2, z: 4, core: 2. Of those that a mesh axis runs over, the one named last changes fastest.
Arguments:
- block_input: bfloat16 [1536, 1536], P(('fsdp', 'heads')), may hold values from -6 to 6
- segments: int32 [1536], replicated, may hold values from 0 to 2, as said below
- routes: int32 [1536, 8], P(('fsdp', 'heads')), may hold values from 0 to 15, all different within a row
- attn_gain: bfloat16 [1536], P(('fsdp', 'heads')), may hold values from 0.5 to 1.5
- ffn_gain: bfloat16 [1536], P(('fsdp', 'heads')), may hold values from 0.5 to 1.5
- query_weight: bfloat16 [1536, 1536], P(('fsdp', 'heads')), may hold values from -0.4375 to 0.4375
- key_matrix: bfloat16 [1536, 512], P(('fsdp', 'heads')), may hold values from -0.4375 to 0.4375
- value_matrix: bfloat16 [1536, 512], P(('fsdp', 'heads')), may hold values from -0.15625 to 0.15625
- out_weight: bfloat16 [1536, 1536], P(('fsdp', 'heads')), may hold values from -12 to 12
- router_weight: bfloat16 [1536, 16], P(('fsdp', 'heads')), may hold values from -0.3125 to 0.3125
- gate_weight: bfloat16 [16, 1536, 512], P(None, ('fsdp', 'heads'), 'tensor'), may hold values from -0.15625 to 0.15625
- up_weight: bfloat16 [16, 1536, 512], P(None, ('fsdp', 'heads'), 'tensor'), may hold values from -0.15625 to 0.15625
- down_weight: bfloat16 [16, 512, 1536], P(None, 'tensor', ('fsdp', 'heads')), may hold values from -1 to 1
- grad_output: float32 [1536, 1536], P(('fsdp', 'heads')), may hold values from -6 to 6
Outputs:
- block_output: float32 [1536, 1536], P(('fsdp', 'heads'), 'tensor')
- grad_input: float32 [1536, 1536], P(('fsdp', 'heads'))
- grad_attn_gain: float32 [1536], P(('fsdp', 'heads'))
- grad_ffn_gain: float32 [1536], P(('fsdp', 'heads'))
- grad_query: float32 [1536, 1536], P(('fsdp', 'heads'))
- grad_key: float32 [1536, 512], P(('fsdp', 'heads'))
- grad_value: float32 [1536, 512], P(('fsdp', 'heads'))
- grad_out_proj: float32 [1536, 1536], P(('fsdp', 'heads'))
- grad_router: float32 [1536, 16], P(('fsdp', 'heads'))
- grad_gate: float32 [16, 1536, 512], P(None, ('fsdp', 'heads'), 'tensor')
- grad_up: float32 [16, 1536, 512], P(None, ('fsdp', 'heads'), 'tensor')
- grad_down: float32 [16, 512, 1536], P(None, 'tensor', ('fsdp', 'heads'))
Inputs may be any that keep to these rules, and one draw needn't show every extreme that they name: `segments`: segment numbers start at 0 and rise by one at each document's start; there are 3 documents, each of 96 to 960 tokens, and the first has exactly 960. `routes`: each token names 8 different experts; every expert is named by some token.
All inputs are finite; a program needn't handle non-finite values.
Results may differ from a plain program's by a relative error of at most 0.017.
Values may be sent and summed in bfloat16 or wider, within the bound.
A program may use at most 256 MiB of HBM per device.

v0:
```python
import math

import jax
import jax.numpy as jnp
from jax import lax
from jax.sharding import PartitionSpec as P

QUERY_HEADS = 24
KEY_VALUE_HEADS = 8
HEAD_DIM = 64
E = 16


norm_eps = 1e-06
score_scale = 0.015625
residual_scale = 0.22
rope_base = 10000.0


def rotary_table(token_positions, head_size):
    half_size = head_size // 2
    inverse = rope_base ** (-(jnp.arange(half_size, dtype=jnp.float32) * 2.0 / head_size))
    angles = token_positions[:, None].astype(jnp.float32) * inverse[None, :]
    return (jnp.cos(angles)[:, None, :], jnp.sin(angles)[:, None, :])


def apply_rotary(vectors, cosine_lookup, sine_lookup):
    half_size = vectors.shape[-1] // 2
    first_half = vectors[..., :half_size]
    second_half = vectors[..., half_size:]
    return jnp.concatenate(
        [
            first_half * cosine_lookup - second_half * sine_lookup,
            second_half * cosine_lookup + first_half * sine_lookup,
        ],
        axis=-1,
    )


def reverse_rotary(gradient, cosine_lookup, sine_lookup):
    half_size = gradient.shape[-1] // 2
    first_half = gradient[..., :half_size]
    second_half = gradient[..., half_size:]
    return jnp.concatenate(
        [
            first_half * cosine_lookup + second_half * sine_lookup,
            second_half * cosine_lookup - first_half * sine_lookup,
        ],
        axis=-1,
    )


def body(
    block_input,
    segments,
    routes,
    attn_gain,
    ffn_gain,
    query_weight,
    key_matrix,
    value_matrix,
    out_weight,
    router_weight,
    gate_weight,
    up_weight,
    down_weight,
    grad_output,
):
    head_count = lax.axis_size("heads")
    n_tensor = lax.axis_size("tensor")
    n_fsdp = lax.axis_size("fsdp")
    fsdp_index = lax.axis_index("fsdp")
    heads_index = lax.axis_index("heads")
    tensor_index = lax.axis_index("tensor")
    token_rows = block_input.shape[0]
    model_width = block_input.shape[1]
    query_rows = token_rows * head_count
    seq_rows = query_rows * n_fsdp
    key_value_local = KEY_VALUE_HEADS // head_count
    heads_per_group = QUERY_HEADS // KEY_VALUE_HEADS
    slice_width = model_width // n_tensor
    gathered = (
        lax.all_gather(attn_gain, ("fsdp", "heads"), axis=0, tiled=True),
        lax.all_gather(ffn_gain, ("fsdp", "heads"), axis=0, tiled=True),
        lax.all_gather(query_weight, ("fsdp", "heads"), axis=0, tiled=True),
        lax.all_gather(key_matrix, ("fsdp", "heads"), axis=0, tiled=True),
        lax.all_gather(value_matrix, ("fsdp", "heads"), axis=0, tiled=True),
        lax.all_gather(out_weight, ("fsdp", "heads"), axis=0, tiled=True),
        lax.all_gather(router_weight, ("fsdp", "heads"), axis=0, tiled=True),
        lax.all_gather(gate_weight, ("fsdp", "heads"), axis=1, tiled=True),
        lax.all_gather(up_weight, ("fsdp", "heads"), axis=1, tiled=True),
        lax.all_gather(down_weight, ("fsdp", "heads"), axis=2, tiled=True),
    )
    gain_attn = gathered[0].astype(jnp.float32)
    gain_ffn = gathered[1].astype(jnp.float32)
    full_query, full_key, full_value, full_out, full_router, full_gate, full_up, full_down = (
        gathered[2:]
    )
    inputs = block_input.astype(jnp.float32)
    scale_one = lax.rsqrt(jnp.mean(inputs * inputs, axis=-1, keepdims=True) + norm_eps)
    unit_one = inputs * scale_one
    normalized_input = (unit_one * gain_attn).astype(jnp.bfloat16)
    query_lin = jnp.dot(normalized_input, full_query, preferred_element_type=jnp.float32)
    key_linear = jnp.dot(normalized_input, full_key, preferred_element_type=jnp.float32)
    value_lin = jnp.dot(normalized_input, full_value, preferred_element_type=jnp.float32)
    own_start = (fsdp_index * head_count + heads_index) * token_rows
    token_positions = own_start + jnp.arange(token_rows, dtype=jnp.int32)
    cosine_lookup, sine_lookup = rotary_table(token_positions, HEAD_DIM)
    query_send = (
        apply_rotary(
            query_lin.reshape(token_rows, QUERY_HEADS, HEAD_DIM), cosine_lookup, sine_lookup
        )
        .reshape(token_rows, QUERY_HEADS * HEAD_DIM)
        .astype(jnp.bfloat16)
    )
    key_send = (
        apply_rotary(
            key_linear.reshape(token_rows, KEY_VALUE_HEADS, HEAD_DIM), cosine_lookup, sine_lookup
        )
        .reshape(token_rows, KEY_VALUE_HEADS * HEAD_DIM)
        .astype(jnp.bfloat16)
    )
    value_send = value_lin.astype(jnp.bfloat16)
    query_heads, key_local, value_local = (
        lax.all_to_all(query_send, "heads", split_axis=1, concat_axis=0, tiled=True),
        lax.all_to_all(key_send, "heads", split_axis=1, concat_axis=0, tiled=True),
        lax.all_to_all(value_send, "heads", split_axis=1, concat_axis=0, tiled=True),
    )
    query_vectors = query_heads.reshape(query_rows, key_value_local, heads_per_group, HEAD_DIM)
    query_start = fsdp_index * query_rows
    query_pos = query_start + jnp.arange(query_rows, dtype=jnp.int32)
    query_seg = lax.dynamic_slice_in_dim(segments, query_start, query_rows, 0)

    def masked_exp(key_block, key_start):
        block_rows = key_block.shape[0]
        raw_scores = (
            jnp.einsum(
                "qkgd,jkd->kgqj", query_vectors, key_block, preferred_element_type=jnp.float32
            )
            * score_scale
        )
        key_pos = key_start + jnp.arange(block_rows, dtype=jnp.int32)
        key_seg = lax.dynamic_slice_in_dim(segments, key_start, block_rows, 0)
        allowed = (query_pos[:, None] >= key_pos[None, :]) & (
            query_seg[:, None] == key_seg[None, :]
        )
        return jnp.where(allowed[None, None], jnp.exp(raw_scores), 0.0)

    def split_blocks(key_piece):
        keys_piece, values_piece = key_piece
        piece_rows = keys_piece.shape[0]
        block_rows = math.gcd(piece_rows, query_rows)
        block_count = piece_rows // block_rows
        starts = jnp.arange(block_count, dtype=jnp.int32) * block_rows
        return (
            keys_piece.reshape(block_count, block_rows, key_value_local, HEAD_DIM),
            values_piece.reshape(block_count, block_rows, key_value_local, HEAD_DIM),
            starts,
        )

    start_state = (
        jnp.zeros((key_value_local, heads_per_group, query_rows), jnp.float32),
        jnp.zeros((key_value_local, heads_per_group, query_rows, HEAD_DIM), jnp.float32),
    )
    fold_state = start_state

    def block_step(running, block_item):
        denominator, numerator = running
        key_block, value_block, key_start = block_item
        weights = masked_exp(key_block, key_start)
        denominator = denominator + jnp.sum(weights, axis=-1)
        numerator = numerator + jnp.einsum(
            "kgqj,jkd->kgqd",
            weights.astype(jnp.bfloat16),
            value_block,
            preferred_element_type=jnp.float32,
        )
        return ((denominator, numerator), None)

    fold_state, _ = lax.scan(
        block_step,
        fold_state,
        split_blocks(
            (
                lax.all_gather(key_local, "fsdp", axis=0, tiled=True),
                lax.all_gather(value_local, "fsdp", axis=0, tiled=True),
            )
        ),
    )
    denominator, numerator = fold_state
    attn_full = numerator / denominator[..., None]
    attn_send = (
        attn_full.transpose(2, 0, 1, 3)
        .reshape(query_rows, key_value_local * heads_per_group * HEAD_DIM)
        .astype(jnp.bfloat16)
    )
    attn_back = lax.all_to_all(attn_send, "heads", split_axis=0, concat_axis=1, tiled=True)
    attn_proj = jnp.dot(attn_back, full_out, preferred_element_type=jnp.float32)
    hidden = inputs + residual_scale * attn_proj
    scale_two = lax.rsqrt(jnp.mean(hidden * hidden, axis=-1, keepdims=True) + norm_eps)
    unit_two = hidden * scale_two
    normed_two = (unit_two * gain_ffn).astype(jnp.bfloat16)
    logits = jnp.dot(normed_two, full_router, preferred_element_type=jnp.float32)
    onehot = (routes[:, :, None] == jnp.arange(E, dtype=jnp.int32)[None, None, :]).astype(
        jnp.float32
    )
    picked = jnp.sum(onehot * logits[:, None, :], axis=-1)
    route_probs = jax.nn.softmax(picked, axis=-1)
    combine = jnp.sum(onehot * route_probs[:, :, None], axis=1)
    gate_pre = jnp.einsum("td,edf->etf", normed_two, full_gate, preferred_element_type=jnp.float32)
    up_pre = jnp.einsum("td,edf->etf", normed_two, full_up, preferred_element_type=jnp.float32)
    sigmoid_gate = jax.nn.sigmoid(gate_pre)
    silu_gate = gate_pre * sigmoid_gate
    active = (silu_gate * up_pre).astype(jnp.bfloat16)
    expert_out = jnp.einsum("etf,efd->etd", active, full_down, preferred_element_type=jnp.float32)
    mixed_part = jnp.sum(combine.T[:, :, None] * expert_out, axis=0)
    mixed_sum = lax.psum_scatter(
        mixed_part.astype(jnp.bfloat16), "tensor", scatter_dimension=1, tiled=True
    ).astype(jnp.float32)
    hidden_mine = lax.dynamic_slice_in_dim(hidden, tensor_index * slice_width, slice_width, 1)
    block_output = hidden_mine + residual_scale * mixed_sum
    mixed_grad = residual_scale * grad_output
    expert_grad = (combine.T[:, :, None] * mixed_grad[None]).astype(jnp.bfloat16)
    combine_part = jnp.sum(expert_out * mixed_grad[None], axis=-1).T
    active_grad = jnp.einsum(
        "etd,efd->etf", expert_grad, full_down, preferred_element_type=jnp.float32
    )
    gate_grad = (
        active_grad * up_pre * sigmoid_gate * (1.0 + gate_pre * (1.0 - sigmoid_gate))
    ).astype(jnp.bfloat16)
    up_grad = (active_grad * silu_gate).astype(jnp.bfloat16)
    normed_part = jnp.einsum(
        "etf,edf->td", gate_grad, full_gate, preferred_element_type=jnp.float32
    ) + jnp.einsum("etf,edf->td", up_grad, full_up, preferred_element_type=jnp.float32)
    gate_full = jnp.einsum("td,etf->edf", normed_two, gate_grad, preferred_element_type=jnp.float32)
    up_full = jnp.einsum("td,etf->edf", normed_two, up_grad, preferred_element_type=jnp.float32)
    down_full = jnp.einsum("etf,etd->efd", active, expert_grad, preferred_element_type=jnp.float32)
    grad_gate, grad_up, grad_down = (
        lax.psum_scatter(gate_full, ("fsdp", "heads"), scatter_dimension=1, tiled=True),
        lax.psum_scatter(up_full, ("fsdp", "heads"), scatter_dimension=1, tiled=True),
        lax.psum_scatter(down_full, ("fsdp", "heads"), scatter_dimension=2, tiled=True),
    )
    normed_grad, combine_grad = lax.psum((normed_part, combine_part), "tensor")
    pick_grad = jnp.sum(onehot * combine_grad[:, None, :], axis=-1)
    picked_grad = route_probs * (
        pick_grad - jnp.sum(route_probs * pick_grad, axis=-1, keepdims=True)
    )
    logit_grad = jnp.sum(onehot * picked_grad[:, :, None], axis=1).astype(jnp.bfloat16)
    router_full = jnp.dot(normed_two.T, logit_grad, preferred_element_type=jnp.float32)
    normed_grad = normed_grad + jnp.dot(
        logit_grad, full_router.T, preferred_element_type=jnp.float32
    )
    gain_ffn_full = jnp.sum(normed_grad * unit_two, axis=0)
    unit_grad = normed_grad * gain_ffn
    hidden_grad = grad_output + scale_two * (
        unit_grad - unit_two * jnp.mean(unit_grad * unit_two, axis=-1, keepdims=True)
    )
    proj_grad = (residual_scale * hidden_grad).astype(jnp.bfloat16)
    out_full = jnp.dot(attn_back.T, proj_grad, preferred_element_type=jnp.float32)
    attn_grad = jnp.dot(proj_grad, full_out.T, preferred_element_type=jnp.float32).astype(
        jnp.bfloat16
    )
    grad_heads = lax.all_to_all(attn_grad, "heads", split_axis=1, concat_axis=0, tiled=True)
    grad_float = (
        grad_heads.reshape(query_rows, key_value_local, heads_per_group, HEAD_DIM)
        .transpose(1, 2, 0, 3)
        .astype(jnp.float32)
    )
    scaled_grad = (grad_float / denominator[..., None]).astype(jnp.bfloat16)
    shift_term = jnp.sum(grad_float * attn_full, axis=-1) / denominator
    start_back = (
        jnp.zeros((key_value_local, heads_per_group, query_rows, HEAD_DIM), jnp.float32),
        jnp.zeros((seq_rows, key_value_local * HEAD_DIM), jnp.float32),
        jnp.zeros((seq_rows, key_value_local * HEAD_DIM), jnp.float32),
    )
    fold_state = start_back

    def block_step(running, block_item):
        query_acc, key_acc, value_acc = running
        key_block, value_block, key_start = block_item
        block_rows = key_block.shape[0]
        weights = masked_exp(key_block, key_start)
        dot_grad = jnp.einsum(
            "kgqd,jkd->kgqj", scaled_grad, value_block, preferred_element_type=jnp.float32
        )
        score_grad = (weights * (dot_grad - shift_term[..., None])).astype(jnp.bfloat16)
        query_acc = (
            query_acc
            + jnp.einsum(
                "kgqj,jkd->kgqd", score_grad, key_block, preferred_element_type=jnp.float32
            )
            * score_scale
        )
        key_part = (
            jnp.einsum(
                "kgqj,qkgd->jkd", score_grad, query_vectors, preferred_element_type=jnp.float32
            )
            * score_scale
        )
        value_part = jnp.einsum(
            "kgqj,kgqd->jkd",
            weights.astype(jnp.bfloat16),
            scaled_grad,
            preferred_element_type=jnp.float32,
        )
        key_old = lax.dynamic_slice_in_dim(key_acc, key_start, block_rows, 0)
        value_old = lax.dynamic_slice_in_dim(value_acc, key_start, block_rows, 0)
        key_acc = lax.dynamic_update_slice_in_dim(
            key_acc,
            key_old + key_part.reshape(block_rows, key_value_local * HEAD_DIM),
            key_start,
            0,
        )
        value_acc = lax.dynamic_update_slice_in_dim(
            value_acc,
            value_old + value_part.reshape(block_rows, key_value_local * HEAD_DIM),
            key_start,
            0,
        )
        return ((query_acc, key_acc, value_acc), None)

    fold_state, _ = lax.scan(
        block_step,
        fold_state,
        split_blocks(
            (
                lax.all_gather(key_local, "fsdp", axis=0, tiled=True),
                lax.all_gather(value_local, "fsdp", axis=0, tiled=True),
            )
        ),
    )
    query_acc, key_acc, value_acc = fold_state
    key_mine, value_mine = (
        lax.psum_scatter(key_acc, "fsdp", scatter_dimension=0, tiled=True),
        lax.psum_scatter(value_acc, "fsdp", scatter_dimension=0, tiled=True),
    )
    query_send_back = (
        query_acc.transpose(2, 0, 1, 3)
        .reshape(query_rows, key_value_local * heads_per_group * HEAD_DIM)
        .astype(jnp.bfloat16)
    )
    query_ret, key_returned, value_ret = (
        lax.all_to_all(query_send_back, "heads", split_axis=0, concat_axis=1, tiled=True),
        lax.all_to_all(
            key_mine.astype(jnp.bfloat16), "heads", split_axis=0, concat_axis=1, tiled=True
        ),
        lax.all_to_all(
            value_mine.astype(jnp.bfloat16), "heads", split_axis=0, concat_axis=1, tiled=True
        ),
    )
    query_lin_grad = (
        reverse_rotary(
            query_ret.astype(jnp.float32).reshape(token_rows, QUERY_HEADS, HEAD_DIM),
            cosine_lookup,
            sine_lookup,
        )
        .reshape(token_rows, QUERY_HEADS * HEAD_DIM)
        .astype(jnp.bfloat16)
    )
    key_lin_grad = (
        reverse_rotary(
            key_returned.astype(jnp.float32).reshape(token_rows, KEY_VALUE_HEADS, HEAD_DIM),
            cosine_lookup,
            sine_lookup,
        )
        .reshape(token_rows, KEY_VALUE_HEADS * HEAD_DIM)
        .astype(jnp.bfloat16)
    )
    query_full = jnp.dot(normalized_input.T, query_lin_grad, preferred_element_type=jnp.float32)
    key_full = jnp.dot(normalized_input.T, key_lin_grad, preferred_element_type=jnp.float32)
    value_full = jnp.dot(normalized_input.T, value_ret, preferred_element_type=jnp.float32)
    normed_one_grad = jnp.dot(query_lin_grad, full_query.T, preferred_element_type=jnp.float32)
    normed_one_grad = normed_one_grad + jnp.dot(
        key_lin_grad, full_key.T, preferred_element_type=jnp.float32
    )
    normed_one_grad = normed_one_grad + jnp.dot(
        value_ret, full_value.T, preferred_element_type=jnp.float32
    )
    gain_attn_full = jnp.sum(normed_one_grad * unit_one, axis=0)
    unit_one_grad = normed_one_grad * gain_attn
    grad_input = hidden_grad + scale_one * (
        unit_one_grad - unit_one * jnp.mean(unit_one_grad * unit_one, axis=-1, keepdims=True)
    )
    grad_attn_gain, grad_ffn_gain, grad_query, grad_key, grad_value, grad_out_proj, grad_router = (
        lax.psum_scatter(gain_attn_full, ("fsdp", "heads"), scatter_dimension=0, tiled=True),
        lax.psum_scatter(gain_ffn_full, ("fsdp", "heads"), scatter_dimension=0, tiled=True),
        lax.psum_scatter(query_full, ("fsdp", "heads"), scatter_dimension=0, tiled=True),
        lax.psum_scatter(key_full, ("fsdp", "heads"), scatter_dimension=0, tiled=True),
        lax.psum_scatter(value_full, ("fsdp", "heads"), scatter_dimension=0, tiled=True),
        lax.psum_scatter(out_full, ("fsdp", "heads"), scatter_dimension=0, tiled=True),
        lax.psum_scatter(router_full, ("fsdp", "heads"), scatter_dimension=0, tiled=True),
    )
    return (
        block_output,
        grad_input,
        grad_attn_gain,
        grad_ffn_gain,
        grad_query,
        grad_key,
        grad_value,
        grad_out_proj,
        grad_router,
        grad_gate,
        grad_up,
        grad_down,
    )


def solution(mesh):
    in_specs = (
        P(("fsdp", "heads"), None),
        P(),
        P(("fsdp", "heads"), None),
        P(("fsdp", "heads")),
        P(("fsdp", "heads")),
        P(("fsdp", "heads"), None),
        P(("fsdp", "heads"), None),
        P(("fsdp", "heads"), None),
        P(("fsdp", "heads"), None),
        P(("fsdp", "heads"), None),
        P(None, ("fsdp", "heads"), "tensor"),
        P(None, ("fsdp", "heads"), "tensor"),
        P(None, "tensor", ("fsdp", "heads")),
        P(("fsdp", "heads"), None),
    )
    out_specs = (
        P(("fsdp", "heads"), "tensor"),
        P(("fsdp", "heads"), None),
        P(("fsdp", "heads")),
        P(("fsdp", "heads")),
        P(("fsdp", "heads"), None),
        P(("fsdp", "heads"), None),
        P(("fsdp", "heads"), None),
        P(("fsdp", "heads"), None),
        P(("fsdp", "heads"), None),
        P(None, ("fsdp", "heads"), "tensor"),
        P(None, ("fsdp", "heads"), "tensor"),
        P(None, "tensor", ("fsdp", "heads")),
    )
    return jax.shard_map(body, mesh=mesh, in_specs=in_specs, out_specs=out_specs, check_vma=False)
```

profile of v0, /device:TPU:16, one launch (start us, length us, event | category | flops | bytes accessed | tf_op | source)
XLA Modules:
  0.0 1416.0 jit_solution(15237264971575318418)
XLA Ops:
  15.0 12.1 all-reduce.5
  27.4 17.9 %all-gather = bf16[8,192,16]{1,2,0:T(8,128)(2,1)S(1)} all-gather(bf16[1,192,16]{1,2,0:T(8,128)(2,1)S(1)} %bitcast.304), channel_id=1, replica_groups=mesh['fsdp'=4,'heads'=2,'tensor'=4] {'fsdp','heads'}, dimensions={0}, use_global_device_ids=true | all-gather | bytes 55296 | tf_op jit(solution)/shard_map/all_gather | solution.py:89
  53.5 19.2 %all_gather.40 = bf16[1536,256]{1,0:T(8,128)(2,1)S(1)} all-gather(bf16[384,256]{1,0:T(8,128)(2,1)S(1)} %bitcast.295), channel_id=1, replica_groups=mesh['fsdp'=4,'heads'=2,'tensor'=4] {'fsdp'}, dimensions={0}, use_global_device_ids=true | all-gather | bytes 983040 | tf_op jit(solution)/shard_map/all_gather | solution.py:185
  83.5 30.7 %all_gather.43 = bf16[1536,256]{1,0:T(8,128)(2,1)S(1)} all-gather(bf16[384,256]{1,0:T(8,128)(2,1)S(1)} %bitcast.296), channel_id=1, replica_groups=mesh['fsdp'=4,'heads'=2,'tensor'=4] {'fsdp'}, dimensions={0}, use_global_device_ids=true | all-gather | bytes 983040 | tf_op jit(solution)/shard_map/all_gather | solution.py:186
  118.4 10.6 all-gather.11.cloned.1.call-done
  146.6 56.7 %while.28 = (s32[]{:T(128)}, f32[4,3,384]{2,1,0:T(4,128)S(1)}, f32[4,3,384,64]{2,3,1,0:T(8,128)S(1)}, s32[4]{0:T(128)S(1)}, s32[384]{0:T(512)S(1)}, /*index=5*/s...) while((s32[]{:T(128)}, f32[4,3,384]{2,1,0:T(4,128)S(1)}, ...), condition=%wide.region_3.4_spmd.clone, body=%wide.region_1.3_spmd.clone.sunk | while | flops 464639232 | bytes 18026704 | solution.py:180
  224.1 21.3 %all-gather.19.cloned.1.call-done = bf16[16,1536,128]{2,1,0:T(8,128)(2,1)} async-done(((bf16[16,192,128]{2,1,0:T(8,128)(2,1)}), bf16[16,1536,128]{2,1,0:T(8,128)(2,1)}) %all-gather.19.cloned.1.call-update) | async-done | bytes 6291472 | tf_op jit(solution)/shard_map/all_gather | solution.py:91
  250.7 59.5 %all-gather.17.cloned.1.call-done = bf16[16,1536,128]{2,1,0:T(8,128)(2,1)} async-done(((bf16[16,192,128]{2,1,0:T(8,128)(2,1)}), bf16[16,1536,128]{2,1,0:T(8,128)(2,1)}) %all-gather.17.cloned.1.call-update) | async-done | bytes 6291472 | tf_op jit(solution)/shard_map/all_gather | solution.py:90
  315.5 59.7 %all-gather.21.cloned.1.call-done = bf16[16,128,1536]{1,2,0:T(8,128)(2,1)} async-done(((bf16[16,128,192]{1,2,0:T(8,128)(2,1)}), bf16[16,128,1536]{1,2,0:T(8,128)(2,1)}) %all-gather.21.cloned.1.call-update) | async-done | bytes 6291472 | tf_op jit(solution)/shard_map/all_gather | solution.py:92
  399.1 16.3 %psum.15 = f32[192,16]{0,1:T(8,128)S(1)} all-reduce(f32[192,16]{0,1:T(8,128)S(1)} %bitcast.303), channel_id=1, replica_groups=mesh['fsdp'=4,'heads'=2,'tensor'=4] {'tensor'}, use_global_device_ids=true, to_apply=%region_13.14 | all-reduce | flops 3072 | bytes 24576 | tf_op jit(solution)/shard_map/psum | solution.py:243
  415.5 30.6 %all-reduce.8.cloned.1.call-done = f32[192,1536]{1,0:T(8,128)} async-done(((f32[192,1536]{1,0:T(8,128)}), f32[192,1536]{1,0:T(8,128)}) %all-reduce.8.cloned.1.call-update) | async-done | bytes 1179664 | tf_op jit(solution)/shard_map/psum | solution.py:243
  469.1 130.9 %while.29 = (s32[]{:T(128)}, f32[4,3,384,64]{2,3,1,0:T(8,128)}, f32[1536,256]{1,0:T(8,128)}, f32[1536,256]{1,0:T(8,128)}, s32[4]{0:T(128)S(1)}, /*index=5*/s32[3...) while((s32[]{:T(128)}, f32[4,3,384,64]{2,3,1,0:T(8,128)}, ...), condition=%wide.region_20.21_spmd.clone, body=%wide.region_19.20_spmd.clone.sunk | while | flops 1148240640 | bytes 58479036 | solution.py:322
  610.4 12.7 copy.157
  630.7 12.7 copy.158
  652.2 19.3 %reduce-scatter.18.cloned.1.call-done = f32[384,256]{1,0:T(8,128)} async-done(((f32[1536,256]{1,0:T(8,128)}), f32[384,256]{1,0:T(8,128)}) %reduce-scatter.18.cloned.1.call-update) | async-done | bytes 393232 | tf_op jit(solution)/shard_map/reduce_scatter | solution.py:335
  712.0 20.9 %reduce-scatter.34.cloned.1.call-done = bf16[384,192]{1,0:T(8,128)(2,1)} async-done(((bf16[1536,192]{1,0:T(8,128)(2,1)}), bf16[384,192]{1,0:T(8,128)(2,1)}) %reduce-scatter.34.cloned.1.call-update) | async-done | bytes 147472
  742.2 22.7 %all-reduce.4 = (f32[1536]{0:T(1024)S(1)}, f32[1536]{0:T(1024)S(1)}) all-reduce(f32[1536]{0:T(1024)S(1)} %get-tuple-element.376, f32[1536]{0:T(1024)S(1)} %copy-done.51), channel_id=5, replica_groups=mesh['fsdp'=4,'heads'=2,'tensor'=4] {'fsdp','heads'}, use_global_device_ids=true, to_apply=%region_25.26.clone | all-reduce | flops 3072 | bytes 24576
  767.5 95.1 %reduce-scatter.28.cloned.1.call-done = f32[16,192,128]{2,0,1:T(8,128)} async-done(((f32[16,1536,128]{2,0,1:T(8,128)}), f32[16,192,128]{2,0,1:T(8,128)}) %reduce-scatter.28.cloned.1.call-update) | async-done | bytes 1572880 | tf_op jit(solution)/shard_map/reduce_scatter | solution.py:239
  865.7 126.7 %reduce-scatter.30.cloned.1.call-done = f32[16,192,128]{2,0,1:T(8,128)} async-done(((f32[16,1536,128]{2,0,1:T(8,128)}), f32[16,192,128]{2,0,1:T(8,128)}) %reduce-scatter.30.cloned.1.call-update) | async-done | bytes 1572880 | tf_op jit(solution)/shard_map/reduce_scatter | solution.py:240
  995.5 37.9 %reduce-scatter.22.cloned.1.call-done = f32[192,512]{1,0:T(8,128)} async-done(((f32[1536,512]{1,0:T(8,128)}), f32[192,512]{1,0:T(8,128)}) %reduce-scatter.22.cloned.1.call-update) | async-done | bytes 393232 | tf_op jit(solution)/shard_map/reduce_scatter | solution.py:388
  1033.3 42.4 %reduce-scatter.24.cloned.1.call-done = f32[192,512]{1,0:T(8,128)} async-done(((f32[1536,512]{1,0:T(8,128)}), f32[192,512]{1,0:T(8,128)}) %reduce-scatter.24.cloned.1.call-update) | async-done | bytes 393232 | tf_op jit(solution)/shard_map/reduce_scatter | solution.py:389
  1075.7 102.1 %reduce-scatter.20.cloned.1.call-done = f32[192,1536]{1,0:T(8,128)} async-done(((f32[1536,1536]{1,0:T(8,128)}), f32[192,1536]{1,0:T(8,128)}) %reduce-scatter.20.cloned.1.call-update) | async-done | bytes 1179664 | tf_op jit(solution)/shard_map/reduce_scatter | solution.py:387
  1177.8 100.6 %reduce-scatter.26.cloned.1.call-done = f32[192,1536]{1,0:T(8,128)} async-done(((f32[1536,1536]{1,0:T(8,128)}), f32[192,1536]{1,0:T(8,128)}) %reduce-scatter.26.cloned.1.call-update) | async-done | bytes 1179664 | tf_op jit(solution)/shard_map/reduce_scatter | solution.py:390
  1278.5 130.5 %reduce-scatter.32.cloned.1.call-done = f32[16,128,192]{1,2,0:T(8,128)} async-done(((f32[16,128,1536]{1,2,0:T(8,128)}), f32[16,128,192]{1,2,0:T(8,128)}) %reduce-scatter.32.cloned.1.call-update) | async-done | bytes 1572880 | tf_op jit(solution)/shard_map/reduce_scatter | solution.py:241
  (423 shorter events, 381.3 us)
Async XLA Ops:
  7.2 39.9 %all-gather.9.cloned.1.call-start = ((), (), s32[]{:S(2)}) async-start(), calls=%async_computation.19 | async-start | bytes 1769472 | tf_op jit(solution)/shard_map/all_gather | solution.py:86
  7.9 69.7 %all-gather.13.cloned.1.call-start = ((), (), s32[]{:S(2)}) async-start(), calls=%async_computation.21 | async-start | bytes 1769472 | tf_op jit(solution)/shard_map/all_gather | solution.py:87
  8.7 120.3 %all-gather.11.cloned.1.call-start = ((), (), s32[]{:S(2)}) async-start(), calls=%async_computation.20 | async-start | bytes 5308416 | tf_op jit(solution)/shard_map/all_gather | solution.py:85
  9.4 207.8 %all-gather.15.cloned.1.call-start = ((), (), s32[]{:S(2)}) async-start(), calls=%async_computation.22 | async-start | bytes 5308416 | tf_op jit(solution)/shard_map/all_gather | solution.py:88
  10.0 235.4 %all-gather.19.cloned.1.call-start = ((), (), s32[]{:S(2)}) async-start(), calls=%async_computation.24 | async-start | bytes 7077888 | tf_op jit(solution)/shard_map/all_gather | solution.py:91
  10.6 299.6 %all-gather.17.cloned.1.call-start = ((), (), s32[]{:S(2)}) async-start(), calls=%async_computation.23 | async-start | bytes 7077888 | tf_op jit(solution)/shard_map/all_gather | solution.py:90
  11.2 364.0 %all-gather.21.cloned.1.call-start = ((), (), s32[]{:S(2)}) async-start(), calls=%async_computation.25 | async-start | bytes 7077888 | tf_op jit(solution)/shard_map/all_gather | solution.py:92
  12.0 434.2 %all-reduce.8.cloned.1.call-start = ((), (), s32[]{:S(2)}) async-start(), calls=%async_computation.26 | async-start | bytes 2359296 | tf_op jit(solution)/shard_map/psum | solution.py:243
  27.1 101.9 %copy-start.41 = (f32[1536]{0:T(1024)}, f32[1536]{0:T(1024)S(1)}, u32[]{:S(2)}) copy-start(f32[1536]{0:T(1024)S(1)} %convert_element_type.143) | copy-start | bytes 18436
  27.3 101.7 %copy-start.49 = (f32[192]{0:T(256)}, f32[192]{0:T(256)S(1)}, u32[]{:S(2)}) copy-start(f32[192]{0:T(256)S(1)} %add_rsqrt_fusion.1) | copy-start | bytes 2308
  27.3 193.7 %copy-start.45 = (f32[1536]{0:T(1024)}, f32[1536]{0:T(1024)S(1)}, u32[]{:S(2)}) copy-start(f32[1536]{0:T(1024)S(1)} %convert_element_type.152) | copy-start | bytes 18436
  221.0 227.7 %copy-start.12 = (f32[192,1536]{1,0:T(8,128)}, f32[192,1536]{1,0:T(8,128)S(1)}, u32[]{:S(2)}) copy-start(f32[192,1536]{1,0:T(8,128)S(1)} %get-tuple-element.454) | copy-start | bytes 3538948
  221.8 88.4 %copy-start.5 = (bf16[192,1536]{1,0:T(8,128)(2,1)}, bf16[192,1536]{1,0:T(8,128)(2,1)S(1)}, u32[]{:S(2)}) copy-start(bf16[192,1536]{1,0:T(8,128)(2,1)S(1)} %multiply_convert_fusion.5) | copy-start | bytes 1769476
  391.5 252.1 %reduce-scatter.16.cloned.1.call-start = ((), (), s32[]{:S(2)}) async-start(), calls=%async_computation.27 | async-start | bytes 1966080 | tf_op jit(solution)/shard_map/reduce_scatter | solution.py:334
  600.0 71.5 %reduce-scatter.18.cloned.1.call-start = ((), (), s32[]{:S(2)}) async-start(), calls=%async_computation.28 | async-start | bytes 1966080 | tf_op jit(solution)/shard_map/reduce_scatter | solution.py:335
  600.6 109.8 %reduce-scatter.36.cloned.1.call-start = ((), (), s32[]{:S(2)}) async-start(), calls=%async_computation.37 | async-start | bytes 884736
  602.5 130.5 %reduce-scatter.34.cloned.1.call-start = ((), (), s32[]{:S(2)}) async-start(), calls=%async_computation.36 | async-start | bytes 983040
  603.7 258.9 %reduce-scatter.28.cloned.1.call-start = ((), (), s32[]{:S(2)}) async-start(), calls=%async_computation.33 | async-start | bytes 14155776 | tf_op jit(solution)/shard_map/reduce_scatter | solution.py:239
  623.1 369.3 %reduce-scatter.30.cloned.1.call-start = ((), (), s32[]{:S(2)}) async-start(), calls=%async_computation.34 | async-start | bytes 14155776 | tf_op jit(solution)/shard_map/reduce_scatter | solution.py:240
  643.5 389.9 %reduce-scatter.22.cloned.1.call-start = ((), (), s32[]{:S(2)}) async-start(), calls=%async_computation.30 | async-start | bytes 3538944 | tf_op jit(solution)/shard_map/reduce_scatter | solution.py:388
  652.2 423.5 %reduce-scatter.24.cloned.1.call-start = ((), (), s32[]{:S(2)}) async-start(), calls=%async_computation.31 | async-start | bytes 3538944 | tf_op jit(solution)/shard_map/reduce_scatter | solution.py:389
  678.8 499.0 %reduce-scatter.20.cloned.1.call-start = ((), (), s32[]{:S(2)}) async-start(), calls=%async_computation.29 | async-start | bytes 10616832 | tf_op jit(solution)/shard_map/reduce_scatter | solution.py:387
  693.2 585.3 %reduce-scatter.26.cloned.1.call-start = ((), (), s32[]{:S(2)}) async-start(), calls=%async_computation.32 | async-start | bytes 10616832 | tf_op jit(solution)/shard_map/reduce_scatter | solution.py:390
  699.6 709.4 %reduce-scatter.32.cloned.1.call-start = ((), (), s32[]{:S(2)}) async-start(), calls=%async_computation.35 | async-start | bytes 14155776 | tf_op jit(solution)/shard_map/reduce_scatter | solution.py:241
  (78 other events, 644.8 us)
Sparse Core Ops, SparseCore 0:
  9.6 25.8 all-gather.8
  37.2 25.7 all-gather.12
  64.6 64.3 all-gather.10
  130.5 49.9 all-gather.14
  182.0 63.3 all-gather.18
  246.8 63.3 all-gather.16
  311.8 63.3 all-gather.20
  391.6 54.5 all-reduce.7
  600.1 34.2 reduce-scatter.15
  637.2 34.2 reduce-scatter.17
  673.8 25.8 reduce-scatter.35
  702.5 30.4 reduce-scatter.33
  735.3 127.2 reduce-scatter.27
  864.8 127.6 reduce-scatter.29
  995.1 38.1 reduce-scatter.21
  1036.1 39.5 reduce-scatter.23
  1078.4 99.3 reduce-scatter.19
  1180.6 97.8 reduce-scatter.25
  1281.3 127.6 reduce-scatter.31
where the time goes:
time: 1430 us; the launch traced here: 1420 us
  waiting for transfers between devices  862 us (60%)
  matrix products  218 us (15%)
  blocking collectives  154 us (11%)
  local copies, waits for them, and re-layouts  124 us (9%)
  other arithmetic  23.7 us (2%)
  between operations  16.7 us (1%)
  loops' own time  16.3 us (1%)
    reduce_scatter x1, waiting for transfers between devices, body(): lax.psum_scatter(down_full, ('fsdp', 'heads'), scatter_dimension=2, tiled...  131 us
    reduce_scatter x1, waiting for transfers between devices, body(): lax.psum_scatter(up_full, ('fsdp', 'heads'), scatter_dimension=1, tiled=T...  127 us
    reduce_scatter x1, waiting for transfers between devices, body(): lax.psum_scatter(query_full, ('fsdp', 'heads'), scatter_dimension=0, tile...  102 us
    reduce_scatter x1, waiting for transfers between devices, body(): lax.psum_scatter(out_full, ('fsdp', 'heads'), scatter_dimension=0, tiled=...  101 us
    reduce_scatter x1, waiting for transfers between devices, body(): lax.psum_scatter(gate_full, ('fsdp', 'heads'), scatter_dimension=1, tiled...  95.1 us
    all_gather x1, waiting for transfers between devices, body(): lax.all_gather(down_weight, ('fsdp', 'heads'), axis=2, tiled=True)  59.7 us
    all_gather x1, waiting for transfers between devices, body(): lax.all_gather(gate_weight, ('fsdp', 'heads'), axis=1, tiled=True)  59.5 us
    reduce_scatter x1, waiting for transfers between devices, body(): lax.psum_scatter(value_full, ('fsdp', 'heads'), scatter_dimension=0, tile...  42.4 us
  transfers between devices with their start and end apart: 19, of which 14 were waited for; matrix products, arithmetic and copies ran while one was open for 14% of the time, Pallas kernels for 0%

commit v1 on v0

--- a/solution.py
+++ b/solution.py
@@ -236,9 +236,9 @@
     up_full = jnp.einsum("td,etf->edf", normed_two, up_grad, preferred_element_type=jnp.float32)
     down_full = jnp.einsum("etf,etd->efd", active, expert_grad, preferred_element_type=jnp.float32)
     grad_gate, grad_up, grad_down = (
-        lax.psum_scatter(gate_full, ("fsdp", "heads"), scatter_dimension=1, tiled=True),
-        lax.psum_scatter(up_full, ("fsdp", "heads"), scatter_dimension=1, tiled=True),
-        lax.psum_scatter(down_full, ("fsdp", "heads"), scatter_dimension=2, tiled=True),
+        lax.psum_scatter(gate_full.astype(jnp.bfloat16), ("fsdp", "heads"), scatter_dimension=1, tiled=True),
+        lax.psum_scatter(up_full.astype(jnp.bfloat16), ("fsdp", "heads"), scatter_dimension=1, tiled=True),
+        lax.psum_scatter(down_full.astype(jnp.bfloat16), ("fsdp", "heads"), scatter_dimension=2, tiled=True),
     )
     normed_grad, combine_grad = lax.psum((normed_part, combine_part), "tensor")
     pick_grad = jnp.sum(onehot * combine_grad[:, None, :], axis=-1)
@@ -384,11 +384,15 @@
     grad_attn_gain, grad_ffn_gain, grad_query, grad_key, grad_value, grad_out_proj, grad_router = (
         lax.psum_scatter(gain_attn_full, ("fsdp", "heads"), scatter_dimension=0, tiled=True),
         lax.psum_scatter(gain_ffn_full, ("fsdp", "heads"), scatter_dimension=0, tiled=True),
-        lax.psum_scatter(query_full, ("fsdp", "heads"), scatter_dimension=0, tiled=True),
-        lax.psum_scatter(key_full, ("fsdp", "heads"), scatter_dimension=0, tiled=True),
-        lax.psum_scatter(value_full, ("fsdp", "heads"), scatter_dimension=0, tiled=True),
-        lax.psum_scatter(out_full, ("fsdp", "heads"), scatter_dimension=0, tiled=True),
+        lax.psum_scatter(query_full.astype(jnp.bfloat16), ("fsdp", "heads"), scatter_dimension=0, tiled=True),
+        lax.psum_scatter(key_full.astype(jnp.bfloat16), ("fsdp", "heads"), scatter_dimension=0, tiled=True),
+        lax.psum_scatter(value_full.astype(jnp.bfloat16), ("fsdp", "heads"), scatter_dimension=0, tiled=True),
+        lax.psum_scatter(out_full.astype(jnp.bfloat16), ("fsdp", "heads"), scatter_dimension=0, tiled=True),
         lax.psum_scatter(router_full, ("fsdp", "heads"), scatter_dimension=0, tiled=True),
+    )
+    grad_query, grad_key, grad_value, grad_out_proj, grad_gate, grad_up, grad_down = (
+        g.astype(jnp.float32)
+        for g in (grad_query, grad_key, grad_value, grad_out_proj, grad_gate, grad_up, grad_down)
     )
     return (
         block_output,

time: 1430 us -> 1150 us (0.80)
  waiting for transfers between devices: 862 us -> 586 us
    reduce_scatter x7, waiting for transfers between devices: 635 us -> 342 us  [the longest x1 68.2 us: body(): lax.psum_scatter(gate_full.astype(jnp.bfloat16), ('fsdp', 'heads'), scatt...]
    reduce_scatter x1, waiting for transfers between devices: 0.02 us -> 30.7 us  [body(): lax.psum_scatter(key_acc, 'fsdp', scatter_dimension=0, tiled=True)]
    transpose x2 -> x0, local copies, waits for them, and re-layouts: 25.5 us -> none  [the longest x1 12.7 us: body(): jnp.einsum('td,etf->edf', normed_two, gate_grad, preferred_element_type=j...]
    unnamed x21, waiting for transfers between devices: 26 us -> 5.06 us
    convert_element_type x0 -> x2, local copies, waits for them, and re-layouts: none -> 18.1 us  [the longest x1 9.08 us: body(): up_full.astype(jnp.bfloat16)]
  transfers between devices with their start and end apart: 19 -> 19, of which waited for: 14 -> 13; matrix products, arithmetic and copies ran while one was open for 14% -> 17% of each run, Pallas kernels for 0% -> 0%
where the time goes in v1:
time: 1150 us; the launch traced here: 1130 us
  waiting for transfers between devices  586 us (51%)
  matrix products  213 us (19%)
  blocking collectives  152 us (13%)
  local copies, waits for them, and re-layouts  112 us (10%)
  other arithmetic  37.1 us (3%)
  between operations  16.6 us (1%)
  loops' own time  16.3 us (1%)
    reduce_scatter x1, waiting for transfers between devices, body(): lax.psum_scatter(gate_full.astype(jnp.bfloat16), ('fsdp', 'heads'), scatt...  68.2 us
    reduce_scatter x1, waiting for transfers between devices, body(): lax.psum_scatter(down_full.astype(jnp.bfloat16), ('fsdp', 'heads'), scatt...  68.1 us
    reduce_scatter x1, waiting for transfers between devices, body(): lax.psum_scatter(up_full.astype(jnp.bfloat16), ('fsdp', 'heads'), scatter...  67.9 us
    all_gather x1, waiting for transfers between devices, body(): lax.all_gather(down_weight, ('fsdp', 'heads'), axis=2, tiled=True)  59.7 us
    all_gather x1, waiting for transfers between devices, body(): lax.all_gather(gate_weight, ('fsdp', 'heads'), axis=1, tiled=True)  59.5 us
    reduce_scatter x1, waiting for transfers between devices, body(): lax.psum_scatter(query_full.astype(jnp.bfloat16), ('fsdp', 'heads'), scat...  57.6 us
    reduce_scatter x1, waiting for transfers between devices, body(): lax.psum_scatter(out_full.astype(jnp.bfloat16), ('fsdp', 'heads'), scatte...  53.3 us
    dot_general x8, matrix products, masked_exp(): jnp.einsum('qkgd,jkd->kgqj', query_vectors, key_block, preferred_element_...  42.1 us
  transfers between devices with their start and end apart: 19, of which 13 were waited for; matrix products, arithmetic and copies ran while one was open for 17% of the time, Pallas kernels for 0%

profile of v1, /device:TPU:16, one launch (start us, length us, event | category | flops | bytes accessed | tf_op | source)
XLA Modules:
  0.0 1134.1 jit_solution(12789077553630770022)
XLA Ops:
  15.5 11.6 %all-reduce.5 = (bf16[1536]{0:T(1024)(128)(2,1)S(1)}, bf16[1536]{0:T(1024)(128)(2,1)S(1)}) all-reduce(bf16[1536]{0:T(1024)(128)(2,1)S(1)} %dynamic-update-slice, bf16[1536]{0:T(1024)(128)(2,1)S(1)} %dynamic-update-slice.1), channel_id=1, replica_groups=mesh['fsdp'=4,'heads'=2,'tensor'=4] {'fsdp','heads'}, use_global_device_ids=true, to_apply=%add | all-reduce | flops 3072 | bytes 12288
  27.4 18.5 %all-gather = bf16[8,192,16]{1,2,0:T(8,128)(2,1)S(1)} all-gather(bf16[1,192,16]{1,2,0:T(8,128)(2,1)S(1)} %bitcast.304), channel_id=1, replica_groups=mesh['fsdp'=4,'heads'=2,'tensor'=4] {'fsdp','heads'}, dimensions={0}, use_global_device_ids=true | all-gather | bytes 55296 | tf_op jit(solution)/shard_map/all_gather | solution.py:89
  54.0 18.6 %all_gather.40 = bf16[1536,256]{1,0:T(8,128)(2,1)S(1)} all-gather(bf16[384,256]{1,0:T(8,128)(2,1)S(1)} %bitcast.295), channel_id=1, replica_groups=mesh['fsdp'=4,'heads'=2,'tensor'=4] {'fsdp'}, dimensions={0}, use_global_device_ids=true | all-gather | bytes 983040 | tf_op jit(solution)/shard_map/all_gather | solution.py:185
  83.5 30.7 %all_gather.43 = bf16[1536,256]{1,0:T(8,128)(2,1)S(1)} all-gather(bf16[384,256]{1,0:T(8,128)(2,1)S(1)} %bitcast.296), channel_id=1, replica_groups=mesh['fsdp'=4,'heads'=2,'tensor'=4] {'fsdp'}, dimensions={0}, use_global_device_ids=true | all-gather | bytes 983040 | tf_op jit(solution)/shard_map/all_gather | solution.py:186
  118.3 9.9 all-gather.11.cloned.1.call-done
  145.8 56.7 %while.28 = (s32[]{:T(128)}, f32[4,3,384]{2,1,0:T(4,128)S(1)}, f32[4,3,384,64]{2,3,1,0:T(8,128)S(1)}, s32[4]{0:T(128)S(1)}, s32[384]{0:T(512)S(1)}, /*index=5*/s...) while((s32[]{:T(128)}, f32[4,3,384]{2,1,0:T(4,128)S(1)}, ...), condition=%wide.region_3.4_spmd.clone, body=%wide.region_1.3_spmd.clone.sunk | while | flops 464639232 | bytes 18026704 | solution.py:180
  225.2 19.3 %all-gather.19.cloned.1.call-done = bf16[16,1536,128]{2,1,0:T(8,128)(2,1)} async-done(((bf16[16,192,128]{2,1,0:T(8,128)(2,1)}), bf16[16,1536,128]{2,1,0:T(8,128)(2,1)}) %all-gather.19.cloned.1.call-update) | async-done | bytes 6291472 | tf_op jit(solution)/shard_map/all_gather | solution.py:91
  249.9 59.5 %all-gather.17.cloned.1.call-done = bf16[16,1536,128]{2,1,0:T(8,128)(2,1)} async-done(((bf16[16,192,128]{2,1,0:T(8,128)(2,1)}), bf16[16,1536,128]{2,1,0:T(8,128)(2,1)}) %all-gather.17.cloned.1.call-update) | async-done | bytes 6291472 | tf_op jit(solution)/shard_map/all_gather | solution.py:90
  314.7 59.7 %all-gather.21.cloned.1.call-done = bf16[16,128,1536]{1,2,0:T(8,128)(2,1)} async-done(((bf16[16,128,192]{1,2,0:T(8,128)(2,1)}), bf16[16,128,1536]{1,2,0:T(8,128)(2,1)}) %all-gather.21.cloned.1.call-update) | async-done | bytes 6291472 | tf_op jit(solution)/shard_map/all_gather | solution.py:92
  398.4 16.3 %psum.15 = f32[192,16]{0,1:T(8,128)S(1)} all-reduce(f32[192,16]{0,1:T(8,128)S(1)} %bitcast.303), channel_id=1, replica_groups=mesh['fsdp'=4,'heads'=2,'tensor'=4] {'tensor'}, use_global_device_ids=true, to_apply=%region_13.14 | all-reduce | flops 3072 | bytes 24576 | tf_op jit(solution)/shard_map/psum | solution.py:243
  414.8 30.5 %all-reduce.8.cloned.1.call-done = f32[192,1536]{1,0:T(8,128)} async-done(((f32[192,1536]{1,0:T(8,128)}), f32[192,1536]{1,0:T(8,128)}) %all-reduce.8.cloned.1.call-update) | async-done | bytes 1179664 | tf_op jit(solution)/shard_map/psum | solution.py:243
  468.3 131.0 %while.29 = (s32[]{:T(128)}, f32[4,3,384,64]{2,3,1,0:T(8,128)}, f32[1536,256]{1,0:T(8,128)}, f32[1536,256]{1,0:T(8,128)}, s32[4]{0:T(128)S(1)}, /*index=5*/s32[3...) while((s32[]{:T(128)}, f32[4,3,384,64]{2,3,1,0:T(8,128)}, ...), condition=%wide.region_20.21_spmd.clone, body=%wide.region_19.20_spmd.clone.sunk | while | flops 1148240640 | bytes 58479036 | solution.py:322
  603.1 30.7 %reduce-scatter.16.cloned.1.call-done = f32[384,256]{1,0:T(8,128)} async-done(((f32[1536,256]{1,0:T(8,128)}), f32[384,256]{1,0:T(8,128)}) %reduce-scatter.16.cloned.1.call-update) | async-done | bytes 393232 | tf_op jit(solution)/shard_map/reduce_scatter | solution.py:334
  641.4 29.4 %reduce-scatter.18.cloned.1.call-done = f32[384,256]{1,0:T(8,128)} async-done(((f32[1536,256]{1,0:T(8,128)}), f32[384,256]{1,0:T(8,128)}) %reduce-scatter.18.cloned.1.call-update) | async-done | bytes 393232 | tf_op jit(solution)/shard_map/reduce_scatter | solution.py:335
  701.8 9.0 copy.157
  716.5 9.1 copy.158
  726.3 8.4 fusion.48
  746.4 20.7 %all-reduce.4 = (f32[1536]{0:T(1024)S(1)}, f32[1536]{0:T(1024)S(1)}) all-reduce(f32[1536]{0:T(1024)S(1)} %get-tuple-element.376, f32[1536]{0:T(1024)S(1)} %copy-done.45), channel_id=5, replica_groups=mesh['fsdp'=4,'heads'=2,'tensor'=4] {'fsdp','heads'}, use_global_device_ids=true, to_apply=%region_25.26.clone | all-reduce | flops 3072 | bytes 24576
  771.4 27.3 %reduce-scatter.24.cloned.1.call-done = bf16[192,512]{1,0:T(8,128)(2,1)} async-done(((bf16[1536,512]{1,0:T(8,128)(2,1)}), bf16[192,512]{1,0:T(8,128)(2,1)}) %reduce-scatter.24.cloned.1.call-update) | async-done | bytes 196624 | tf_op jit(solution)/shard_map/reduce_scatter | solution.py:389
  800.3 57.6 %reduce-scatter.20.cloned.1.call-done = bf16[192,1536]{1,0:T(8,128)(2,1)} async-done(((bf16[1536,1536]{1,0:T(8,128)(2,1)}), bf16[192,1536]{1,0:T(8,128)(2,1)}) %reduce-scatter.20.cloned.1.call-update) | async-done | bytes 589840 | tf_op jit(solution)/shard_map/reduce_scatter | solution.py:387
  860.1 53.3 %reduce-scatter.26.cloned.1.call-done = bf16[192,1536]{1,0:T(8,128)(2,1)} async-done(((bf16[1536,1536]{1,0:T(8,128)(2,1)}), bf16[192,1536]{1,0:T(8,128)(2,1)}) %reduce-scatter.26.cloned.1.call-update) | async-done | bytes 589840 | tf_op jit(solution)/shard_map/reduce_scatter | solution.py:390
  915.7 68.2 %reduce-scatter.28.cloned.1.call-done = bf16[16,192,128]{2,0,1:T(8,128)(2,1)} async-done(((bf16[16,1536,128]{2,0,1:T(8,128)(2,1)}), bf16[16,192,128]{2,0,1:T(8,128)(2,1)}) %reduce-scatter.28.cloned.1.call-update) | async-done | bytes 786448 | tf_op jit(solution)/shard_map/reduce_scatter | solution.py:239
  986.3 67.9 %reduce-scatter.30.cloned.1.call-done = bf16[16,192,128]{2,0,1:T(8,128)(2,1)} async-done(((bf16[16,1536,128]{2,0,1:T(8,128)(2,1)}), bf16[16,192,128]{2,0,1:T(8,128)(2,1)}) %reduce-scatter.30.cloned.1.call-update) | async-done | bytes 786448 | tf_op jit(solution)/shard_map/reduce_scatter | solution.py:240
  1056.7 68.1 %reduce-scatter.32.cloned.1.call-done = bf16[16,128,192]{1,2,0:T(8,128)(2,1)} async-done(((bf16[16,128,1536]{1,2,0:T(8,128)(2,1)}), bf16[16,128,192]{1,2,0:T(8,128)(2,1)}) %reduce-scatter.32.cloned.1.call-update) | async-done | bytes 786448 | tf_op jit(solution)/shard_map/reduce_scatter | solution.py:241
  (422 shorter events, 376.9 us)
Async XLA Ops:
  7.2 40.5 %all-gather.9.cloned.1.call-start = ((), (), s32[]{:S(2)}) async-start(), calls=%async_computation.19 | async-start | bytes 1769472 | tf_op jit(solution)/shard_map/all_gather | solution.py:86
  7.9 69.7 %all-gather.13.cloned.1.call-start = ((), (), s32[]{:S(2)}) async-start(), calls=%async_computation.21 | async-start | bytes 1769472 | tf_op jit(solution)/shard_map/all_gather | solution.py:87
  8.7 119.6 %all-gather.11.cloned.1.call-start = ((), (), s32[]{:S(2)}) async-start(), calls=%async_computation.20 | async-start | bytes 5308416 | tf_op jit(solution)/shard_map/all_gather | solution.py:85
  9.4 207.0 %all-gather.15.cloned.1.call-start = ((), (), s32[]{:S(2)}) async-start(), calls=%async_computation.22 | async-start | bytes 5308416 | tf_op jit(solution)/shard_map/all_gather | solution.py:88
  10.0 234.6 %all-gather.19.cloned.1.call-start = ((), (), s32[]{:S(2)}) async-start(), calls=%async_computation.24 | async-start | bytes 7077888 | tf_op jit(solution)/shard_map/all_gather | solution.py:91
  10.6 298.8 %all-gather.17.cloned.1.call-start = ((), (), s32[]{:S(2)}) async-start(), calls=%async_computation.23 | async-start | bytes 7077888 | tf_op jit(solution)/shard_map/all_gather | solution.py:90
  11.2 363.2 %all-gather.21.cloned.1.call-start = ((), (), s32[]{:S(2)}) async-start(), calls=%async_computation.25 | async-start | bytes 7077888 | tf_op jit(solution)/shard_map/all_gather | solution.py:92
  12.0 433.4 %all-reduce.8.cloned.1.call-start = ((), (), s32[]{:S(2)}) async-start(), calls=%async_computation.26 | async-start | bytes 2359296 | tf_op jit(solution)/shard_map/psum | solution.py:243
  27.3 100.9 %copy-start.43 = (f32[192]{0:T(256)}, f32[192]{0:T(256)S(1)}, u32[]{:S(2)}) copy-start(f32[192]{0:T(256)S(1)} %add_rsqrt_fusion.1) | copy-start | bytes 2308
  27.4 192.9 %copy-start.37 = (f32[1536]{0:T(1024)}, f32[1536]{0:T(1024)S(1)}, u32[]{:S(2)}) copy-start(f32[1536]{0:T(1024)S(1)} %convert_element_type.200) | copy-start | bytes 18436
  47.6 84.9 %copy-start.24 = (f32[192,32]{0,1:T(8,128)}, f32[192,32]{0,1:T(8,128)S(1)}, u32[]{:S(2)}) copy-start(f32[192,32]{0,1:T(8,128)S(1)} %get-tuple-element.449) | copy-start | bytes 73732
  220.2 227.7 %copy-start.12 = (f32[192,1536]{1,0:T(8,128)}, f32[192,1536]{1,0:T(8,128)S(1)}, u32[]{:S(2)}) copy-start(f32[192,1536]{1,0:T(8,128)S(1)} %get-tuple-element.454) | copy-start | bytes 3538948
  221.0 88.4 %copy-start.5 = (bf16[192,1536]{1,0:T(8,128)(2,1)}, bf16[192,1536]{1,0:T(8,128)(2,1)S(1)}, u32[]{:S(2)}) copy-start(bf16[192,1536]{1,0:T(8,128)(2,1)S(1)} %multiply_convert_fusion.7) | copy-start | bytes 1769476
  390.7 243.1 %reduce-scatter.16.cloned.1.call-start = ((), (), s32[]{:S(2)}) async-start(), calls=%async_computation.27 | async-start | bytes 1966080 | tf_op jit(solution)/shard_map/reduce_scatter | solution.py:334
  599.3 71.5 %reduce-scatter.18.cloned.1.call-start = ((), (), s32[]{:S(2)}) async-start(), calls=%async_computation.28 | async-start | bytes 1966080 | tf_op jit(solution)/shard_map/reduce_scatter | solution.py:335
  599.9 135.5 %reduce-scatter.36.cloned.1.call-start = ((), (), s32[]{:S(2)}) async-start(), calls=%async_computation.37 | async-start | bytes 884736
  601.7 135.2 %reduce-scatter.34.cloned.1.call-start = ((), (), s32[]{:S(2)}) async-start(), calls=%async_computation.36 | async-start | bytes 983040
  603.0 166.6 %reduce-scatter.22.cloned.1.call-start = ((), (), s32[]{:S(2)}) async-start(), calls=%async_computation.30 | async-start | bytes 1769472 | tf_op jit(solution)/shard_map/reduce_scatter | solution.py:388
  641.4 157.3 %reduce-scatter.24.cloned.1.call-start = ((), (), s32[]{:S(2)}) async-start(), calls=%async_computation.31 | async-start | bytes 1769472 | tf_op jit(solution)/shard_map/reduce_scatter | solution.py:389
  677.7 180.2 %reduce-scatter.20.cloned.1.call-start = ((), (), s32[]{:S(2)}) async-start(), calls=%async_computation.29 | async-start | bytes 5308416 | tf_op jit(solution)/shard_map/reduce_scatter | solution.py:387
  690.3 223.2 %reduce-scatter.26.cloned.1.call-start = ((), (), s32[]{:S(2)}) async-start(), calls=%async_computation.32 | async-start | bytes 5308416 | tf_op jit(solution)/shard_map/reduce_scatter | solution.py:390
  696.2 287.7 %reduce-scatter.28.cloned.1.call-start = ((), (), s32[]{:S(2)}) async-start(), calls=%async_computation.33 | async-start | bytes 7077888 | tf_op jit(solution)/shard_map/reduce_scatter | solution.py:239
  710.9 343.3 %reduce-scatter.30.cloned.1.call-start = ((), (), s32[]{:S(2)}) async-start(), calls=%async_computation.34 | async-start | bytes 7077888 | tf_op jit(solution)/shard_map/reduce_scatter | solution.py:240
  725.6 399.1 %reduce-scatter.32.cloned.1.call-start = ((), (), s32[]{:S(2)}) async-start(), calls=%async_computation.35 | async-start | bytes 7077888 | tf_op jit(solution)/shard_map/reduce_scatter | solution.py:241
  (75 other events, 646.9 us)
Sparse Core Ops, SparseCore 0:
  9.6 25.8 all-gather.8
  37.2 25.0 all-gather.12
  63.9 64.2 all-gather.10
  129.7 49.9 all-gather.14
  181.2 63.3 all-gather.18
  246.0 63.3 all-gather.16
  311.0 63.3 all-gather.20
  390.8 54.4 all-reduce.7
  599.5 34.2 reduce-scatter.15
  636.5 34.2 reduce-scatter.17
  673.1 25.8 reduce-scatter.35
  701.8 30.4 reduce-scatter.33
  735.2 27.9 reduce-scatter.21
  765.9 32.6 reduce-scatter.23
  800.8 57.0 reduce-scatter.19
  860.1 53.3 reduce-scatter.25
  915.6 68.1 reduce-scatter.27
  986.0 68.1 reduce-scatter.29
  1056.5 68.1 reduce-scatter.31

commit v2 on v1

--- a/solution.py
+++ b/solution.py
@@ -3,6 +3,8 @@
 import jax
 import jax.numpy as jnp
 from jax import lax
+from jax.experimental import pallas as pl
+from jax.experimental.pallas import tpu as pltpu
 from jax.sharding import PartitionSpec as P
 
 QUERY_HEADS = 24
@@ -410,6 +412,1143 @@
     )
 
 
+MESH_ID = pl.DeviceIdType.MESH
+F32 = jnp.float32
+BF16 = jnp.bfloat16
+
+TB = 192
+DM = 1536
+TC = 384
+NBLK = 8
+NQ = 6
+FIRST_DOC_BLOCKS = 5
+
+
+def contract(left, right, left_dim, right_dim, precision=None):
+    return lax.dot_general(
+        left,
+        right,
+        (((left_dim,), (right_dim,)), ((), ())),
+        preferred_element_type=F32,
+        precision=precision,
+    )
+
+
+def rows(index):
+    return pl.ds(pl.multiple_of(index * TB, TB), TB)
+
+
+def cols(index):
+    return pl.ds(pl.multiple_of(index * TC, 128), TC)
+
+
+class Place:
+    def __init__(self):
+        self.z = lax.axis_index("fsdp")
+        self.c = lax.axis_index("heads")
+        self.t = lax.axis_index("tensor")
+        self.b = 2 * self.z + self.c
+
+    def partner(self):
+        return (self.z, 1 - self.c, self.t)
+
+    def at_z(self, z):
+        return (z, self.c, self.t)
+
+    def at_block(self, block):
+        return (block // 2, block % 2, self.t)
+
+    def peer_t(self, k):
+        if k == 1:
+            return self.t + 1 - 2 * (self.t % 2)
+        if k == 2:
+            return (self.t + 2) % 4
+        return 3 - self.t
+
+    def plane(self, k):
+        return (self.z, self.c, self.peer_t(k))
+
+    def other(self, k):
+        return (self.b + k) % NBLK
+
+    def arrival(self, i):
+        if i == 0:
+            return self.z + 1 - 2 * (self.z % 2)
+        if i == 1:
+            return 2 - self.z // 2
+        return 3 - 3 * (self.z // 2)
+
+    def forward_to(self, i):
+        return 3 - self.z if i == 0 else 3 * (self.z - 1)
+
+    def middle(self):
+        return self.z * (3 - self.z) > 0
+
+
+def remote(src, dst, send_sem, recv_sem, device):
+    return pltpu.make_async_remote_copy(
+        src_ref=src,
+        dst_ref=dst,
+        send_sem=send_sem,
+        recv_sem=recv_sem,
+        device_id=device,
+        device_id_type=MESH_ID,
+    )
+
+
+class Pending:
+    def __init__(self):
+        self.items = []
+
+    def start(self, copy, when=None):
+        if when is None:
+            copy.start()
+        else:
+
+            @pl.when(when)
+            def _():
+                copy.start()
+
+        self.items.append((copy, when))
+
+    def drain(self):
+        for copy, when in self.items:
+            if when is None:
+                copy.wait_send()
+            else:
+
+                @pl.when(when)
+                def _(copy=copy):
+                    copy.wait_send()
+
+        self.items = []
+
+
+class LineGather:
+    def __init__(self, me, pend, view, line_view, sems):
+        self.me, self.pend, self.view, self.line_view = me, pend, view, line_view
+        self.send, self.recv, self.psend, self.precv = sems
+
+    def start(self):
+        me = self.me
+        own = self.line_view(me.b)
+        self.pend.start(
+            remote(own, own, self.send.at[0], self.recv.at[me.z], me.at_z(me.z + 1)), me.z < 3
+        )
+        self.pend.start(
+            remote(own, own, self.send.at[1], self.recv.at[me.z], me.at_z(me.z - 1)), me.z > 0
+        )
+        whole = self.view(me.b)
+        self.pend.start(
+            remote(whole, whole, self.psend.at[3], self.precv.at[me.z], me.partner())
+        )
+
+    def arrive(self, i):
+        me = self.me
+        source = me.arrival(i)
+        block = self.line_view(2 * source + me.c)
+        remote(block, block, self.send.at[0], self.recv.at[source], me.partner()).wait_recv()
+        self.pend.start(
+            remote(
+                block, block, self.send.at[2 + i], self.recv.at[source], me.at_z(me.forward_to(i))
+            ),
+            me.middle(),
+        )
+        return source, block
+
+    def share(self, i):
+        me = self.me
+        source = me.arrival(i)
+        whole = self.view(2 * source + me.c)
+        self.pend.start(
+            remote(whole, whole, self.psend.at[i], self.precv.at[source], me.partner())
+        )
+
+    def finish(self):
+        me = self.me
+        for source in range(4):
+            whole = self.view(2 * source + (1 - me.c))
+            remote(
+                whole, whole, self.psend.at[0], self.precv.at[source], me.partner()
+            ).wait_recv()
+
+
+class FullGather(LineGather):
+    def __init__(self, me, pend, buffer, sems):
+        super().__init__(
+            me,
+            pend,
+            lambda block: buffer.at[rows(block), :],
+            lambda block: buffer.at[rows(block), cols(me.t)],
+            sems[:4],
+        )
+        self.buffer = buffer
+        self.xsend, self.xrecv = sems[4:]
+
+    def arrive(self, i):
+        source, block = super().arrive(i)
+        for k in (3, 1, 2):
+            self.pend.start(
+                remote(
+                    block,
+                    block,
+                    self.xsend.at[i, k - 1],
+                    self.xrecv.at[k - 1, source],
+                    self.me.plane(k),
+                )
+            )
+
+    def cross(self, i):
+        me = self.me
+        source = me.arrival(i)
+        for k in (1, 2, 3):
+            piece = self.buffer.at[rows(2 * source + me.c), cols(me.peer_t(k))]
+            remote(
+                piece, piece, self.xsend.at[i, k - 1], self.xrecv.at[k - 1, source], me.plane(k)
+            ).wait_recv()
+        self.share(i)
+
+
+def swap_halves(u):
+    lane = lax.broadcasted_iota(jnp.int32, u.shape, 1)
+    return jnp.where(lane % 64 < 32, pltpu.roll(u, 96, 1), pltpu.roll(u, 32, 1))
+
+
+def half_mask(half):
+    lane = lax.broadcasted_iota(jnp.int32, (TB, 128), 1)
+    return (lane // 64) == half
+
+
+def head_from_chunk(chunk, h):
+    if h % 2 != h // 3:
+        chunk = pltpu.roll(chunk, 64, 1)
+    return jnp.where(half_mask(h // 3), chunk, 0.0)
+
+
+def chunk_from_heads(first, second, pair):
+    if (2 * pair) // 3 != 0:
+        first = pltpu.roll(first, 64, 1)
+    if (2 * pair + 1) // 3 != 1:
+        second = pltpu.roll(second, 64, 1)
+    return jnp.where(half_mask(0), first, second)
+
+
+def row_chunks(body, size=64):
+    def step(i, carry):
+        body(pl.ds(pl.multiple_of(i * size, size), size))
+        return carry
+
+    lax.fori_loop(0, TB // size, step, 0)
+
+
+class Bag(dict):
+    __getattr__ = dict.__getitem__
+
+
+def bags(tree):
+    return Bag({k: bags(v) for k, v in tree.items()}) if isinstance(tree, dict) else tree
+
+
+def scratch_tree():
+    def f32(*shape):
+        return pltpu.VMEM(shape, F32)
+
+    def b16(*shape):
+        return pltpu.VMEM(shape, BF16)
+
+    dma = pltpu.SemaphoreType.DMA
+
+    def pair(*shape):
+        return (dma(shape), dma(shape))
+
+    def line():
+        return (dma((5,)), dma((4,)), dma((4,)), dma((4,)))
+
+    def full():
+        return (*line(), dma((3, 3)), dma((3, 4)))
+
+    def scatter():
+        return dict(
+            part=b16(DM, DM),
+            core=b16(4, TB, DM),
+            plane=b16(4, 3, TB, TC),
+            line=b16(4, TB, TC),
+            sems=(*pair(4), *pair(4, 3), *pair(4)),
+        )
+
+    def reduce(width):
+        return dict(core=b16(4, TB, width), line=b16(4, TB, width), sems=(*pair(4), *pair(4)))
+
+    return dict(
+        w_qkv=b16(DM, 640),
+        small=b16(NBLK, 32, 256),
+        w_out=b16(DM, DM),
+        d_moe=b16(DM, DM),
+        hn=b16(DM, DM),
+        kv=b16(DM, 256),
+        w_moe=b16(DM, 768),
+        comb=f32(NBLK, 16, 256),
+        xn=b16(TB, DM),
+        r_one=f32(TB, 1),
+        r_two=f32(TB, 1),
+        hidden=f32(TB, DM),
+        qz=b16(NQ, TB, 128),
+        oz=f32(NQ, TB, 128),
+        den=f32(NQ, TB, 128),
+        o_full=b16(TB, DM),
+        gains=f32(8, DM),
+        router_t=b16(16, DM),
+        dgu=b16(DM, 512),
+        cz=b16(DM, 256),
+        h=scatter(),
+        y=scatter(),
+        dhn=b16(TB, DM),
+        dc_own=f32(NBLK, 8, 256),
+        dc_in=f32(NBLK, 8, 256),
+        dc_plane=f32(3, NBLK, 8, 256),
+        dc_t=f32(16, 256),
+        g_moe=b16(DM, 768),
+        dh=f32(TB, DM),
+        dproj=b16(TB, DM),
+        flat=f32(24, DM),
+        sm=dict(own=f32(NBLK, 24, 256), inn=f32(NBLK, 24, 256)),
+        sn=dict(own=f32(NBLK, 8, 256), inn=f32(NBLK, 8, 256)),
+        g_out_sum=b16(TB, TC),
+        dnz=b16(NQ, TB, 128),
+        shift=f32(NQ, TB, 128),
+        dq=f32(NQ, TB, 128),
+        dkv=b16(DM, 256),
+        dqkv=b16(TB, 640),
+        g_qkv_sum=b16(TB, 640),
+        dx=b16(TB, DM),
+        dx_in=b16(3, TB, TC),
+        dxn=b16(TB, DM),
+        local_sem=dma((10,)),
+        lg=dict(s=line(), w=line(), kv=line(), c=line()),
+        fg=dict(wo=full(), dm=full(), hn=full()),
+        aa=dict(wm=pair(8), gm=pair(8), dc=pair(8), sm=pair(8), sn=pair(8)),
+        pl=dict(o=pair(3), dc=pair(3), dh=pair(3), go=pair(3), gq=pair(3), xs=pair(3), xg=pair(3)),
+        rd=dict(go=reduce(TC), dkv=reduce(256), gq=reduce(640)),
+    )
+
+
+def kernel(r):
+    g_out_part = r.dgu.at[:, 0:TC]
+    g_qkv_part = r.w_moe.at[:, 0:640]
+    me = Place()
+    pend = Pending()
+    z, c, t, b = me.z, me.c, me.t, me.b
+
+    loc = r.local_sem
+    local = [
+        pltpu.make_async_copy(r.wq.at[:, cols(t)], r.w_qkv.at[rows(b), 0:384], loc.at[0]),
+        pltpu.make_async_copy(
+            r.wk.at[:, pl.ds(pl.multiple_of(128 * t, 128), 128)],
+            r.w_qkv.at[rows(b), 384:512], loc.at[1],
+        ),
+        pltpu.make_async_copy(
+            r.wv.at[:, pl.ds(pl.multiple_of(128 * t, 128), 128)],
+            r.w_qkv.at[rows(b), 512:640], loc.at[2],
+        ),
+        pltpu.make_async_copy(r.wo, r.w_out.at[rows(b), :], loc.at[3]),
+    ]
+    moe_sources = []
+    for which, shard in enumerate((r.gate, r.up, r.down_t)):
+        for e in range(2):
+            moe_sources.append((shard, e, pl.ds(256 * which + 128 * e, 128)))
+    own_moe = [
+        pltpu.make_async_copy(shard.at[2 * b + e], r.w_moe.at[rows(b), lanes], loc.at[4 + i])
+        for i, (shard, e, lanes) in enumerate(moe_sources)
+    ]
+    for copy in local:
+        copy.start()
+    for copy in own_moe:
+        copy.start()
+    barrier = pltpu.get_barrier_semaphore()
+    for k in range(1, NBLK):
+        pl.semaphore_signal(
+            barrier, inc=1, device_id=me.at_block(me.other(k)), device_id_type=MESH_ID
+        )
+    for k in (1, 2, 3):
+        pl.semaphore_signal(barrier, inc=1, device_id=me.plane(k), device_id_type=MESH_ID)
+    r.small[b] = r.small_own[...]
+    r.d_moe[rows(b), :] = (residual_scale * r.gout[...]).astype(BF16)
+    pl.semaphore_wait(barrier, NBLK - 1 + 3)
+
+    def line(view, sems):
+        return LineGather(me, pend, view, view, sems)
+
+    g_small = line(lambda k: r.small.at[k], r.lg.s)
+    g_qkv = line(lambda k: r.w_qkv.at[rows(k), :], r.lg.w)
+    g_kv = line(lambda k: r.kv.at[rows(k), :], r.lg.kv)
+    g_comb = line(lambda k: r.comb.at[k], r.lg.c)
+    g_wout = FullGather(me, pend, r.w_out, r.fg.wo)
+    g_dmoe = FullGather(me, pend, r.d_moe, r.fg.dm)
+    g_hn = FullGather(me, pend, r.hn, r.fg.hn)
+
+    g_small.start()
+    for copy in local[:3]:
+        copy.wait()
+    g_qkv.start()
+    local[3].wait()
+    g_wout.start()
+    g_dmoe.start()
+
+    def rms_one(chunk):
+        v = r.x[chunk, :].astype(F32)
+        r.r_one[chunk, :] = lax.rsqrt(jnp.mean(v * v, axis=1, keepdims=True) + norm_eps)
+
+    row_chunks(rms_one)
+    for i in range(3):
+        g_small.arrive(i)
+        g_small.share(i)
+        g_qkv.arrive(i)
+        g_qkv.share(i)
+        g_wout.arrive(i)
+    g_small.finish()
+    for k in range(NBLK):
+        piece = r.small[k].astype(F32)
+        r.router_t[:, TB * k : TB * (k + 1)] = piece[0:16, 0:TB].astype(BF16)
+        r.gains[0:8, TB * k : TB * (k + 1)] = piece[16:24, 0:TB]
+
+    def normalize_one(chunk):
+        v = r.x[chunk, :].astype(F32)
+        r.xn[chunk, :] = (v * r.r_one[chunk, :] * r.gains[0:1, :]).astype(BF16)
+
+    row_chunks(normalize_one)
+    g_qkv.finish()
+    qkv = jnp.dot(r.xn[...], r.w_qkv[...], preferred_element_type=F32)
+    cosine, sine = r.rope_c[...], r.rope_s[...]
+    key = qkv[:, 384:512]
+    r.kv[rows(b), 0:128] = (key * cosine + swap_halves(key) * sine).astype(BF16)
+    r.kv[rows(b), 128:256] = qkv[:, 512:640].astype(BF16)
+    g_kv.start()
+    for pair in range(3):
+        u = qkv[:, 128 * pair : 128 * (pair + 1)]
+        u = (u * cosine + swap_halves(u) * sine).astype(BF16).astype(F32)
+        r.qz[2 * pair] = head_from_chunk(u, 2 * pair).astype(BF16)
+        r.qz[2 * pair + 1] = head_from_chunk(u, 2 * pair + 1).astype(BF16)
+    for h in range(NQ):
+        r.oz[h] = jnp.zeros((TB, 128), F32)
+        r.den[h] = jnp.zeros((TB, 128), F32)
+    for i in range(3):
+        g_kv.arrive(i)
+        g_kv.share(i)
+        g_dmoe.arrive(i)
+
+    moe_send, moe_recv = r.aa.wm
+    for k in range(1, NBLK):
+        peer = me.other(k)
+        for shard, e, lanes in moe_sources:
+            remote(
+                shard.at[2 * peer + e],
+                r.w_moe.at[rows(b), lanes],
+                moe_send.at[k],
+                moe_recv.at[b],
+                me.at_block(peer),
+            ).start()
+    g_kv.finish()
+
+    first_block = FIRST_DOC_BLOCKS * (b // FIRST_DOC_BLOCKS)
+
+    def allowed(kb):
+        q_pos = b * TB + lax.broadcasted_iota(jnp.int32, (TB, TB), 0)
+        k_pos = kb * TB + lax.broadcasted_iota(jnp.int32, (TB, TB), 1)
+        same = r.seg_q[...] == r.seg_k[pl.ds(kb, 1), 0:TB]
+        return (q_pos >= k_pos) & same
+
+    def attend(kb, carry):
+        keys = r.kv[rows(kb), 0:128]
+        values = r.kv[rows(kb), 128:256]
+        mask = allowed(kb)
+        for h in range(NQ):
+            scores = contract(r.qz[h], keys, 1, 1) * score_scale
+            e = jnp.where(mask, jnp.exp(scores), 0.0)
+            r.den[h] += jnp.broadcast_to(jnp.sum(e, axis=1, keepdims=True), (TB, 128))
+            r.oz[h] += jnp.dot(e.astype(BF16), values, preferred_element_type=F32)
+        return carry
+
+    lax.fori_loop(first_block, b + 1, attend, 0)
+    for i in range(3):
+        g_wout.cross(i)
+    for pair in range(3):
+        heads = []
+        for h in (2 * pair, 2 * pair + 1):
+            o = jnp.where(half_mask(h // 3), r.oz[h] / r.den[h], 0.0)
+            r.oz[h] = o
+            heads.append(o)
+        chunk = chunk_from_heads(heads[0], heads[1], pair).astype(BF16)
+        r.o_full[:, pl.ds(pl.multiple_of(TC * t + 128 * pair, 128), 128)] = chunk
+
+    def plane_gather(sems, own_view, peer_view):
+        send, recv = sems
+        for k in (3, 1, 2):
+            pend.start(
+                remote(own_view, own_view, send.at[k - 1], recv.at[k - 1], me.plane(k))
+            )
+
+        def wait():
+            for k in (1, 2, 3):
+                piece = peer_view(k)
+                remote(piece, piece, send.at[k - 1], recv.at[k - 1], me.plane(k)).wait_recv()
+
+        return wait
+
+    wait_o = plane_gather(
+        r.pl.o, r.o_full.at[:, cols(t)], lambda k: r.o_full.at[:, cols(me.peer_t(k))]
+    )
+    g_wout.finish()
+    wait_o()
+
+    def project(n, carry):
+        lanes = pl.ds(pl.multiple_of(n * 256, 256), 256)
+        r.hidden[:, lanes] = r.x[:, lanes].astype(F32) + residual_scale * jnp.dot(
+            r.o_full[...], r.w_out[:, lanes], preferred_element_type=F32
+        )
+        return carry
+
+    lax.fori_loop(0, DM // 256, project, 0)
+
+    def normalize_two(chunk):
+        v = r.hidden[chunk, :]
+        factor = lax.rsqrt(jnp.mean(v * v, axis=1, keepdims=True) + norm_eps)
+        r.r_two[chunk, :] = factor
+        r.dproj[chunk, :] = (v * factor * r.gains[1:2, :]).astype(BF16)
+
+    row_chunks(normalize_two)
+    r.hn[rows(b), :] = r.dproj[...]
+    g_hn.start()
+    logits = contract(r.router_t[...], r.dproj[...], 1, 1)
+    chosen = r.mask_t[...] > 0.5
+    top = jnp.max(jnp.where(chosen, logits, -1e30), axis=0, keepdims=True)
+    weight = jnp.where(chosen, jnp.exp(jnp.where(chosen, logits - top, 0.0)), 0.0)
+    combine = weight / jnp.sum(weight, axis=0, keepdims=True)
+    r.comb[b, :, 0:TB] = combine
+    g_comb.start()
+    for i in range(3):
+        g_dmoe.cross(i)
+    for i in range(3):
+        g_comb.arrive(i)
+        g_comb.share(i)
+        g_hn.arrive(i)
+    g_dmoe.finish()
+    g_comb.finish()
+    for i in range(3):
+        g_hn.cross(i)
+    g_hn.finish()
+    for copy in own_moe:
+        copy.wait()
+    for k in range(1, NBLK):
+        peer = me.other(k)
+        whole = r.w_moe.at[rows(peer), :]
+        remote(whole, whole, moe_send.at[k], moe_recv.at[peer], me.partner()).wait_recv()
+
+    lane = lax.broadcasted_iota(jnp.int32, (16, 256), 1)
+    expert = lax.broadcasted_iota(jnp.int32, (16, 256), 0)
+    spread = (expert == 2 * b + lane // 128).astype(F32)
+    sel_row = lax.broadcasted_iota(jnp.int32, (8, 256), 0)
+    sel_lane = lax.broadcasted_iota(jnp.int32, (8, 256), 1)
+    select = (sel_row == sel_lane // 128).astype(F32)
+
+    def core_copy(own, i):
+        part = own.part.at[rows(2 * i + (1 - c)), :]
+        return remote(part, own.core.at[i], own.sems[0].at[i], own.sems[1].at[i], me.partner())
+
+    def plane_copy(own, i, k):
+        piece = own.part.at[rows(2 * i + c), cols(me.peer_t(k))]
+        return remote(
+            piece,
+            own.plane.at[i, k - 1],
+            own.sems[2].at[i, k - 1],
+            own.sems[3].at[i, k - 1],
+            me.plane(k),
+        )
+
+    def line_copy(own, i):
+        return remote(
+            own.part.at[rows(2 * i + c), cols(t)],
+            own.line.at[z],
+            own.sems[4].at[i],
+            own.sems[5].at[z],
+            me.at_z(i),
+        )
+
+    def core_sum(own, i):
+        core_copy(own, i).wait_recv()
+
+        def add(chunk):
+            where = pl.ds(pl.multiple_of((2 * i + c) * TB + chunk.start, 64), 64)
+            own.part[where, :] = (
+                own.part[where, :].astype(F32) + own.core[i, chunk, :].astype(F32)
+            ).astype(BF16)
+
+        row_chunks(add)
+        for k in (3, 1, 2):
+            plane_copy(own, i, k).start()
+
+    def expert_block(step, carry):
+        i = step % 4
+        late = step // 4
+        block = 2 * i + (1 - c) + late * (2 * c - 1)
+        where = rows(block)
+        gate_up = jnp.dot(r.hn[where, :], r.w_moe[:, 0:512], preferred_element_type=F32)
+        v = jnp.dot(r.d_moe[where, :], r.w_moe[:, 512:768], preferred_element_type=F32)
+        g, u = gate_up[:, 0:256], gate_up[:, 256:512]
+        scale = contract(r.comb[block, :, 0:TB], spread, 0, 0, lax.Precision.HIGHEST)
+        sig = 1.0 / (1.0 + jnp.exp(-g))
+        silu = g * sig
+        active = (silu * u).astype(BF16).astype(F32)
+        r.cz[where, :] = (scale * active).astype(BF16)
+        dc = contract(select, active * v, 1, 1, lax.Precision.HIGHEST)
+        r.dc_own[block, :, 0:TB] = dc
+        dz = scale * v
+        r.dgu[where, 0:256] = (dz * u * sig * (1.0 + g * (1.0 - sig))).astype(BF16)
+        r.dgu[where, 256:512] = (dz * silu).astype(BF16)
+        dgu = r.dgu[where, :]
+        for n in range(3):
+            lanes = slice(512 * n, 512 * (n + 1))
+            r.h.part[where, lanes] = contract(dgu, r.w_moe[lanes, 0:512], 1, 1).astype(BF16)
+
+        @pl.when(late == 0)
+        def _():
+            core_copy(r.h, i).start()
+
+        @pl.when(late == 1)
+        def _():
+            core_sum(r.h, i)
+
+        return carry
+
+    lax.fori_loop(0, NBLK, expert_block, 0)
+
+    dc_send, dc_recv = r.aa.dc
+    for k in range(1, NBLK):
+        peer = me.other(k)
+        pend.start(
+            remote(
+                r.dc_own.at[peer], r.dc_in.at[b], dc_send.at[k], dc_recv.at[b],
+                me.at_block(peer),
+            )
+        )
+    r.dc_in[b] = r.dc_own[b]
+
+    def output_block(step, carry):
+        i = step % 4
+        late = step // 4
+        block = 2 * i + (1 - c) + late * (2 * c - 1)
+        where = rows(block)
+        cz = r.cz[where, :]
+        for n in range(3):
+            lanes = slice(512 * n, 512 * (n + 1))
+            r.y.part[where, lanes] = contract(cz, r.w_moe[lanes, 512:768], 1, 1).astype(BF16)
+
+        @pl.when(late == 0)
+        def _():
+            core_copy(r.y, i).start()
+
+        @pl.when(late == 1)
+        def _():
+            core_sum(r.y, i)
+
+        return carry
+
+    lax.fori_loop(0, NBLK, output_block, 0)
+
+    def weight_grads(n, carry):
+        lanes = pl.ds(pl.multiple_of(n * 256, 256), 256)
+        r.g_moe[lanes, 0:512] = contract(r.hn[:, lanes], r.dgu[...], 0, 0).astype(BF16)
+        r.g_moe[lanes, 512:768] = contract(r.d_moe[:, lanes], r.cz[...], 0, 0).astype(BF16)
+        return carry
+
+    lax.fori_loop(0, DM // 256, weight_grads, 0)
+
+    def plane_sum(own):
+        def step(i, carry):
+            for k in (1, 2, 3):
+                plane_copy(own, i, k).wait_recv()
+            total = own.part[rows(2 * i + c), cols(t)].astype(F32)
+            for k in range(3):
+                total = total + own.plane[i, k].astype(F32)
+            total = total.astype(BF16)
+
+            @pl.when(i == z)
+            def _():
+                own.line[z] = total
+
+            @pl.when(i != z)
+            def _():
+                own.part[rows(2 * i + c), cols(t)] = total
+                line_copy(own, i).start()
+
+            return carry
+
+        lax.fori_loop(0, 4, step, 0)
+
+    def line_wait(own):
+        def step(i, carry):
+            @pl.when(i != z)
+            def _():
+                there = own.line.at[i]
+                remote(there, there, own.sems[4].at[i], own.sems[5].at[i], me.partner()).wait_recv()
+
+            return carry
+
+        lax.fori_loop(0, 4, step, 0)
+        total = own.line[0].astype(F32)
+        for i in range(1, 4):
+            total = total + own.line[i].astype(F32)
+        return total
+
+    def scatter_drain(own):
+        def step(i, carry):
+            core_copy(own, i).wait_send()
+            for k in (1, 2, 3):
+                plane_copy(own, i, k).wait_send()
+
+            @pl.when(i != z)
+            def _():
+                line_copy(own, i).wait_send()
+
+            return carry
+
+        lax.fori_loop(0, 4, step, 0)
+
+    plane_sum(r.h)
+
+    gm_send, gm_recv = r.aa.gm
+    moe_targets = []
+    for which, target in enumerate((r.gate_out, r.up_out, r.down_out)):
+        for e in range(2):
+            moe_targets.append((target, e, pl.ds(256 * which + 128 * e, 128)))
+    for k in range(1, NBLK):
+        peer = me.other(k)
+        for target, e, lanes in moe_targets:
+            remote(
+                r.g_moe.at[rows(peer), lanes],
+                target.at[2 * b + e],
+                gm_send.at[k],
+                gm_recv.at[b],
+                me.at_block(peer),
+            ).start()
+    own_grads = [
+        pltpu.make_async_copy(r.g_moe.at[rows(b), lanes], target.at[2 * b + e], loc.at[4 + i])
+        for i, (target, e, lanes) in enumerate(moe_targets)
+    ]
+    for copy in own_grads:
+        copy.start()
+
+    for k in range(1, NBLK):
+        peer = me.other(k)
+        there = r.dc_in.at[peer]
+        remote(there, there, dc_send.at[k], dc_recv.at[peer], me.partner()).wait_recv()
+    dcp_send, dcp_recv = r.pl.dc
+    dc_copies = [
+        remote(
+            r.dc_in, r.dc_plane.at[k - 1], dcp_send.at[k - 1], dcp_recv.at[k - 1], me.plane(k)
+        )
+        for k in (1, 2, 3)
+    ]
+    for copy in dc_copies:
+        pend.start(copy)
+    for copy in dc_copies:
+        copy.wait_recv()
+    for k in range(NBLK):
+        total = r.dc_in[k] + r.dc_plane[0, k] + r.dc_plane[1, k] + r.dc_plane[2, k]
+        r.dc_t[2 * k : 2 * k + 2, :] = total[0:2, :]
+    dc = r.dc_t[:, 0:TB]
+    combine = r.comb[b, :, 0:TB]
+    d_logits = combine * (dc - jnp.sum(combine * dc, axis=0, keepdims=True))
+    d_logits = d_logits.astype(BF16)
+    r.flat[0:16, :] = jnp.dot(d_logits, r.hn[rows(b), :], preferred_element_type=F32)
+
+    r.dhn[:, cols(t)] = line_wait(r.h).astype(BF16)
+    plane_gather(r.pl.dh, r.dhn.at[:, cols(t)], lambda k: r.dhn.at[:, cols(me.peer_t(k))])()
+
+    r.dh[...] = r.dhn[...].astype(F32) + contract(d_logits, r.router_t[...], 0, 0)
+    r.flat[16:24, :] = jnp.zeros((8, DM), F32)
+
+    def norm_two_back(chunk):
+        dhn = r.dh[chunk, :]
+        unit = r.hidden[chunk, :] * r.r_two[chunk, :]
+        r.flat[16:17, :] += jnp.sum(dhn * unit, axis=0, keepdims=True)
+        du = dhn * r.gains[1:2, :]
+        mean = jnp.mean(du * unit, axis=1, keepdims=True)
+        dh = r.gout[chunk, :] + r.r_two[chunk, :] * (du - unit * mean)
+        r.dh[chunk, :] = dh
+        r.dproj[chunk, :] = (residual_scale * dh).astype(BF16)
+
+    row_chunks(norm_two_back)
+
+    def to_owners(store, sems, width):
+        send, recv = sems
+        for k in range(NBLK):
+            store.own[k, :, 0:TB] = r.flat[0:width, TB * k : TB * (k + 1)]
+        store.inn[b] = store.own[b]
+        for k in range(1, NBLK):
+            peer = me.other(k)
+            pend.start(
+                remote(
+                    store.own.at[peer], store.inn.at[b], send.at[k], recv.at[b],
+                    me.at_block(peer),
+                )
+            )
+
+        def wait():
+            for k in range(1, NBLK):
+                peer = me.other(k)
+                there = store.inn.at[peer]
+                remote(there, there, send.at[k], recv.at[peer], me.partner()).wait_recv()
+            total = store.inn[0]
+            for k in range(1, NBLK):
+                total = total + store.inn[k]
+            return total
+
+        return wait
+
+    wait_sm = to_owners(r.sm, r.aa.sm, 24)
+
+    d_o = contract(r.dproj[...], r.w_out[cols(t), :], 1, 1).astype(BF16).astype(F32)
+    for h in range(NQ):
+        pair = h // 2
+        dh_z = head_from_chunk(d_o[:, 128 * pair : 128 * (pair + 1)], h)
+        den = r.den[h]
+        r.dnz[h] = (dh_z / den).astype(BF16)
+        r.shift[h] = (
+            jnp.broadcast_to(jnp.sum(dh_z * r.oz[h], axis=1, keepdims=True), (TB, 128)) / den
+        )
+        r.dq[h] = jnp.zeros((TB, 128), F32)
+
+    def out_grads(n, carry):
+        lanes = pl.ds(pl.multiple_of(n * 256, 256), 256)
+        g_out_part[lanes, :] = contract(
+            r.o_full[:, lanes], r.dproj[:, cols(t)], 0, 0
+        ).astype(BF16)
+        return carry
+
+    lax.fori_loop(0, DM // 256, out_grads, 0)
+
+    class Reduce:
+        def __init__(self, part, own):
+            self.part, self.core, self.line, self.sems = part, own.core, own.line, own.sems
+
+        def core_copy(self, i):
+            return remote(
+                self.part.at[rows(2 * i + (1 - c)), :],
+                self.core.at[i],
+                self.sems[0].at[i],
+                self.sems[1].at[i],
+                me.partner(),
+            )
+
+        def line_copy(self, i):
+            return remote(
+                self.part.at[rows(2 * i + c), :],
+                self.line.at[z],
+                self.sems[2].at[i],
+                self.sems[3].at[z],
+                me.at_z(i),
+            )
+
+        def start(self):
+            def step(i, carry):
+                self.core_copy(i).start()
+                return carry
+
+            lax.fori_loop(0, 4, step, 0)
+
+        def middle(self):
+            def step(i, carry):
+                self.core_copy(i).wait_recv()
+                where = rows(2 * i + c)
+                total = self.part[where, :].astype(F32) + self.core[i].astype(F32)
+                total = total.astype(BF16)
+                self.part[where, :] = total
+
+                @pl.when(i == z)
+                def _():
+                    self.line[z] = total
+
+                @pl.when(i != z)
+                def _():
+                    self.line_copy(i).start()
+
+                return carry
+
+            lax.fori_loop(0, 4, step, 0)
+
+        def total(self):
+            def step(i, carry):
+                @pl.when(i != z)
+                def _():
+                    there = self.line.at[i]
+                    remote(
+                        there, there, self.sems[2].at[i], self.sems[3].at[i], me.partner()
+                    ).wait_recv()
+
+                return carry
+
+            lax.fori_loop(0, 4, step, 0)
+            total = self.line[0].astype(F32)
+            for i in range(1, 4):
+                total = total + self.line[i].astype(F32)
+            return total
+
+        def drain(self):
+            def step(i, carry):
+                self.core_copy(i).wait_send()
+
+                @pl.when(i != z)
+                def _():
+                    self.line_copy(i).wait_send()
+
+                return carry
+
+            lax.fori_loop(0, 4, step, 0)
+
+    red_out = Reduce(g_out_part, r.rd.go)
+    red_out.start()
+
+    plane_sum(r.y)
+
+    def clear(i, carry):
+        r.dkv[rows(i), :] = jnp.zeros((TB, 256), BF16)
+        return carry
+
+    lax.fori_loop(0, NBLK, clear, 0)
+
+    def attend_back(kb, carry):
+        keys = r.kv[rows(kb), 0:128]
+        values = r.kv[rows(kb), 128:256]
+        mask = allowed(kb)
+        dk = jnp.zeros((TB, 128), F32)
+        dv = jnp.zeros((TB, 128), F32)
+        for h in range(NQ):
+            q = r.qz[h]
+            dn = r.dnz[h]
+            scores = contract(q, keys, 1, 1) * score_scale
+            e = jnp.where(mask, jnp.exp(scores), 0.0)
+            dp = contract(dn, values, 1, 1)
+            ds = (e * (dp - r.shift[h][:, 0:1])).astype(BF16)
+            r.dq[h] += jnp.dot(ds, keys, preferred_element_type=F32)
+            dk = dk + contract(ds, q, 0, 0)
+            dv = dv + contract(e.astype(BF16), dn, 0, 0)
+        r.dkv[rows(kb), 0:128] = (dk * score_scale).astype(BF16)
+        r.dkv[rows(kb), 128:256] = dv.astype(BF16)
+        return carry
+
+    lax.fori_loop(first_block, b + 1, attend_back, 0)
+    red_kv = Reduce(r.dkv, r.rd.dkv)
+    red_kv.start()
+    red_out.middle()
+    for pair in range(3):
+        heads = [
+            jnp.where(half_mask(h // 3), r.dq[h] * score_scale, 0.0)
+            for h in (2 * pair, 2 * pair + 1)
+        ]
+        u = chunk_from_heads(heads[0], heads[1], pair).astype(BF16).astype(F32)
+        r.dqkv[:, 128 * pair : 128 * (pair + 1)] = (
+            u * cosine - swap_halves(u) * sine
+        ).astype(BF16)
+    red_kv.middle()
+    r.g_out_sum[...] = red_out.total().astype(BF16)
+    go_send, go_recv = r.pl.go
+    own_go = pltpu.make_async_copy(r.g_out_sum, r.g_out_out.at[:, cols(t)], loc.at[0])
+    own_go.start()
+    for k in (3, 1, 2):
+        pend.start(
+            remote(
+                r.g_out_sum, r.g_out_out.at[:, cols(t)], go_send.at[k - 1], go_recv.at[k - 1],
+                me.plane(k),
+            )
+        )
+    d_kv = red_kv.total().astype(BF16)
+    u = d_kv[:, 0:128].astype(F32)
+    r.dqkv[:, 384:512] = (u * cosine - swap_halves(u) * sine).astype(BF16)
+    r.dqkv[:, 512:640] = d_kv[:, 128:256]
+
+    for n in range(3):
+        lanes = slice(512 * n, 512 * (n + 1))
+        r.dx[:, lanes] = contract(r.dqkv[...], r.w_qkv[lanes, :], 1, 1).astype(BF16)
+    xs_send, xs_recv = r.pl.xs
+    dx_copies = [
+        remote(
+            r.dx.at[:, cols(me.peer_t(k))], r.dx_in.at[k - 1], xs_send.at[k - 1],
+            xs_recv.at[k - 1], me.plane(k),
+        )
+        for k in (3, 1, 2)
+    ]
+    for copy in dx_copies:
+        pend.start(copy)
+
+    def qkv_grads(n, carry):
+        lanes = pl.ds(pl.multiple_of(n * 256, 256), 256)
+        g_qkv_part[lanes, :] = contract(r.xn[:, lanes], r.dqkv[...], 0, 0).astype(BF16)
+        return carry
+
+    lax.fori_loop(0, DM // 256, qkv_grads, 0)
+    red_qkv = Reduce(g_qkv_part, r.rd.gq)
+    red_qkv.start()
+    for copy in dx_copies:
+        copy.wait_recv()
+    total = r.dx[:, cols(t)].astype(F32)
+    for k in range(3):
+        total = total + r.dx_in[k].astype(F32)
+    r.dxn[:, cols(t)] = total.astype(BF16)
+    wait_dx = plane_gather(
+        r.pl.xg, r.dxn.at[:, cols(t)], lambda k: r.dxn.at[:, cols(me.peer_t(k))]
+    )
+    red_qkv.middle()
+    r.block_out[...] = r.hidden[:, cols(t)] + residual_scale * line_wait(r.y)
+    wait_dx()
+    r.flat[0:8, :] = jnp.zeros((8, DM), F32)
+
+    def norm_one_back(chunk):
+        dxn = r.dxn[chunk, :].astype(F32)
+        factor = r.r_one[chunk, :]
+        unit = r.x[chunk, :].astype(F32) * factor
+        r.flat[0:1, :] += jnp.sum(dxn * unit, axis=0, keepdims=True)
+        du = dxn * r.gains[0:1, :]
+        mean = jnp.mean(du * unit, axis=1, keepdims=True)
+        r.grad_in[chunk, :] = r.dh[chunk, :] + factor * (du - unit * mean)
+
+    row_chunks(norm_one_back)
+    wait_sn = to_owners(r.sn, r.aa.sn, 8)
+    r.g_qkv_sum[...] = red_qkv.total().astype(BF16)
+    gq_send, gq_recv = r.pl.gq
+    own_gq = pltpu.make_async_copy(r.g_qkv_sum, r.g_qkv_out.at[t], loc.at[1])
+    own_gq.start()
+    for k in (3, 1, 2):
+        pend.start(
+            remote(
+                r.g_qkv_sum, r.g_qkv_out.at[t], gq_send.at[k - 1], gq_recv.at[k - 1],
+                me.plane(k),
+            )
+        )
+    r.sm_out[...] = wait_sm()
+    r.sn_out[...] = wait_sn()
+
+    for k in (1, 2, 3):
+        there = r.g_out_out.at[:, cols(me.peer_t(k))]
+        remote(there, there, go_send.at[k - 1], go_recv.at[k - 1], me.plane(k)).wait_recv()
+        there = r.g_qkv_out.at[me.peer_t(k)]
+        remote(there, there, gq_send.at[k - 1], gq_recv.at[k - 1], me.plane(k)).wait_recv()
+    own_go.wait()
+    own_gq.wait()
+    for copy in own_grads:
+        copy.wait()
+    for k in range(1, NBLK):
+        peer = me.other(k)
+        whole = r.g_moe.at[rows(peer), :]
+        remote(whole, whole, gm_send.at[k], gm_recv.at[peer], me.partner()).wait_recv()
+        remote(whole, whole, gm_send.at[k], gm_recv.at[peer], me.partner()).wait_send()
+        remote(whole, whole, moe_send.at[k], moe_recv.at[peer], me.partner()).wait_send()
+    scatter_drain(r.h)
+    scatter_drain(r.y)
+    red_out.drain()
+    red_kv.drain()
+    red_qkv.drain()
+    pend.drain()
+
+
+def fast_body(
+    block_input,
+    segments,
+    routes,
+    attn_gain,
+    ffn_gain,
+    query_weight,
+    key_matrix,
+    value_matrix,
+    out_weight,
+    router_weight,
+    gate_weight,
+    up_weight,
+    down_weight,
+    grad_output,
+):
+    block = 2 * lax.axis_index("fsdp") + lax.axis_index("heads")
+    start = block * TB
+    positions = start + jnp.arange(TB, dtype=jnp.int32)
+    half = HEAD_DIM // 2
+    inverse = rope_base ** (-(jnp.arange(half, dtype=F32) * 2.0 / HEAD_DIM))
+    angles = positions[:, None].astype(F32) * inverse[None, :]
+    cosine, sine = jnp.cos(angles), jnp.sin(angles)
+    rope_c = jnp.concatenate([cosine] * 4, axis=1)
+    rope_s = jnp.concatenate([-sine, sine, -sine, sine], axis=1)
+    seg_rows = segments.reshape(NBLK, TB)
+    seg_k = jnp.pad(seg_rows, ((0, 0), (0, 256 - TB)))
+    seg_q = lax.dynamic_slice_in_dim(segments, start, TB, 0)[:, None]
+    mask_t = jnp.sum(
+        (routes.T[:, None, :] == jnp.arange(E, dtype=jnp.int32)[None, :, None]).astype(F32), axis=0
+    )
+    small = jnp.concatenate(
+        [router_weight.T, attn_gain[None], ffn_gain[None], jnp.zeros((14, TB), BF16)], axis=0
+    )
+    small = jnp.pad(small, ((0, 0), (0, 256 - TB)))
+    down_t = down_weight.transpose(0, 2, 1)
+
+    vmem, hbm = pl.BlockSpec(memory_space=pltpu.VMEM), pl.BlockSpec(memory_space=pl.ANY)
+    ins = dict(
+        x=(block_input, vmem), gout=(grad_output, vmem), rope_c=(rope_c, vmem),
+        rope_s=(rope_s, vmem), seg_q=(seg_q, vmem), seg_k=(seg_k, vmem), mask_t=(mask_t, vmem),
+        small_own=(small, vmem), wq=(query_weight, hbm), wk=(key_matrix, hbm),
+        wv=(value_matrix, hbm), wo=(out_weight, hbm), gate=(gate_weight, hbm),
+        up=(up_weight, hbm), down_t=(down_t, hbm),
+    )
+    outs = dict(
+        block_out=((TB, TC), F32, vmem),
+        grad_in=((TB, DM), F32, vmem),
+        sm_out=((24, 256), F32, vmem),
+        sn_out=((8, 256), F32, vmem),
+        g_qkv_out=((4, TB, 640), BF16, hbm),
+        g_out_out=((TB, DM), BF16, hbm),
+        gate_out=((E, TB, 128), BF16, hbm),
+        up_out=((E, TB, 128), BF16, hbm),
+        down_out=((E, TB, 128), BF16, hbm),
+    )
+    leaves, tree = jax.tree.flatten(scratch_tree())
+
+    def entry(*refs):
+        table = bags(jax.tree.unflatten(tree, refs[len(ins) + len(outs) :]))
+        table.update(zip((*ins, *outs), refs))
+        kernel(table)
+
+    results = pl.pallas_call(
+        entry,
+        name="layer",
+        out_shape=[jax.ShapeDtypeStruct(shape, kind) for shape, kind, _ in outs.values()],
+        in_specs=[spec for _, spec in ins.values()],
+        out_specs=[spec for _, _, spec in outs.values()],
+        scratch_shapes=leaves,
+        compiler_params=pltpu.CompilerParams(
+            collective_id=0, has_side_effects=True, vmem_limit_bytes=VMEM_BYTES
+        ),
+    )(*[value for value, _ in ins.values()])
+    res = Bag(zip(outs, results))
+    g_qkv = res.g_qkv_out.astype(F32).transpose(1, 0, 2)
+    return (
+        res.block_out,
+        res.grad_in,
+        res.sn_out[0, :TB],
+        res.sm_out[16, :TB],
+        g_qkv[:, :, 0:384].reshape(TB, DM),
+        g_qkv[:, :, 384:512].reshape(TB, 512),
+        g_qkv[:, :, 512:640].reshape(TB, 512),
+        res.g_out_out.astype(F32),
+        res.sm_out[0:16, :TB].T,
+        res.gate_out.astype(F32),
+        res.up_out.astype(F32),
+        res.down_out.astype(F32).transpose(0, 2, 1),
+    )
+
+
+VMEM_BYTES = 67043328
+
+
+def fits(mesh):
+    return (mesh.shape["fsdp"], mesh.shape["heads"], mesh.shape["tensor"]) == (4, 2, 4)
+
+
 def solution(mesh):
     in_specs = (
         P(("fsdp", "heads"), None),
@@ -441,4 +1580,5 @@
         P(None, ("fsdp", "heads"), "tensor"),
         P(None, "tensor", ("fsdp", "heads")),
     )
-    return jax.shard_map(body, mesh=mesh, in_specs=in_specs, out_specs=out_specs, check_vma=False)
+    chosen = fast_body if fits(mesh) else body
+    return jax.shard_map(chosen, mesh=mesh, in_specs=in_specs, out_specs=out_specs, check_vma=False)

time: 1150 us -> 328 us (0.29)
  waiting for transfers between devices: 586 us -> 0 us
  Pallas kernels: 0 us -> 300 us
  matrix products: 213 us -> 0 us
  blocking collectives: 152 us -> 0 us
  local copies, waits for them, and re-layouts: 112 us -> 12.7 us
  other arithmetic: 37.1 us -> 9.79 us
  loops' own time: 16.3 us -> 0 us
  between operations: 16.6 us -> 0.73 us
    reduce_scatter x9 -> x0, waiting for transfers between devices: 402 us -> none  [the longest x1 68.2 us: body(): lax.psum_scatter(gate_full.astype(jnp.bfloat16), ('fsdp', 'heads'), scatt...]
    pallas_call x0 -> x1, Pallas kernels: none -> 300 us  [fast_body(): pl.pallas_call(entry, name='layer', out_shape=[jax.ShapeDtypeStruct(shape...]
    dot_general x51 -> x0, matrix products: 212 us -> none  [the longest x8 42.1 us: masked_exp(): jnp.einsum('qkgd,jkd->kgqj', query_vectors, key_block, preferred_element_...]
    all_gather x7 -> x0, waiting for transfers between devices: 148 us -> none  [the longest x1 59.7 us: body(): lax.all_gather(down_weight, ('fsdp', 'heads'), axis=2, tiled=True)]
    all_gather x3 -> x0, blocking collectives: 67.9 us -> none  [the longest x1 30.7 us: body(): lax.all_gather(value_local, 'fsdp', axis=0, tiled=True)]
    all_to_all x8 -> x0, blocking collectives: 35.2 us -> none  [the longest x1 5.69 us: body(): lax.all_to_all(attn_send, 'heads', split_axis=0, concat_axis=1, tiled=True)]
    convert_element_type x12 -> x0, local copies, waits for them, and re-layouts: 33.4 us -> none  [the longest x1 9.08 us: body(): up_full.astype(jnp.bfloat16)]
    unnamed x2 -> x0, blocking collectives: 32.3 us -> none
  transfers between devices with their start and end apart: 19 -> 0, of which waited for: 13 -> 0; matrix products, arithmetic and copies ran while one was open for 17% -> 0% of each run, Pallas kernels for 0% -> 0%
where the time goes in v2:
time: 328 us; the launch traced here: 323 us
  Pallas kernels  300 us (91%)
  local copies, waits for them, and re-layouts  12.7 us (4%)
  other arithmetic  9.79 us (3%)
    pallas_call x1, Pallas kernels, fast_body(): pl.pallas_call(entry, name='layer', out_shape=[jax.ShapeDtypeStruct(shape...  300 us

profile of v2, /device:TPU:16, one launch (start us, length us, event | category | flops | bytes accessed | tf_op | source)
XLA Modules:
  0.0 323.5 jit_solution(13172136237110988324)
XLA Ops:
  1.1 0.9 pad_maximum_fusion
  2.0 0.8 dynamic_slice.3
  2.8 0.8 copy.30.refs_4_
  3.5 0.8 reshape.49
  4.3 0.6 pad.8.refs_5_
  4.9 1.3 convert_reduce_fusion.refs_6_
  6.2 0.7 broadcast_in_dim.18
  6.9 0.7 broadcast_in_dim.17
  7.6 0.8 maximum_maximum_fusion
  8.4 0.6 pad.9.refs_7_
  9.0 300.3 %layer.1 = (f32[192,384]{1,0:T(8,128)}, f32[192,1536]{1,0:T(8,128)}, f32[24,256]{1,0:T(8,128)}, f32[8,256]{1,0:T(8,128)}, bf16[4,192,640]{2,1,0:T(8,128)(2,1)}, ...) custom-call(bf16[192,1536]{1,0:T(8,128)(2,1)} %refs_0_.1, ...), custom_call_target="tpu_custom_call" | custom-call | tf_op jit(solution)/shard_map/layer/pallas_call | solution.py:1516
  309.3 1.3 slice.18
  310.6 1.3 slice.19
  311.8 1.3 convert_bitcast_fusion
  313.2 1.2 copy.34
  314.5 0.8 copy.40
  315.3 0.8 copy.39
  316.1 1.1 convert_element_type.26
  317.2 0.6 slice_bitcast_fusion.3
  317.8 1.3 convert_element_type.27
  319.1 1.3 convert_element_type.28
  320.4 1.3 convert_bitcast_fusion.1
  321.7 0.7 copy.43
  322.4 1.0 copy.44
  (21 shorter events, 0.7 us)
Async XLA Ops:
  314.4 1.7 copy-start.4
  314.4 2.8 copy-start.6
  314.5 3.4 %copy-start.3 = (bf16[16,192,128]{2,1,0:T(8,128)(2,1)S(1)}, bf16[16,192,128]{2,1,0:T(8,128)(2,1)}, u32[]{:S(2)}) copy-start(bf16[16,192,128]{2,1,0:T(8,128)(2,1)} %get-tuple-element.27) | copy-start | bytes 2359300
  317.2 1.9 copy-start.2
  319.1 1.3 copy-start.1
  320.4 1.3 copy-start.5
  320.4 2.0 copy-start

commit v3 on v2

--- a/solution.py
+++ b/solution.py
@@ -484,6 +484,12 @@
     def middle(self):
         return self.z * (3 - self.z) > 0
 
+    def dest(self, j):
+        inner = (self.z * (3 - self.z)) // 2
+        turned = j + inner * (j // 2) * (1 - 2 * (j % 2))
+        upper = self.z // 2
+        return 3 * (1 - upper) + (2 * upper - 1) * turned
+
 
 def remote(src, dst, send_sem, recv_sem, device):
     return pltpu.make_async_remote_copy(
@@ -573,6 +579,72 @@
             ).wait_recv()
 
 
+class UpGather(LineGather):
+    def start(self):
+        me = self.me
+        own = self.view(me.b)
+        self.pend.start(
+            remote(own, own, self.send.at[0], self.recv.at[me.z], me.at_z(me.z + 1)),
+            me.z < 2 + me.c,
+        )
+        self.pend.start(remote(own, own, self.psend.at[3], self.precv.at[me.z], me.partner()))
+
+    def near(self, core):
+        return self.me.z * (3 + core - self.me.z) > 0
+
+    def take(self, source):
+        block = self.view(2 * source + self.me.c)
+        remote(
+            block, block, self.send.at[0], self.recv.at[source], self.me.partner()
+        ).wait_recv()
+        return block
+
+    def relay(self):
+        me = self.me
+
+        @pl.when(self.near(me.c))
+        def _():
+            self.take(me.z - 1)
+
+        block = self.view(2 * (me.z - 1) + me.c)
+        self.pend.start(
+            remote(block, block, self.send.at[1], self.recv.at[me.z - 1], me.at_z(me.z + 1)),
+            me.z == 1,
+        )
+        self.pend.start(
+            remote(block, block, self.psend.at[0], self.precv.at[me.z - 1], me.partner()),
+            self.near(me.c),
+        )
+
+        @pl.when(me.z == 2)
+        def _():
+            self.take(0)
+
+        block = self.view(me.c)
+        self.pend.start(
+            remote(block, block, self.psend.at[1], self.precv.at[0], me.partner()), me.z == 2
+        )
+
+    def finish(self):
+        me = self.me
+
+        def take(source):
+            block = self.view(2 * source + (1 - me.c))
+            remote(
+                block, block, self.psend.at[0], self.precv.at[source], me.partner()
+            ).wait_recv()
+
+        take(me.z)
+
+        @pl.when(self.near(1 - me.c))
+        def _():
+            take(me.z - 1)
+
+        @pl.when(me.z == 2)
+        def _():
+            take(0)
+
+
 class FullGather(LineGather):
     def __init__(self, me, pend, buffer, sems):
         super().__init__(
@@ -585,8 +657,9 @@
         self.buffer = buffer
         self.xsend, self.xrecv = sems[4:]
 
-    def arrive(self, i):
-        source, block = super().arrive(i)
+    def spread(self, i):
+        source = self.me.arrival(i)
+        block = self.line_view(2 * source + self.me.c)
         for k in (3, 1, 2):
             self.pend.start(
                 remote(
@@ -672,12 +745,14 @@
             part=b16(DM, DM),
             core=b16(4, TB, DM),
             plane=b16(4, 3, TB, TC),
-            line=b16(4, TB, TC),
-            sems=(*pair(4), *pair(4, 3), *pair(4)),
+            line=b16(6, TB, TC),
+            sems=(*pair(4), *pair(4, 3), dma((3,)), dma((6,))),
         )
 
     def reduce(width):
-        return dict(core=b16(4, TB, width), line=b16(4, TB, width), sems=(*pair(4), *pair(4)))
+        return dict(
+            core=b16(4, TB, width), line=b16(6, TB, width), sems=(*pair(4), dma((3,)), dma((6,)))
+        )
 
     return dict(
         w_qkv=b16(DM, 640),
@@ -708,6 +783,7 @@
         dc_plane=f32(3, NBLK, 8, 256),
         dc_t=f32(16, 256),
         g_moe=b16(DM, 768),
+        acc=f32(TB, 640),
         dh=f32(TB, DM),
         dproj=b16(TB, DM),
         flat=f32(24, DM),
@@ -724,9 +800,9 @@
         dx_in=b16(3, TB, TC),
         dxn=b16(TB, DM),
         local_sem=dma((10,)),
-        lg=dict(s=line(), w=line(), kv=line(), c=line()),
+        lg=dict(s=line(), w=line(), v=line(), kv=line(), c=line()),
         fg=dict(wo=full(), dm=full(), hn=full()),
-        aa=dict(wm=pair(8), gm=pair(8), dc=pair(8), sm=pair(8), sn=pair(8)),
+        aa=dict(wm=[pair(8), pair(8)], gm=[pair(8), pair(8)], dc=pair(8), sm=pair(8), sn=pair(8)),
         pl=dict(o=pair(3), dc=pair(3), dh=pair(3), go=pair(3), gq=pair(3), xs=pair(3), xg=pair(3)),
         rd=dict(go=reduce(TC), dkv=reduce(256), gq=reduce(640)),
     )
@@ -752,13 +828,14 @@
         ),
         pltpu.make_async_copy(r.wo, r.w_out.at[rows(b), :], loc.at[3]),
     ]
-    moe_sources = []
-    for which, shard in enumerate((r.gate, r.up, r.down_t)):
-        for e in range(2):
-            moe_sources.append((shard, e, pl.ds(256 * which + 128 * e, 128)))
+    moe_lanes = [[pl.ds(384 * e + 128 * which, 128) for which in range(3)] for e in range(2)]
+    moe_sources = [list(zip((r.gate, r.up, r.down_t), lanes)) for lanes in moe_lanes]
     own_moe = [
-        pltpu.make_async_copy(shard.at[2 * b + e], r.w_moe.at[rows(b), lanes], loc.at[4 + i])
-        for i, (shard, e, lanes) in enumerate(moe_sources)
+        pltpu.make_async_copy(
+            shard.at[2 * b + e], r.w_moe.at[rows(b), lanes], loc.at[4 + 3 * e + i]
+        )
+        for e in range(2)
+        for i, (shard, lanes) in enumerate(moe_sources[e])
     ]
     for copy in local:
         copy.start()
@@ -779,20 +856,43 @@
         return LineGather(me, pend, view, view, sems)
 
     g_small = line(lambda k: r.small.at[k], r.lg.s)
-    g_qkv = line(lambda k: r.w_qkv.at[rows(k), :], r.lg.w)
-    g_kv = line(lambda k: r.kv.at[rows(k), :], r.lg.kv)
+    def half(h):
+        return lambda k: r.w_qkv.at[pl.ds(pl.multiple_of(TB * k + 96 * h, 96), 96), :]
+
+    g_qkv = [line(half(h), sems) for h, sems in enumerate((r.lg.w, r.lg.v))]
+    kv_view = lambda k: r.kv.at[rows(k), :]
+    g_kv = UpGather(me, pend, kv_view, kv_view, r.lg.kv)
     g_comb = line(lambda k: r.comb.at[k], r.lg.c)
     g_wout = FullGather(me, pend, r.w_out, r.fg.wo)
     g_dmoe = FullGather(me, pend, r.d_moe, r.fg.dm)
     g_hn = FullGather(me, pend, r.hn, r.fg.hn)
 
+    def send_weights(e, ks):
+        send, recv = r.aa.wm[e]
+        for k in ks:
+            peer = me.other(k)
+            for shard, lanes in moe_sources[e]:
+                remote(
+                    shard.at[2 * peer + e],
+                    r.w_moe.at[rows(b), lanes],
+                    send.at[k],
+                    recv.at[b],
+                    me.at_block(peer),
+                ).start()
+
+    def weights_from(e, k):
+        send, recv = r.aa.wm[e]
+        peer = me.other(k)
+        whole = r.w_moe.at[rows(peer), pl.ds(384 * e, 384)]
+        return remote(whole, whole, send.at[k], recv.at[peer], me.partner())
+
     g_small.start()
     for copy in local[:3]:
         copy.wait()
-    g_qkv.start()
+    for g in g_qkv:
+        g.start()
     local[3].wait()
     g_wout.start()
-    g_dmoe.start()
 
     def rms_one(chunk):
         v = r.x[chunk, :].astype(F32)
@@ -802,9 +902,12 @@
     for i in range(3):
         g_small.arrive(i)
         g_small.share(i)
-        g_qkv.arrive(i)
-        g_qkv.share(i)
-        g_wout.arrive(i)
+        for g in g_qkv:
+            g.arrive(i)
+            g.share(i)
+        if i == 1:
+            g_wout.arrive(0)
+            g_wout.spread(0)
     g_small.finish()
     for k in range(NBLK):
         piece = r.small[k].astype(F32)
@@ -816,7 +919,8 @@
         r.xn[chunk, :] = (v * r.r_one[chunk, :] * r.gains[0:1, :]).astype(BF16)
 
     row_chunks(normalize_one)
-    g_qkv.finish()
+    for g in g_qkv:
+        g.finish()
     qkv = jnp.dot(r.xn[...], r.w_qkv[...], preferred_element_type=F32)
     cosine, sine = r.rope_c[...], r.rope_s[...]
     key = qkv[:, 384:512]
@@ -831,22 +935,13 @@
     for h in range(NQ):
         r.oz[h] = jnp.zeros((TB, 128), F32)
         r.den[h] = jnp.zeros((TB, 128), F32)
-    for i in range(3):
-        g_kv.arrive(i)
-        g_kv.share(i)
-        g_dmoe.arrive(i)
-
-    moe_send, moe_recv = r.aa.wm
-    for k in range(1, NBLK):
-        peer = me.other(k)
-        for shard, e, lanes in moe_sources:
-            remote(
-                shard.at[2 * peer + e],
-                r.w_moe.at[rows(b), lanes],
-                moe_send.at[k],
-                moe_recv.at[b],
-                me.at_block(peer),
-            ).start()
+    g_kv.relay()
+    for i in (1, 2):
+        g_wout.arrive(i)
+        g_wout.spread(i)
+    g_dmoe.start()
+    send_weights(0, (1, 7, 2))
+
     g_kv.finish()
 
     first_block = FIRST_DOC_BLOCKS * (b // FIRST_DOC_BLOCKS)
@@ -869,8 +964,6 @@
         return carry
 
     lax.fori_loop(first_block, b + 1, attend, 0)
-    for i in range(3):
-        g_wout.cross(i)
     for pair in range(3):
         heads = []
         for h in (2 * pair, 2 * pair + 1):
@@ -897,6 +990,12 @@
     wait_o = plane_gather(
         r.pl.o, r.o_full.at[:, cols(t)], lambda k: r.o_full.at[:, cols(me.peer_t(k))]
     )
+    for i in range(3):
+        g_dmoe.arrive(i)
+        g_dmoe.spread(i)
+    send_weights(0, (6,))
+    for i in range(3):
+        g_wout.cross(i)
     g_wout.finish()
     wait_o()
 
@@ -926,11 +1025,14 @@
     r.comb[b, :, 0:TB] = combine
     g_comb.start()
     for i in range(3):
-        g_dmoe.cross(i)
-    for i in range(3):
+        g_hn.arrive(i)
+        g_hn.spread(i)
         g_comb.arrive(i)
         g_comb.share(i)
-        g_hn.arrive(i)
+        send_weights(0, (3 + i,))
+    send_weights(1, (4, 3, 5, 2, 6, 1, 7))
+    for i in range(3):
+        g_dmoe.cross(i)
     g_dmoe.finish()
     g_comb.finish()
     for i in range(3):
@@ -939,16 +1041,10 @@
     for copy in own_moe:
         copy.wait()
     for k in range(1, NBLK):
-        peer = me.other(k)
-        whole = r.w_moe.at[rows(peer), :]
-        remote(whole, whole, moe_send.at[k], moe_recv.at[peer], me.partner()).wait_recv()
-
-    lane = lax.broadcasted_iota(jnp.int32, (16, 256), 1)
-    expert = lax.broadcasted_iota(jnp.int32, (16, 256), 0)
-    spread = (expert == 2 * b + lane // 128).astype(F32)
-    sel_row = lax.broadcasted_iota(jnp.int32, (8, 256), 0)
-    sel_lane = lax.broadcasted_iota(jnp.int32, (8, 256), 1)
-    select = (sel_row == sel_lane // 128).astype(F32)
+        weights_from(0, k).wait_recv()
+
+    expert = lax.broadcasted_iota(jnp.int32, (16, 128), 0)
+    first_row = (lax.broadcasted_iota(jnp.int32, (8, 128), 0) == 0).astype(F32)
 
     def core_copy(own, i):
         part = own.part.at[rows(2 * i + (1 - c)), :]
@@ -986,28 +1082,87 @@
         for k in (3, 1, 2):
             plane_copy(own, i, k).start()
 
-    def expert_block(step, carry):
-        i = step % 4
+    def expert_block(e, where, block):
+        base = 384 * e
+        gate_up = jnp.dot(
+            r.hn[where, :], r.w_moe[:, base : base + 256], preferred_element_type=F32
+        )
+        v = jnp.dot(
+            r.d_moe[where, :], r.w_moe[:, base + 256 : base + 384], preferred_element_type=F32
+        )
+        g, u = gate_up[:, 0:128], gate_up[:, 128:256]
+        chosen_one = (expert == 2 * b + e).astype(F32)
+        scale = contract(r.comb[block, :, 0:TB], chosen_one, 0, 0, lax.Precision.HIGHEST)
+        sig = 1.0 / (1.0 + jnp.exp(-g))
+        silu = g * sig
+        active = (silu * u).astype(BF16).astype(F32)
+        r.cz[where, 128 * e : 128 * (e + 1)] = (scale * active).astype(BF16)
+        dc = contract(first_row, active * v, 1, 1, lax.Precision.HIGHEST)
+        r.dc_own[block, e : e + 1, 0:TB] = dc[0:1, :]
+        dz = scale * v
+        r.dgu[where, 256 * e : 256 * e + 128] = (dz * u * sig * (1.0 + g * (1.0 - sig))).astype(
+            BF16
+        )
+        r.dgu[where, 256 * e + 128 : 256 * e + 256] = (dz * silu).astype(BF16)
+
+    def expert_one(block, carry):
+        expert_block(0, rows(block), block)
+        return carry
+
+    lax.fori_loop(0, NBLK, expert_one, 0)
+
+    def weight_grads(e):
+        def step(n, carry):
+            lanes = pl.ds(pl.multiple_of(n * 256, 256), 256)
+            base = 384 * e
+            r.g_moe[lanes, base : base + 256] = contract(
+                r.hn[:, lanes], r.dgu[:, 256 * e : 256 * (e + 1)], 0, 0
+            ).astype(BF16)
+            r.g_moe[lanes, base + 256 : base + 384] = contract(
+                r.d_moe[:, lanes], r.cz[:, 128 * e : 128 * (e + 1)], 0, 0
+            ).astype(BF16)
+            return carry
+
+        lax.fori_loop(0, DM // 256, step, 0)
+
+    moe_targets = [list(zip((r.gate_out, r.up_out, r.down_out), lanes)) for lanes in moe_lanes]
+
+    def send_grads(e, ks):
+        send, recv = r.aa.gm[e]
+        for k in ks:
+            peer = me.other(k)
+            for target, lanes in moe_targets[e]:
+                remote(
+                    r.g_moe.at[rows(peer), lanes],
+                    target.at[2 * b + e],
+                    send.at[k],
+                    recv.at[b],
+                    me.at_block(peer),
+                ).start()
+
+    def grads_copy(e, k):
+        send, recv = r.aa.gm[e]
+        peer = me.other(k)
+        whole = r.g_moe.at[rows(peer), pl.ds(384 * e, 384)]
+        return remote(whole, whole, send.at[k], recv.at[peer], me.partner())
+
+    weight_grads(0)
+    send_grads(0, (1, 7, 2, 6, 3))
+    for k in range(1, NBLK):
+        weights_from(1, k).wait_recv()
+
+    def expert_two(step, carry):
+        i = me.dest(step % 4)
         late = step // 4
         block = 2 * i + (1 - c) + late * (2 * c - 1)
         where = rows(block)
-        gate_up = jnp.dot(r.hn[where, :], r.w_moe[:, 0:512], preferred_element_type=F32)
-        v = jnp.dot(r.d_moe[where, :], r.w_moe[:, 512:768], preferred_element_type=F32)
-        g, u = gate_up[:, 0:256], gate_up[:, 256:512]
-        scale = contract(r.comb[block, :, 0:TB], spread, 0, 0, lax.Precision.HIGHEST)
-        sig = 1.0 / (1.0 + jnp.exp(-g))
-        silu = g * sig
-        active = (silu * u).astype(BF16).astype(F32)
-        r.cz[where, :] = (scale * active).astype(BF16)
-        dc = contract(select, active * v, 1, 1, lax.Precision.HIGHEST)
-        r.dc_own[block, :, 0:TB] = dc
-        dz = scale * v
-        r.dgu[where, 0:256] = (dz * u * sig * (1.0 + g * (1.0 - sig))).astype(BF16)
-        r.dgu[where, 256:512] = (dz * silu).astype(BF16)
-        dgu = r.dgu[where, :]
+        expert_block(1, where, block)
         for n in range(3):
             lanes = slice(512 * n, 512 * (n + 1))
-            r.h.part[where, lanes] = contract(dgu, r.w_moe[lanes, 0:512], 1, 1).astype(BF16)
+            r.h.part[where, lanes] = (
+                contract(r.dgu[where, 0:256], r.w_moe[lanes, 0:256], 1, 1)
+                + contract(r.dgu[where, 256:512], r.w_moe[lanes, 384:640], 1, 1)
+            ).astype(BF16)
 
         @pl.when(late == 0)
         def _():
@@ -1019,7 +1174,7 @@
 
         return carry
 
-    lax.fori_loop(0, NBLK, expert_block, 0)
+    lax.fori_loop(0, NBLK, expert_two, 0)
 
     dc_send, dc_recv = r.aa.dc
     for k in range(1, NBLK):
@@ -1032,107 +1187,93 @@
         )
     r.dc_in[b] = r.dc_own[b]
 
-    def output_block(step, carry):
-        i = step % 4
-        late = step // 4
-        block = 2 * i + (1 - c) + late * (2 * c - 1)
-        where = rows(block)
-        cz = r.cz[where, :]
-        for n in range(3):
-            lanes = slice(512 * n, 512 * (n + 1))
-            r.y.part[where, lanes] = contract(cz, r.w_moe[lanes, 512:768], 1, 1).astype(BF16)
-
-        @pl.when(late == 0)
-        def _():
-            core_copy(r.y, i).start()
-
-        @pl.when(late == 1)
-        def _():
-            core_sum(r.y, i)
-
-        return carry
-
-    lax.fori_loop(0, NBLK, output_block, 0)
-
-    def weight_grads(n, carry):
-        lanes = pl.ds(pl.multiple_of(n * 256, 256), 256)
-        r.g_moe[lanes, 0:512] = contract(r.hn[:, lanes], r.dgu[...], 0, 0).astype(BF16)
-        r.g_moe[lanes, 512:768] = contract(r.d_moe[:, lanes], r.cz[...], 0, 0).astype(BF16)
-        return carry
-
-    lax.fori_loop(0, DM // 256, weight_grads, 0)
-
-    def plane_sum(own):
-        def step(i, carry):
-            for k in (1, 2, 3):
-                plane_copy(own, i, k).wait_recv()
-            total = own.part[rows(2 * i + c), cols(t)].astype(F32)
-            for k in range(3):
-                total = total + own.plane[i, k].astype(F32)
-            total = total.astype(BF16)
-
-            @pl.when(i == z)
+    weight_grads(1)
+    class Chain:
+        def __init__(self, piece, line, send, recv, arrived):
+            self.piece, self.line, self.send, self.recv = piece, line, send, recv
+            self.arrived = arrived
+
+        def copy(self, j):
+            i = me.dest(j)
+            upper = z // 2
+            inner = (z * (3 - z)) // 2
+            if j == 0:
+                to, slot = z + 1 - 2 * upper, i
+            elif j == 1:
+                to, slot = z + 1 - 2 * upper, i + inner * (4 + upper - i)
+            else:
+                to, slot = i, 4 + z % 2
+            return remote(
+                self.piece(i), self.line.at[slot], self.send.at[j], self.recv.at[slot], me.at_z(to)
+            )
+
+        def wait_slot(self, slot):
+            there = self.line.at[slot]
+            remote(
+                there, there, self.send.at[0], self.recv.at[slot], me.partner()
+            ).wait_recv()
+
+        def step(self, j):
+            i = me.dest(j)
+            self.arrived(i)
+
+            @pl.when(me.middle())
             def _():
-                own.line[z] = total
-
-            @pl.when(i != z)
-            def _():
-                own.part[rows(2 * i + c), cols(t)] = total
-                line_copy(own, i).start()
-
-            return carry
-
-        lax.fori_loop(0, 4, step, 0)
-
-    def line_wait(own):
-        def step(i, carry):
-            @pl.when(i != z)
-            def _():
-                there = own.line.at[i]
-                remote(there, there, own.sems[4].at[i], own.sems[5].at[i], me.partner()).wait_recv()
-
-            return carry
-
-        lax.fori_loop(0, 4, step, 0)
-        total = own.line[0].astype(F32)
-        for i in range(1, 4):
-            total = total + own.line[i].astype(F32)
-        return total
+                self.wait_slot(i)
+                piece = self.piece(i)
+                piece[...] = (piece[...].astype(F32) + self.line[i].astype(F32)).astype(BF16)
+
+            self.copy(j).start()
+
+        def total(self, acc):
+            self.arrived(z)
+            acc[...] = self.piece(z)[...].astype(F32)
+            for slot, there in ((4, z > 0), (5, z < 3)):
+
+                @pl.when(there)
+                def _(slot=slot):
+                    self.wait_slot(slot)
+                    acc[...] += self.line[slot].astype(F32)
+
+        def drain(self):
+            for j in range(3):
+                self.copy(j).wait_send()
+
+    def plane_add(own, i):
+        for k in (1, 2, 3):
+            plane_copy(own, i, k).wait_recv()
+        where = rows(2 * i + c)
+        total = own.part[where, cols(t)].astype(F32)
+        for k in range(3):
+            total = total + own.plane[i, k].astype(F32)
+        own.part[where, cols(t)] = total.astype(BF16)
+
+    def scatter_chain(own):
+        return Chain(
+            lambda i: own.part.at[rows(2 * i + c), cols(t)],
+            own.line,
+            own.sems[4],
+            own.sems[5],
+            lambda i: plane_add(own, i),
+        )
 
     def scatter_drain(own):
         def step(i, carry):
             core_copy(own, i).wait_send()
             for k in (1, 2, 3):
                 plane_copy(own, i, k).wait_send()
-
-            @pl.when(i != z)
-            def _():
-                line_copy(own, i).wait_send()
-
             return carry
 
         lax.fori_loop(0, 4, step, 0)
 
-    plane_sum(r.h)
-
-    gm_send, gm_recv = r.aa.gm
-    moe_targets = []
-    for which, target in enumerate((r.gate_out, r.up_out, r.down_out)):
-        for e in range(2):
-            moe_targets.append((target, e, pl.ds(256 * which + 128 * e, 128)))
-    for k in range(1, NBLK):
-        peer = me.other(k)
-        for target, e, lanes in moe_targets:
-            remote(
-                r.g_moe.at[rows(peer), lanes],
-                target.at[2 * b + e],
-                gm_send.at[k],
-                gm_recv.at[b],
-                me.at_block(peer),
-            ).start()
+    chain_h, chain_y = scatter_chain(r.h), scatter_chain(r.y)
+
     own_grads = [
-        pltpu.make_async_copy(r.g_moe.at[rows(b), lanes], target.at[2 * b + e], loc.at[4 + i])
-        for i, (target, e, lanes) in enumerate(moe_targets)
+        pltpu.make_async_copy(
+            r.g_moe.at[rows(b), lanes], target.at[2 * b + e], loc.at[4 + 3 * e + i]
+        )
+        for e in range(2)
+        for i, (target, lanes) in enumerate(moe_targets[e])
     ]
     for copy in own_grads:
         copy.start()
@@ -1150,6 +1291,37 @@
     ]
     for copy in dc_copies:
         pend.start(copy)
+    def output_block(step, carry):
+        i = me.dest(step % 4)
+        late = step // 4
+        where = rows(2 * i + (1 - c) + late * (2 * c - 1))
+        cz = r.cz[where, :]
+        for n in range(3):
+            lanes = slice(512 * n, 512 * (n + 1))
+            r.y.part[where, lanes] = (
+                contract(cz[:, 0:128], r.w_moe[lanes, 256:384], 1, 1)
+                + contract(cz[:, 128:256], r.w_moe[lanes, 640:768], 1, 1)
+            ).astype(BF16)
+
+        @pl.when(late == 0)
+        def _():
+            core_copy(r.y, i).start()
+
+        return carry
+
+    lax.fori_loop(0, NBLK, output_block, 0)
+
+    for j in range(3):
+        chain_h.step(j)
+        send_grads(0, ((5,), (4,), ())[j])
+    chain_h.total(r.acc.at[:, 0:TC])
+    r.dhn[:, cols(t)] = r.acc[:, 0:TC].astype(BF16)
+    send_grads(1, (1, 7, 2))
+    wait_dh = plane_gather(
+        r.pl.dh, r.dhn.at[:, cols(t)], lambda k: r.dhn.at[:, cols(me.peer_t(k))]
+    )
+    for j in range(4):
+        core_sum(r.y, me.dest(j))
     for copy in dc_copies:
         copy.wait_recv()
     for k in range(NBLK):
@@ -1161,8 +1333,7 @@
     d_logits = d_logits.astype(BF16)
     r.flat[0:16, :] = jnp.dot(d_logits, r.hn[rows(b), :], preferred_element_type=F32)
 
-    r.dhn[:, cols(t)] = line_wait(r.h).astype(BF16)
-    plane_gather(r.pl.dh, r.dhn.at[:, cols(t)], lambda k: r.dhn.at[:, cols(me.peer_t(k))])()
+    wait_dh()
 
     r.dh[...] = r.dhn[...].astype(F32) + contract(d_logits, r.router_t[...], 0, 0)
     r.flat[16:24, :] = jnp.zeros((8, DM), F32)
@@ -1227,9 +1398,12 @@
 
     lax.fori_loop(0, DM // 256, out_grads, 0)
 
-    class Reduce:
+    class Reduce(Chain):
         def __init__(self, part, own):
-            self.part, self.core, self.line, self.sems = part, own.core, own.line, own.sems
+            self.part, self.core, self.sems = part, own.core, own.sems
+            super().__init__(
+                lambda i: part.at[rows(2 * i + c), :], own.line, own.sems[2], own.sems[3], self.chip
+            )
 
         def core_copy(self, i):
             return remote(
@@ -1240,75 +1414,61 @@
                 me.partner(),
             )
 
-        def line_copy(self, i):
-            return remote(
-                self.part.at[rows(2 * i + c), :],
-                self.line.at[z],
-                self.sems[2].at[i],
-                self.sems[3].at[z],
-                me.at_z(i),
-            )
-
         def start(self):
-            def step(i, carry):
-                self.core_copy(i).start()
-                return carry
-
-            lax.fori_loop(0, 4, step, 0)
-
-        def middle(self):
-            def step(i, carry):
-                self.core_copy(i).wait_recv()
-                where = rows(2 * i + c)
-                total = self.part[where, :].astype(F32) + self.core[i].astype(F32)
-                total = total.astype(BF16)
-                self.part[where, :] = total
-
-                @pl.when(i == z)
-                def _():
-                    self.line[z] = total
-
-                @pl.when(i != z)
-                def _():
-                    self.line_copy(i).start()
-
-                return carry
-
-            lax.fori_loop(0, 4, step, 0)
-
-        def total(self):
-            def step(i, carry):
-                @pl.when(i != z)
-                def _():
-                    there = self.line.at[i]
+            for j in range(4):
+                self.core_copy(me.dest(j)).start()
+
+        def chip(self, i):
+            self.core_copy(i).wait_recv()
+            piece = self.piece(i)
+            piece[...] = (piece[...].astype(F32) + self.core[i].astype(F32)).astype(BF16)
+
+        def drain(self):
+            super().drain()
+            self.drain_core()
+
+        def drain_core(self):
+            for i in range(4):
+                self.core_copy(i).wait_send()
+
+        def down(self):
+            for i in range(4):
+                self.chip(i)
+
+            @pl.when(z == 1)
+            def _():
+                self.wait_slot(0)
+                piece = self.piece(0)
+                piece[...] = (piece[...].astype(F32) + self.line[0].astype(F32)).astype(BF16)
+
+            for i, slot, when in (
+                (0, 0, z == 2),
+                (1, 5, z == 2),
+                (0, 5, z == 1),
+                (2, 5, z + c == 4),
+            ):
+                pend.start(
                     remote(
-                        there, there, self.sems[2].at[i], self.sems[3].at[i], me.partner()
-                    ).wait_recv()
-
-                return carry
-
-            lax.fori_loop(0, 4, step, 0)
-            total = self.line[0].astype(F32)
-            for i in range(1, 4):
-                total = total + self.line[i].astype(F32)
-            return total
-
-        def drain(self):
-            def step(i, carry):
-                self.core_copy(i).wait_send()
-
-                @pl.when(i != z)
-                def _():
-                    self.line_copy(i).wait_send()
-
-                return carry
-
-            lax.fori_loop(0, 4, step, 0)
-
+                        self.piece(i),
+                        self.line.at[slot],
+                        self.send.at[1 if i == 1 else 0],
+                        self.recv.at[slot],
+                        me.at_z(z - 1),
+                    ),
+                    when,
+                )
+
+        def down_total(self, acc):
+            acc[...] = self.piece(z)[...].astype(F32)
+
+            @pl.when(z < 2 + c)
+            def _():
+                self.wait_slot(5)
+                acc[...] += self.line[5].astype(F32)
+
+    send_grads(1, (6, 3))
     red_out = Reduce(g_out_part, r.rd.go)
     red_out.start()
-
-    plane_sum(r.y)
 
     def clear(i, carry):
         r.dkv[rows(i), :] = jnp.zeros((TB, 256), BF16)
@@ -1339,7 +1499,6 @@
     lax.fori_loop(first_block, b + 1, attend_back, 0)
     red_kv = Reduce(r.dkv, r.rd.dkv)
     red_kv.start()
-    red_out.middle()
     for pair in range(3):
         heads = [
             jnp.where(half_mask(h // 3), r.dq[h] * score_scale, 0.0)
@@ -1349,8 +1508,53 @@
         r.dqkv[:, 128 * pair : 128 * (pair + 1)] = (
             u * cosine - swap_halves(u) * sine
         ).astype(BF16)
-    red_kv.middle()
-    r.g_out_sum[...] = red_out.total().astype(BF16)
+    red_kv.down()
+    send_grads(1, (5,))
+    for j in range(3):
+        red_out.step(j)
+    d_kv_acc = r.acc.at[:, 384:640]
+    red_kv.down_total(d_kv_acc)
+    d_kv = d_kv_acc[...].astype(BF16)
+    u = d_kv[:, 0:128].astype(F32)
+    r.dqkv[:, 384:512] = (u * cosine - swap_halves(u) * sine).astype(BF16)
+    r.dqkv[:, 512:640] = d_kv[:, 128:256]
+
+    for n in range(3):
+        lanes = slice(512 * n, 512 * (n + 1))
+        r.dx[:, lanes] = contract(r.dqkv[...], r.w_qkv[lanes, :], 1, 1).astype(BF16)
+    xs_send, xs_recv = r.pl.xs
+    dx_copies = [
+        remote(
+            r.dx.at[:, cols(me.peer_t(k))], r.dx_in.at[k - 1], xs_send.at[k - 1],
+            xs_recv.at[k - 1], me.plane(k),
+        )
+        for k in (3, 1, 2)
+    ]
+    for copy in dx_copies:
+        pend.start(copy)
+
+    def qkv_grads(n, carry):
+        lanes = pl.ds(pl.multiple_of(n * 256, 256), 256)
+        g_qkv_part[lanes, :] = contract(r.xn[:, lanes], r.dqkv[...], 0, 0).astype(BF16)
+        return carry
+
+    lax.fori_loop(0, DM // 256, qkv_grads, 0)
+    red_qkv = Reduce(g_qkv_part, r.rd.gq)
+    red_qkv.start()
+    for j in range(3):
+        red_qkv.step(j)
+    send_grads(1, (4,))
+    for copy in dx_copies:
+        copy.wait_recv()
+    total = r.dx[:, cols(t)].astype(F32)
+    for k in range(3):
+        total = total + r.dx_in[k].astype(F32)
+    r.dxn[:, cols(t)] = total.astype(BF16)
+    wait_dx = plane_gather(
+        r.pl.xg, r.dxn.at[:, cols(t)], lambda k: r.dxn.at[:, cols(me.peer_t(k))]
+    )
+    red_out.total(r.acc.at[:, 0:TC])
+    r.g_out_sum[...] = r.acc[:, 0:TC].astype(BF16)
     go_send, go_recv = r.pl.go
     own_go = pltpu.make_async_copy(r.g_out_sum, r.g_out_out.at[:, cols(t)], loc.at[0])
     own_go.start()
@@ -1361,44 +1565,8 @@
                 me.plane(k),
             )
         )
-    d_kv = red_kv.total().astype(BF16)
-    u = d_kv[:, 0:128].astype(F32)
-    r.dqkv[:, 384:512] = (u * cosine - swap_halves(u) * sine).astype(BF16)
-    r.dqkv[:, 512:640] = d_kv[:, 128:256]
-
-    for n in range(3):
-        lanes = slice(512 * n, 512 * (n + 1))
-        r.dx[:, lanes] = contract(r.dqkv[...], r.w_qkv[lanes, :], 1, 1).astype(BF16)
-    xs_send, xs_recv = r.pl.xs
-    dx_copies = [
-        remote(
-            r.dx.at[:, cols(me.peer_t(k))], r.dx_in.at[k - 1], xs_send.at[k - 1],
-            xs_recv.at[k - 1], me.plane(k),
-        )
-        for k in (3, 1, 2)
-    ]
-    for copy in dx_copies:
-        pend.start(copy)
-
-    def qkv_grads(n, carry):
-        lanes = pl.ds(pl.multiple_of(n * 256, 256), 256)
-        g_qkv_part[lanes, :] = contract(r.xn[:, lanes], r.dqkv[...], 0, 0).astype(BF16)
-        return carry
-
-    lax.fori_loop(0, DM // 256, qkv_grads, 0)
-    red_qkv = Reduce(g_qkv_part, r.rd.gq)
-    red_qkv.start()
-    for copy in dx_copies:
-        copy.wait_recv()
-    total = r.dx[:, cols(t)].astype(F32)
-    for k in range(3):
-        total = total + r.dx_in[k].astype(F32)
-    r.dxn[:, cols(t)] = total.astype(BF16)
-    wait_dx = plane_gather(
-        r.pl.xg, r.dxn.at[:, cols(t)], lambda k: r.dxn.at[:, cols(me.peer_t(k))]
-    )
-    red_qkv.middle()
-    r.block_out[...] = r.hidden[:, cols(t)] + residual_scale * line_wait(r.y)
+    for j in range(3):
+        chain_y.step(j)
     wait_dx()
     r.flat[0:8, :] = jnp.zeros((8, DM), F32)
 
@@ -1413,7 +1581,8 @@
 
     row_chunks(norm_one_back)
     wait_sn = to_owners(r.sn, r.aa.sn, 8)
-    r.g_qkv_sum[...] = red_qkv.total().astype(BF16)
+    red_qkv.total(r.acc)
+    r.g_qkv_sum[...] = r.acc[...].astype(BF16)
     gq_send, gq_recv = r.pl.gq
     own_gq = pltpu.make_async_copy(r.g_qkv_sum, r.g_qkv_out.at[t], loc.at[1])
     own_gq.start()
@@ -1424,6 +1593,8 @@
                 me.plane(k),
             )
         )
+    chain_y.total(r.acc.at[:, 0:TC])
+    r.block_out[...] = r.hidden[:, cols(t)] + residual_scale * r.acc[:, 0:TC]
     r.sm_out[...] = wait_sm()
     r.sn_out[...] = wait_sn()
 
@@ -1437,15 +1608,15 @@
     for copy in own_grads:
         copy.wait()
     for k in range(1, NBLK):
-        peer = me.other(k)
-        whole = r.g_moe.at[rows(peer), :]
-        remote(whole, whole, gm_send.at[k], gm_recv.at[peer], me.partner()).wait_recv()
-        remote(whole, whole, gm_send.at[k], gm_recv.at[peer], me.partner()).wait_send()
-        remote(whole, whole, moe_send.at[k], moe_recv.at[peer], me.partner()).wait_send()
+        for e in range(2):
+            grads_copy(e, k).wait()
+            weights_from(e, k).wait_send()
     scatter_drain(r.h)
     scatter_drain(r.y)
+    chain_h.drain()
+    chain_y.drain()
     red_out.drain()
-    red_kv.drain()
+    red_kv.drain_core()
     red_qkv.drain()
     pend.drain()
 

time: 328 us -> 272 us (0.83)
  Pallas kernels: 300 us -> 247 us
    pallas_call x1, Pallas kernels: 300 us -> 247 us  [fast_body(): pl.pallas_call(entry, name='layer', out_shape=[jax.ShapeDtypeStruct(shape...]
where the time goes in v3:
time: 272 us; the launch traced here: 271 us
  Pallas kernels  247 us (91%)
  local copies, waits for them, and re-layouts  12.7 us (5%)
  other arithmetic  9.79 us (4%)
    pallas_call x1, Pallas kernels, fast_body(): pl.pallas_call(entry, name='layer', out_shape=[jax.ShapeDtypeStruct(shape...  247 us

profile of v3, /device:TPU:16, one launch (start us, length us, event | category | flops | bytes accessed | tf_op | source)
XLA Modules:
  0.0 270.7 jit_solution(9746287781985700070)
XLA Ops:
  1.1 0.9 pad_maximum_fusion
  2.0 0.8 dynamic_slice.3
  2.8 0.8 copy.30.refs_4_
  3.5 0.8 reshape.49
  4.3 0.6 pad.8.refs_5_
  4.9 1.3 convert_reduce_fusion.refs_6_
  6.2 0.7 broadcast_in_dim.18
  6.9 0.7 broadcast_in_dim.17
  7.6 0.8 maximum_maximum_fusion
  8.4 0.6 pad.9.refs_7_
  9.0 247.5 %layer.1 = (f32[192,384]{1,0:T(8,128)}, f32[192,1536]{1,0:T(8,128)}, f32[24,256]{1,0:T(8,128)}, f32[8,256]{1,0:T(8,128)}, bf16[4,192,640]{2,1,0:T(8,128)(2,1)}, ...) custom-call(bf16[192,1536]{1,0:T(8,128)(2,1)} %refs_0_.1, ...), custom_call_target="tpu_custom_call" | custom-call | tf_op jit(solution)/shard_map/layer/pallas_call | solution.py:1687
  256.5 1.3 slice.18
  257.8 1.3 slice.19
  259.0 1.3 convert_bitcast_fusion
  260.4 1.2 copy.34
  261.7 0.8 copy.40
  262.5 0.8 copy.39
  263.3 1.1 convert_element_type.26
  264.4 0.6 slice_bitcast_fusion.3
  265.0 1.3 convert_element_type.27
  266.3 1.3 convert_element_type.28
  267.6 1.3 convert_bitcast_fusion.1
  268.9 0.7 copy.43
  269.6 1.0 copy.44
  (21 shorter events, 0.7 us)
Async XLA Ops:
  261.6 1.7 copy-start.4
  261.7 2.8 %copy-start.6 = (f32[24,256]{1,0:T(8,128)S(1)}, f32[24,256]{1,0:T(8,128)}, u32[]{:S(2)}) copy-start(f32[24,256]{1,0:T(8,128)} %get-tuple-element.24) | copy-start | bytes 73732
  261.7 3.4 %copy-start.3 = (bf16[16,192,128]{2,1,0:T(8,128)(2,1)S(1)}, bf16[16,192,128]{2,1,0:T(8,128)(2,1)}, u32[]{:S(2)}) copy-start(bf16[16,192,128]{2,1,0:T(8,128)(2,1)} %get-tuple-element.27) | copy-start | bytes 2359300
  264.4 1.9 copy-start.2
  266.3 1.3 copy-start.1
  267.6 1.3 copy-start.5
  267.6 2.0 copy-start

commit v4 on v3

--- a/solution.py
+++ b/solution.py
@@ -2,6 +2,7 @@
 
 import jax
 import jax.numpy as jnp
+import numpy as np
 from jax import lax
 from jax.experimental import pallas as pl
 from jax.experimental.pallas import tpu as pltpu
@@ -419,8 +420,10 @@
 TB = 192
 DM = 1536
 TC = 384
+HALF = 96
 NBLK = 8
 NQ = 6
+TOPK = 8
 FIRST_DOC_BLOCKS = 5
 
 
@@ -507,6 +510,10 @@
         self.items = []
 
     def start(self, copy, when=None):
+        self.begin(copy, when)
+        self.later(copy, when)
+
+    def begin(self, copy, when=None):
         if when is None:
             copy.start()
         else:
@@ -515,6 +522,7 @@
             def _():
                 copy.start()
 
+    def later(self, copy, when=None):
         self.items.append((copy, when))
 
     def drain(self):
@@ -531,22 +539,33 @@
 
 
 class LineGather:
-    def __init__(self, me, pend, view, line_view, sems):
+    def __init__(self, me, pend, view, line_view, several, several_line, sems):
         self.me, self.pend, self.view, self.line_view = me, pend, view, line_view
+        self.several, self.several_line = several, several_line
         self.send, self.recv, self.psend, self.precv = sems
+
+    def bytes_of(self, ref, send_sem, recv_sem):
+        return remote(ref, ref, send_sem.at[0], recv_sem.at[0], self.me.partner())
 
     def start(self):
         me = self.me
         own = self.line_view(me.b)
-        self.pend.start(
-            remote(own, own, self.send.at[0], self.recv.at[me.z], me.at_z(me.z + 1)), me.z < 3
-        )
-        self.pend.start(
-            remote(own, own, self.send.at[1], self.recv.at[me.z], me.at_z(me.z - 1)), me.z > 0
-        )
-        whole = self.view(me.b)
-        self.pend.start(
-            remote(whole, whole, self.psend.at[3], self.precv.at[me.z], me.partner())
+        for dz, when in ((1, me.z < 3), (-1, me.z > 0)):
+            self.pend.begin(
+                remote(own, own, self.send.at[0], self.recv.at[me.z], me.at_z(me.z + dz)), when
+            )
+        for count, when in ((5, me.middle()), (1, me.z * (3 - me.z) == 0)):
+            self.pend.later(self.bytes_of(self.several_line(count), self.send, self.recv), when)
+        self.share_own()
+
+    def share_own(self):
+        self.share_block(self.me.b)
+        self.pend.later(self.bytes_of(self.several(4), self.psend, self.precv))
+
+    def share_block(self, block):
+        whole = self.view(block)
+        self.pend.begin(
+            remote(whole, whole, self.psend.at[0], self.precv.at[0], self.me.partner())
         )
 
     def arrive(self, i):
@@ -554,32 +573,25 @@
         source = me.arrival(i)
         block = self.line_view(2 * source + me.c)
         remote(block, block, self.send.at[0], self.recv.at[source], me.partner()).wait_recv()
-        self.pend.start(
+        self.pend.begin(
             remote(
-                block, block, self.send.at[2 + i], self.recv.at[source], me.at_z(me.forward_to(i))
+                block, block, self.send.at[0], self.recv.at[source], me.at_z(me.forward_to(i))
             ),
             me.middle(),
         )
-        return source, block
 
     def share(self, i):
-        me = self.me
-        source = me.arrival(i)
-        whole = self.view(2 * source + me.c)
-        self.pend.start(
-            remote(whole, whole, self.psend.at[i], self.precv.at[source], me.partner())
-        )
+        self.share_block(2 * self.me.arrival(i) + self.me.c)
 
     def finish(self):
-        me = self.me
-        for source in range(4):
-            whole = self.view(2 * source + (1 - me.c))
-            remote(
-                whole, whole, self.psend.at[0], self.precv.at[source], me.partner()
-            ).wait_recv()
+        self.bytes_of(self.several(4), self.psend, self.precv).wait_recv()
 
 
 class UpGather(LineGather):
+    def __init__(self, me, pend, view, sems):
+        self.me, self.pend, self.view = me, pend, view
+        self.send, self.recv, self.psend, self.precv = sems
+
     def start(self):
         me = self.me
         own = self.view(me.b)
@@ -652,33 +664,44 @@
             pend,
             lambda block: buffer.at[rows(block), :],
             lambda block: buffer.at[rows(block), cols(me.t)],
+            lambda count: buffer.at[0 : TB * count, :],
+            lambda count: buffer.at[0 : TB * count, 0:TC],
             sems[:4],
         )
         self.buffer = buffer
         self.xsend, self.xrecv = sems[4:]
 
+    def piece(self, i, k):
+        lanes = cols(self.me.t if k == 0 else self.me.peer_t(k))
+        return self.buffer.at[rows(2 * self.me.arrival(i) + self.me.c), lanes]
+
+    def part(self, i, k, half):
+        start = (2 * self.me.arrival(i) + self.me.c) * TB + HALF * half
+        return self.buffer.at[pl.ds(pl.multiple_of(start, HALF), HALF), cols(self.me.peer_t(k))]
+
+    def copy(self, view, i, relayed, k):
+        return remote(
+            view,
+            view,
+            self.xsend.at[0],
+            self.xrecv.at[relayed, self.me.arrival(i)],
+            self.me.plane(k),
+        )
+
     def spread(self, i):
-        source = self.me.arrival(i)
-        block = self.line_view(2 * source + self.me.c)
-        for k in (3, 1, 2):
-            self.pend.start(
-                remote(
-                    block,
-                    block,
-                    self.xsend.at[i, k - 1],
-                    self.xrecv.at[k - 1, source],
-                    self.me.plane(k),
-                )
-            )
+        for k in (1, 2):
+            self.pend.begin(self.copy(self.piece(i, 0), i, 0, k))
+        if i == 2:
+            nine = self.buffer.at[0:864, 0:768]
+            self.pend.later(self.copy(nine, i, 0, 1))
+
+    def relay(self, i):
+        self.copy(self.buffer.at[0 : 2 * TB, 0:TC], i, 0, 1).wait_recv()
+        for k in (1, 2):
+            self.pend.begin(self.copy(self.part(i, k, k - 1), i, 1, 3 - k))
 
     def cross(self, i):
-        me = self.me
-        source = me.arrival(i)
-        for k in (1, 2, 3):
-            piece = self.buffer.at[rows(2 * source + me.c), cols(me.peer_t(k))]
-            remote(
-                piece, piece, self.xsend.at[i, k - 1], self.xrecv.at[k - 1, source], me.plane(k)
-            ).wait_recv()
+        self.copy(self.buffer.at[0:TB, 0:TC], i, 1, 1).wait_recv()
         self.share(i)
 
 
@@ -735,28 +758,34 @@
         return (dma(shape), dma(shape))
 
     def line():
-        return (dma((5,)), dma((4,)), dma((4,)), dma((4,)))
+        return (dma((1,)), dma((4,)), dma((1,)), dma((1,)))
+
+    def up():
+        return (dma((2,)), dma((4,)), dma((4,)), dma((4,)))
 
     def full():
-        return (*line(), dma((3, 3)), dma((3, 4)))
+        return (*line(), dma((1,)), dma((2, 4)))
 
     def scatter():
         return dict(
             part=b16(DM, DM),
             core=b16(4, TB, DM),
-            plane=b16(4, 3, TB, TC),
+            plane=b16(4, 2, TB, TC),
+            diagonal=b16(4, 2, HALF, TC),
             line=b16(6, TB, TC),
-            sems=(*pair(4), *pair(4, 3), dma((3,)), dma((6,))),
+            sems=(dma((1,)), dma((4,)), dma((1,)), dma((4, 2)), dma((1,)), dma((6,))),
         )
 
     def reduce(width):
         return dict(
-            core=b16(4, TB, width), line=b16(6, TB, width), sems=(*pair(4), dma((3,)), dma((6,)))
+            core=b16(4, TB, width),
+            line=b16(6, TB, width),
+            sems=(dma((1,)), dma((4,)), dma((2,)), dma((6,))),
         )
 
     return dict(
         w_qkv=b16(DM, 640),
-        small=b16(NBLK, 32, 256),
+        small=f32(NBLK, 24, 256),
         w_out=b16(DM, DM),
         d_moe=b16(DM, DM),
         hn=b16(DM, DM),
@@ -783,7 +812,7 @@
         dc_plane=f32(3, NBLK, 8, 256),
         dc_t=f32(16, 256),
         g_moe=b16(DM, 768),
-        acc=f32(TB, 640),
+        acc=f32(TB, TC),
         dh=f32(TB, DM),
         dproj=b16(TB, DM),
         flat=f32(24, DM),
@@ -791,26 +820,30 @@
         sn=dict(own=f32(NBLK, 8, 256), inn=f32(NBLK, 8, 256)),
         g_out_sum=b16(TB, TC),
         dnz=b16(NQ, TB, 128),
-        shift=f32(NQ, TB, 128),
-        dq=f32(NQ, TB, 128),
         dkv=b16(DM, 256),
         dqkv=b16(TB, 640),
         g_qkv_sum=b16(TB, 640),
         dx=b16(TB, DM),
         dx_in=b16(3, TB, TC),
         dxn=b16(TB, DM),
-        local_sem=dma((10,)),
-        lg=dict(s=line(), w=line(), v=line(), kv=line(), c=line()),
+        local_sem=dma((11,)),
+        lg=dict(s=line(), w=line(), v=line(), o=line(), kv=up(), c=line()),
         fg=dict(wo=full(), dm=full(), hn=full()),
-        aa=dict(wm=[pair(8), pair(8)], gm=[pair(8), pair(8)], dc=pair(8), sm=pair(8), sn=pair(8)),
-        pl=dict(o=pair(3), dc=pair(3), dh=pair(3), go=pair(3), gq=pair(3), xs=pair(3), xg=pair(3)),
-        rd=dict(go=reduce(TC), dkv=reduce(256), gq=reduce(640)),
+        aa=dict(
+            wm=[pair(1), pair(1)], gm=[pair(1), pair(1)], dc=pair(1), sm=pair(1), sn=pair(1)
+        ),
+        pl=dict(
+            o=pair(1), hc=pair(1), dc=pair(1), dh=pair(1), go=pair(1), gq=pair(1), gk=pair(1),
+            gv=pair(1), xs=pair(1), xg=pair(1),
+        ),
+        rd=dict(go=reduce(TC), dkv=reduce(256), gq=reduce(TC), gkv=reduce(256)),
     )
 
 
 def kernel(r):
     g_out_part = r.dgu.at[:, 0:TC]
-    g_qkv_part = r.w_moe.at[:, 0:640]
+    w_column = r.y.part.at[:, 0:TC]
+    g_q_part, g_kv_part = r.w_moe.at[:, 0:TC], r.w_moe.at[:, TC:640]
     me = Place()
     pend = Pending()
     z, c, t, b = me.z, me.c, me.t, me.b
@@ -826,7 +859,8 @@
             r.wv.at[:, pl.ds(pl.multiple_of(128 * t, 128), 128)],
             r.w_qkv.at[rows(b), 512:640], loc.at[2],
         ),
-        pltpu.make_async_copy(r.wo, r.w_out.at[rows(b), :], loc.at[3]),
+        pltpu.make_async_copy(r.wo.at[:, cols(t)], w_column.at[rows(b), :], loc.at[3]),
+        pltpu.make_async_copy(r.wo, r.w_out.at[rows(b), :], loc.at[10]),
     ]
     moe_lanes = [[pl.ds(384 * e + 128 * which, 128) for which in range(3)] for e in range(2)]
     moe_sources = [list(zip((r.gate, r.up, r.down_t), lanes)) for lanes in moe_lanes]
@@ -848,43 +882,71 @@
         )
     for k in (1, 2, 3):
         pl.semaphore_signal(barrier, inc=1, device_id=me.plane(k), device_id_type=MESH_ID)
-    r.small[b] = r.small_own[...]
+    r.small[b, 0:16, 0:TB] = r.router_own[...].astype(F32)
+    for n in range(2):
+        r.small[b, 16 + n : 17 + n, 0:128] = r.vectors[12 + 2 * n : 13 + 2 * n, :]
+        r.small[b, 16 + n : 17 + n, 128:TB] = r.vectors[13 + 2 * n : 14 + 2 * n, 0:64]
     r.d_moe[rows(b), :] = (residual_scale * r.gout[...]).astype(BF16)
     pl.semaphore_wait(barrier, NBLK - 1 + 3)
 
-    def line(view, sems):
-        return LineGather(me, pend, view, view, sems)
-
-    g_small = line(lambda k: r.small.at[k], r.lg.s)
+    def line(view, several, sems):
+        return LineGather(me, pend, view, view, several, several, sems)
+
+    g_small = line(lambda k: r.small.at[k], lambda n: r.small.at[0:n], r.lg.s)
     def half(h):
         return lambda k: r.w_qkv.at[pl.ds(pl.multiple_of(TB * k + 96 * h, 96), 96), :]
 
-    g_qkv = [line(half(h), sems) for h, sems in enumerate((r.lg.w, r.lg.v))]
-    kv_view = lambda k: r.kv.at[rows(k), :]
-    g_kv = UpGather(me, pend, kv_view, kv_view, r.lg.kv)
-    g_comb = line(lambda k: r.comb.at[k], r.lg.c)
+    g_qkv = [
+        line(half(h), lambda n: r.w_qkv.at[0 : 96 * n, :], sems)
+        for h, sems in enumerate((r.lg.w, r.lg.v))
+    ]
+    g_kv = UpGather(me, pend, lambda k: r.kv.at[rows(k), :], r.lg.kv)
+    g_comb = line(lambda k: r.comb.at[k], lambda n: r.comb.at[0:n], r.lg.c)
+    early = Pending()
+    wcol_view = lambda k: w_column.at[rows(k), :]
+    wcol_several = lambda n: w_column.at[0 : TB * n, :]
+    g_wcol = LineGather(me, early, wcol_view, wcol_view, wcol_several, wcol_several, r.lg.o)
     g_wout = FullGather(me, pend, r.w_out, r.fg.wo)
     g_dmoe = FullGather(me, pend, r.d_moe, r.fg.dm)
     g_hn = FullGather(me, pend, r.hn, r.fg.hn)
 
-    def send_weights(e, ks):
+    def send_weights_to(e, peer):
         send, recv = r.aa.wm[e]
+        for shard, lanes in moe_sources[e]:
+            remote(
+                shard.at[2 * peer + e],
+                r.w_moe.at[rows(b), lanes],
+                send.at[0],
+                recv.at[0],
+                me.at_block(peer),
+            ).start()
+
+    end_chip = z * (3 - z) == 0
+
+    def send_weights_end(e, ks):
+        @pl.when(end_chip)
+        def _():
+            for k in ks:
+                send_weights_to(e, me.other(k))
+
+    def send_weights_inner(e, ks):
         for k in ks:
             peer = me.other(k)
-            for shard, lanes in moe_sources[e]:
-                remote(
-                    shard.at[2 * peer + e],
-                    r.w_moe.at[rows(b), lanes],
-                    send.at[k],
-                    recv.at[b],
-                    me.at_block(peer),
-                ).start()
-
-    def weights_from(e, k):
-        send, recv = r.aa.wm[e]
-        peer = me.other(k)
-        whole = r.w_moe.at[rows(peer), pl.ds(384 * e, 384)]
-        return remote(whole, whole, send.at[k], recv.at[peer], me.partner())
+
+            @pl.when(me.middle() & (peer // 2 + z != 3))
+            def _(peer=peer):
+                send_weights_to(e, peer)
+
+    def send_weights_middle(e):
+        @pl.when(me.middle())
+        def _():
+            for j in range(2):
+                peer = 6 - 2 * z + j
+                send_weights_to(e, peer)
+
+    def seven_blocks(sems):
+        whole = r.w_moe.at[0 : 7 * TB, 0:TC]
+        return remote(whole, whole, sems[0].at[0], sems[1].at[0], me.partner())
 
     g_small.start()
     for copy in local[:3]:
@@ -892,7 +954,7 @@
     for g in g_qkv:
         g.start()
     local[3].wait()
-    g_wout.start()
+    g_wcol.start()
 
     def rms_one(chunk):
         v = r.x[chunk, :].astype(F32)
@@ -906,11 +968,12 @@
             g.arrive(i)
             g.share(i)
         if i == 1:
-            g_wout.arrive(0)
-            g_wout.spread(0)
+            g_wcol.arrive(0)
+            g_wcol.share(0)
+    send_weights_middle(0)
     g_small.finish()
     for k in range(NBLK):
-        piece = r.small[k].astype(F32)
+        piece = r.small[k]
         r.router_t[:, TB * k : TB * (k + 1)] = piece[0:16, 0:TB].astype(BF16)
         r.gains[0:8, TB * k : TB * (k + 1)] = piece[16:24, 0:TB]
 
@@ -922,11 +985,17 @@
     for g in g_qkv:
         g.finish()
     qkv = jnp.dot(r.xn[...], r.w_qkv[...], preferred_element_type=F32)
-    cosine, sine = r.rope_c[...], r.rope_s[...]
+    base_c, base_s = r.rope_block[0, pl.ds(b, 1), :], r.rope_block[1, pl.ds(b, 1), :]
+    row_c, row_s = r.rope_row[0], r.rope_row[1]
+    first_half = lax.broadcasted_iota(jnp.int32, (TB, 128), 1) % 64 < 32
+    cosine = base_c * row_c - base_s * row_s
+    sine = base_s * row_c + base_c * row_s
+    sine = jnp.where(first_half, -sine, sine)
     key = qkv[:, 384:512]
     r.kv[rows(b), 0:128] = (key * cosine + swap_halves(key) * sine).astype(BF16)
     r.kv[rows(b), 128:256] = qkv[:, 512:640].astype(BF16)
     g_kv.start()
+    g_dmoe.start()
     for pair in range(3):
         u = qkv[:, 128 * pair : 128 * (pair + 1)]
         u = (u * cosine + swap_halves(u) * sine).astype(BF16).astype(F32)
@@ -936,31 +1005,41 @@
         r.oz[h] = jnp.zeros((TB, 128), F32)
         r.den[h] = jnp.zeros((TB, 128), F32)
     g_kv.relay()
+    send_weights_middle(1)
     for i in (1, 2):
-        g_wout.arrive(i)
-        g_wout.spread(i)
-    g_dmoe.start()
-    send_weights(0, (1, 7, 2))
+        g_wcol.arrive(i)
+        g_wcol.share(i)
+    g_dmoe.arrive(0)
+    g_dmoe.spread(0)
+    send_weights_inner(0, (1, 7, 2))
+    send_weights_end(0, (1, 7, 2, 6))
 
     g_kv.finish()
 
     first_block = FIRST_DOC_BLOCKS * (b // FIRST_DOC_BLOCKS)
+
+    second_end = (r.vectors[0:12, :] < 1.5).astype(F32)
+    second_end = jnp.sum(jnp.sum(second_end, axis=0, keepdims=True), axis=1, keepdims=True)
 
     def allowed(kb):
         q_pos = b * TB + lax.broadcasted_iota(jnp.int32, (TB, TB), 0)
         k_pos = kb * TB + lax.broadcasted_iota(jnp.int32, (TB, TB), 1)
-        same = r.seg_q[...] == r.seg_k[pl.ds(kb, 1), 0:TB]
-        return (q_pos >= k_pos) & same
+        q_first = (q_pos.astype(F32) < second_end).astype(F32)
+        k_first = (k_pos.astype(F32) < second_end).astype(F32)
+        return (q_pos >= k_pos) & (q_first == k_first)
 
     def attend(kb, carry):
         keys = r.kv[rows(kb), 0:128]
         values = r.kv[rows(kb), 128:256]
         mask = allowed(kb)
-        for h in range(NQ):
-            scores = contract(r.qz[h], keys, 1, 1) * score_scale
-            e = jnp.where(mask, jnp.exp(scores), 0.0)
-            r.den[h] += jnp.broadcast_to(jnp.sum(e, axis=1, keepdims=True), (TB, 128))
-            r.oz[h] += jnp.dot(e.astype(BF16), values, preferred_element_type=F32)
+        for g in range(2):
+            heads = pl.ds(3 * g, 3)
+            q = r.qz[heads].reshape(3 * TB, 128)
+            e = jnp.exp(contract(q, keys, 1, 1) * score_scale).reshape(3, TB, TB)
+            e = jnp.where(mask[None], e, 0.0)
+            r.den[heads] += jnp.broadcast_to(jnp.sum(e, axis=2, keepdims=True), (3, TB, 128))
+            e = e.reshape(3 * TB, TB).astype(BF16)
+            r.oz[heads] += jnp.dot(e, values, preferred_element_type=F32).reshape(3, TB, 128)
         return carry
 
     lax.fori_loop(first_block, b + 1, attend, 0)
@@ -973,43 +1052,33 @@
         chunk = chunk_from_heads(heads[0], heads[1], pair).astype(BF16)
         r.o_full[:, pl.ds(pl.multiple_of(TC * t + 128 * pair, 128), 128)] = chunk
 
-    def plane_gather(sems, own_view, peer_view):
+    def to_plane(sems, copies_of, three, pend=pend):
         send, recv = sems
         for k in (3, 1, 2):
-            pend.start(
-                remote(own_view, own_view, send.at[k - 1], recv.at[k - 1], me.plane(k))
-            )
-
-        def wait():
-            for k in (1, 2, 3):
-                piece = peer_view(k)
-                remote(piece, piece, send.at[k - 1], recv.at[k - 1], me.plane(k)).wait_recv()
-
-        return wait
-
-    wait_o = plane_gather(
-        r.pl.o, r.o_full.at[:, cols(t)], lambda k: r.o_full.at[:, cols(me.peer_t(k))]
-    )
-    for i in range(3):
-        g_dmoe.arrive(i)
-        g_dmoe.spread(i)
-    send_weights(0, (6,))
-    for i in range(3):
-        g_wout.cross(i)
-    g_wout.finish()
+            src, dst = copies_of(k)
+            pend.begin(remote(src, dst, send.at[0], recv.at[0], me.plane(k)))
+        all_three = remote(three, three, send.at[0], recv.at[0], me.plane(1))
+        pend.later(all_three)
+        return all_three.wait_recv
+
+    def plane_gather(sems, buffer, pend=pend):
+        own = buffer.at[:, cols(t)]
+        return to_plane(sems, lambda k: (own, own), buffer.at[:, 0 : 3 * TC], pend)
+
+    wait_o = plane_gather(r.pl.o, r.o_full)
+    send_weights_inner(0, (6, 3))
+    send_weights_end(0, (3, 5))
+    g_wcol.finish()
     wait_o()
 
-    def project(n, carry):
-        lanes = pl.ds(pl.multiple_of(n * 256, 256), 256)
-        r.hidden[:, lanes] = r.x[:, lanes].astype(F32) + residual_scale * jnp.dot(
-            r.o_full[...], r.w_out[:, lanes], preferred_element_type=F32
-        )
-        return carry
-
-    lax.fori_loop(0, DM // 256, project, 0)
+    column = jnp.dot(r.o_full[...], w_column[...], preferred_element_type=F32)
+    r.dx[:, cols(t)] = column.astype(BF16)
+    wait_column = plane_gather(r.pl.hc, r.dx, early)
+    wait_column()
 
     def normalize_two(chunk):
-        v = r.hidden[chunk, :]
+        v = r.x[chunk, :].astype(F32) + residual_scale * r.dx[chunk, :].astype(F32)
+        r.hidden[chunk, :] = v
         factor = lax.rsqrt(jnp.mean(v * v, axis=1, keepdims=True) + norm_eps)
         r.r_two[chunk, :] = factor
         r.dproj[chunk, :] = (v * factor * r.gains[1:2, :]).astype(BF16)
@@ -1018,56 +1087,94 @@
     r.hn[rows(b), :] = r.dproj[...]
     g_hn.start()
     logits = contract(r.router_t[...], r.dproj[...], 1, 1)
-    chosen = r.mask_t[...] > 0.5
+    chosen_expert = lax.broadcasted_iota(jnp.int32, (E, TB), 0)
+    chosen = chosen_expert == r.routes_t[0:1, :]
+    for k in range(1, TOPK):
+        chosen = chosen | (chosen_expert == r.routes_t[k : k + 1, :])
     top = jnp.max(jnp.where(chosen, logits, -1e30), axis=0, keepdims=True)
     weight = jnp.where(chosen, jnp.exp(jnp.where(chosen, logits - top, 0.0)), 0.0)
     combine = weight / jnp.sum(weight, axis=0, keepdims=True)
     r.comb[b, :, 0:TB] = combine
     g_comb.start()
+    g_dmoe.relay(0)
+    for i in (1, 2):
+        g_dmoe.arrive(i)
+        g_dmoe.spread(i)
     for i in range(3):
         g_hn.arrive(i)
         g_hn.spread(i)
         g_comb.arrive(i)
         g_comb.share(i)
-        send_weights(0, (3 + i,))
-    send_weights(1, (4, 3, 5, 2, 6, 1, 7))
+    send_weights_end(0, (4,))
+    send_weights_end(1, (4, 3, 5, 2, 6, 1, 7))
+    send_weights_inner(0, (5, 4))
+    send_weights_inner(1, (4, 3, 5, 2, 6, 1, 7))
+    for i in (1, 2):
+        g_dmoe.relay(i)
+    for i in range(3):
+        g_hn.relay(i)
     for i in range(3):
         g_dmoe.cross(i)
     g_dmoe.finish()
     g_comb.finish()
     for i in range(3):
         g_hn.cross(i)
+    local[4].wait()
+    own_columns = []
+    for i in range(3):
+        where = rows(2 * me.arrival(i) + c)
+        copy = pltpu.make_async_copy(
+            w_column.at[where, :], r.w_out.at[where, cols(t)], loc.at[i]
+        )
+        copy.start()
+        own_columns.append(copy)
+    g_wout.share_own()
+    for i in range(3):
+        own_columns[i].wait()
+        g_wout.spread(i)
     g_hn.finish()
     for copy in own_moe:
         copy.wait()
-    for k in range(1, NBLK):
-        weights_from(0, k).wait_recv()
+    seven_blocks(r.aa.wm[0]).wait_recv()
 
     expert = lax.broadcasted_iota(jnp.int32, (16, 128), 0)
     first_row = (lax.broadcasted_iota(jnp.int32, (8, 128), 0) == 0).astype(F32)
 
     def core_copy(own, i):
         part = own.part.at[rows(2 * i + (1 - c)), :]
-        return remote(part, own.core.at[i], own.sems[0].at[i], own.sems[1].at[i], me.partner())
+        return remote(part, own.core.at[i], own.sems[0].at[0], own.sems[1].at[i], me.partner())
 
     def plane_copy(own, i, k):
-        piece = own.part.at[rows(2 * i + c), cols(me.peer_t(k))]
         return remote(
-            piece,
+            own.part.at[rows(2 * i + c), cols(me.peer_t(k))],
             own.plane.at[i, k - 1],
-            own.sems[2].at[i, k - 1],
-            own.sems[3].at[i, k - 1],
+            own.sems[2].at[0],
+            own.sems[3].at[i, 0],
             me.plane(k),
         )
 
-    def line_copy(own, i):
+    def half_rows(i, k):
+        return pl.ds(pl.multiple_of((2 * i + c) * TB + HALF * (k - 1), HALF), HALF)
+
+    def diagonal_copy(own, i, k):
         return remote(
-            own.part.at[rows(2 * i + c), cols(t)],
-            own.line.at[z],
-            own.sems[4].at[i],
-            own.sems[5].at[z],
-            me.at_z(i),
-        )
+            own.part.at[half_rows(i, k), cols(me.peer_t(3))],
+            own.diagonal.at[i, k - 1],
+            own.sems[2].at[0],
+            own.sems[3].at[i, 1],
+            me.plane(k),
+        )
+
+    def plane_relay(own, i):
+        both = own.diagonal.at[i]
+        remote(both, both, own.sems[2].at[0], own.sems[3].at[i, 1], me.plane(1)).wait_recv()
+        for k in (1, 2):
+            where, lanes = half_rows(i, k), cols(me.peer_t(3 - k))
+            own.part[where, lanes] = (
+                own.part[where, lanes].astype(F32) + own.diagonal[i, k - 1].astype(F32)
+            ).astype(BF16)
+        for k in (1, 2):
+            plane_copy(own, i, k).start()
 
     def core_sum(own, i):
         core_copy(own, i).wait_recv()
@@ -1079,8 +1186,8 @@
             ).astype(BF16)
 
         row_chunks(add)
-        for k in (3, 1, 2):
-            plane_copy(own, i, k).start()
+        for k in (1, 2):
+            diagonal_copy(own, i, k).start()
 
     def expert_block(e, where, block):
         base = 384 * e
@@ -1135,59 +1242,29 @@
                 remote(
                     r.g_moe.at[rows(peer), lanes],
                     target.at[2 * b + e],
-                    send.at[k],
-                    recv.at[b],
+                    send.at[0],
+                    recv.at[0],
                     me.at_block(peer),
                 ).start()
 
-    def grads_copy(e, k):
-        send, recv = r.aa.gm[e]
-        peer = me.other(k)
-        whole = r.g_moe.at[rows(peer), pl.ds(384 * e, 384)]
-        return remote(whole, whole, send.at[k], recv.at[peer], me.partner())
-
     weight_grads(0)
-    send_grads(0, (1, 7, 2, 6, 3))
-    for k in range(1, NBLK):
-        weights_from(1, k).wait_recv()
-
-    def expert_two(step, carry):
-        i = me.dest(step % 4)
-        late = step // 4
-        block = 2 * i + (1 - c) + late * (2 * c - 1)
+    send_grads(0, (4, 3, 5, 2, 6, 1, 7))
+
+    def hidden_one(block, carry):
         where = rows(block)
-        expert_block(1, where, block)
         for n in range(3):
             lanes = slice(512 * n, 512 * (n + 1))
-            r.h.part[where, lanes] = (
-                contract(r.dgu[where, 0:256], r.w_moe[lanes, 0:256], 1, 1)
-                + contract(r.dgu[where, 256:512], r.w_moe[lanes, 384:640], 1, 1)
+            r.h.part[where, lanes] = contract(
+                r.dgu[where, 0:256], r.w_moe[lanes, 0:256], 1, 1
             ).astype(BF16)
-
-        @pl.when(late == 0)
-        def _():
-            core_copy(r.h, i).start()
-
-        @pl.when(late == 1)
-        def _():
-            core_sum(r.h, i)
-
         return carry
 
-    lax.fori_loop(0, NBLK, expert_two, 0)
-
-    dc_send, dc_recv = r.aa.dc
-    for k in range(1, NBLK):
-        peer = me.other(k)
-        pend.start(
-            remote(
-                r.dc_own.at[peer], r.dc_in.at[b], dc_send.at[k], dc_recv.at[b],
-                me.at_block(peer),
-            )
-        )
-    r.dc_in[b] = r.dc_own[b]
-
-    weight_grads(1)
+    lax.fori_loop(0, NBLK, hidden_one, 0)
+    for i in range(3):
+        g_wout.relay(i)
+    seven_blocks(r.aa.wm[1]).wait_recv()
+    early.drain()
+
     class Chain:
         def __init__(self, piece, line, send, recv, arrived):
             self.piece, self.line, self.send, self.recv = piece, line, send, recv
@@ -1204,7 +1281,7 @@
             else:
                 to, slot = i, 4 + z % 2
             return remote(
-                self.piece(i), self.line.at[slot], self.send.at[j], self.recv.at[slot], me.at_z(to)
+                self.piece(i), self.line.at[slot], self.send.at[0], self.recv.at[slot], me.at_z(to)
             )
 
         def wait_slot(self, slot):
@@ -1225,6 +1302,13 @@
 
             self.copy(j).start()
 
+        def steps(self, when=None):
+            if when is None:
+                for j in range(3):
+                    self.step(j)
+            else:
+                pl.when(when)(self.steps)
+
         def total(self, acc):
             self.arrived(z)
             acc[...] = self.piece(z)[...].astype(F32)
@@ -1236,15 +1320,15 @@
                     acc[...] += self.line[slot].astype(F32)
 
         def drain(self):
-            for j in range(3):
-                self.copy(j).wait_send()
+            three = self.line.at[0:3]
+            remote(three, three, self.send.at[0], self.recv.at[0], me.partner()).wait_send()
 
     def plane_add(own, i):
-        for k in (1, 2, 3):
-            plane_copy(own, i, k).wait_recv()
+        both = own.plane.at[i]
+        remote(both, both, own.sems[2].at[0], own.sems[3].at[i, 0], me.plane(1)).wait_recv()
         where = rows(2 * i + c)
         total = own.part[where, cols(t)].astype(F32)
-        for k in range(3):
+        for k in range(2):
             total = total + own.plane[i, k].astype(F32)
         own.part[where, cols(t)] = total.astype(BF16)
 
@@ -1258,16 +1342,81 @@
         )
 
     def scatter_drain(own):
-        def step(i, carry):
-            core_copy(own, i).wait_send()
-            for k in (1, 2, 3):
-                plane_copy(own, i, k).wait_send()
-            return carry
-
-        lax.fori_loop(0, 4, step, 0)
+        remote(own.core, own.core, own.sems[0].at[0], own.sems[1].at[0], me.partner()).wait_send()
+        twelve = own.part.at[0:576, :]
+        remote(twelve, twelve, own.sems[2].at[0], own.sems[3].at[0, 0], me.plane(1)).wait_send()
 
     chain_h, chain_y = scatter_chain(r.h), scatter_chain(r.y)
 
+    def expert_two(step, carry):
+        i = me.dest(step // 2)
+        late = step % 2
+        block = 2 * i + (1 - c) + late * (2 * c - 1)
+        where = rows(block)
+        expert_block(1, where, block)
+        for n in range(3):
+            lanes = slice(512 * n, 512 * (n + 1))
+            r.h.part[where, lanes] = (
+                r.h.part[where, lanes].astype(F32)
+                + contract(r.dgu[where, 256:512], r.w_moe[lanes, 384:640], 1, 1)
+            ).astype(BF16)
+
+        @pl.when(late == 0)
+        def _():
+            core_copy(r.h, i).start()
+
+        for n in range(3):
+            lanes = slice(512 * n, 512 * (n + 1))
+            r.y.part[where, lanes] = (
+                contract(r.cz[where, 0:128], r.w_moe[lanes, 256:384], 1, 1)
+                + contract(r.cz[where, 128:256], r.w_moe[lanes, 640:768], 1, 1)
+            ).astype(BF16)
+
+        @pl.when(late == 0)
+        def _():
+            core_copy(r.y, i).start()
+
+        @pl.when(late == 1)
+        def _():
+            core_sum(r.h, i)
+
+        @pl.when((late == 1) & (step > 1))
+        def _():
+            plane_relay(r.h, me.dest(step // 2 - 1))
+
+        for j in range(2):
+
+            @pl.when(end_chip & (step == 2 * j + 5))
+            def _(j=j):
+                chain_h.step(j)
+
+        return carry
+
+    lax.fori_loop(0, NBLK, expert_two, 0)
+
+    plane_relay(r.h, z)
+    dc_send, dc_recv = r.aa.dc
+    for k in range(1, NBLK):
+        peer = me.other(k)
+        pend.begin(
+            remote(
+                r.dc_own.at[peer], r.dc_in.at[b], dc_send.at[0], dc_recv.at[0],
+                me.at_block(peer),
+            )
+        )
+    dc_seven = r.dc_own.at[0:7]
+    dc_all = remote(dc_seven, dc_seven, dc_send.at[0], dc_recv.at[0], me.partner())
+    pend.later(dc_all)
+    r.dc_in[b] = r.dc_own[b]
+
+
+    @pl.when(me.middle())
+    def _():
+        chain_h.step(0)
+        chain_h.step(1)
+
+    chain_h.step(2)
+    weight_grads(1)
     own_grads = [
         pltpu.make_async_copy(
             r.g_moe.at[rows(b), lanes], target.at[2 * b + e], loc.at[4 + 3 * e + i]
@@ -1278,52 +1427,16 @@
     for copy in own_grads:
         copy.start()
 
-    for k in range(1, NBLK):
-        peer = me.other(k)
-        there = r.dc_in.at[peer]
-        remote(there, there, dc_send.at[k], dc_recv.at[peer], me.partner()).wait_recv()
-    dcp_send, dcp_recv = r.pl.dc
-    dc_copies = [
-        remote(
-            r.dc_in, r.dc_plane.at[k - 1], dcp_send.at[k - 1], dcp_recv.at[k - 1], me.plane(k)
-        )
-        for k in (1, 2, 3)
-    ]
-    for copy in dc_copies:
-        pend.start(copy)
-    def output_block(step, carry):
-        i = me.dest(step % 4)
-        late = step // 4
-        where = rows(2 * i + (1 - c) + late * (2 * c - 1))
-        cz = r.cz[where, :]
-        for n in range(3):
-            lanes = slice(512 * n, 512 * (n + 1))
-            r.y.part[where, lanes] = (
-                contract(cz[:, 0:128], r.w_moe[lanes, 256:384], 1, 1)
-                + contract(cz[:, 128:256], r.w_moe[lanes, 640:768], 1, 1)
-            ).astype(BF16)
-
-        @pl.when(late == 0)
-        def _():
-            core_copy(r.y, i).start()
-
-        return carry
-
-    lax.fori_loop(0, NBLK, output_block, 0)
-
-    for j in range(3):
-        chain_h.step(j)
-        send_grads(0, ((5,), (4,), ())[j])
+    dc_all.wait_recv()
+    wait_dc = to_plane(r.pl.dc, lambda k: (r.dc_in, r.dc_plane.at[k - 1]), r.dc_plane)
+    send_grads(1, (1, 7, 2))
     chain_h.total(r.acc.at[:, 0:TC])
     r.dhn[:, cols(t)] = r.acc[:, 0:TC].astype(BF16)
-    send_grads(1, (1, 7, 2))
-    wait_dh = plane_gather(
-        r.pl.dh, r.dhn.at[:, cols(t)], lambda k: r.dhn.at[:, cols(me.peer_t(k))]
-    )
+    send_grads(1, (6, 3, 5))
+    wait_dh = plane_gather(r.pl.dh, r.dhn)
     for j in range(4):
         core_sum(r.y, me.dest(j))
-    for copy in dc_copies:
-        copy.wait_recv()
+    wait_dc()
     for k in range(NBLK):
         total = r.dc_in[k] + r.dc_plane[0, k] + r.dc_plane[1, k] + r.dc_plane[2, k]
         r.dc_t[2 * k : 2 * k + 2, :] = total[0:2, :]
@@ -1357,18 +1470,18 @@
         store.inn[b] = store.own[b]
         for k in range(1, NBLK):
             peer = me.other(k)
-            pend.start(
+            pend.begin(
                 remote(
-                    store.own.at[peer], store.inn.at[b], send.at[k], recv.at[b],
+                    store.own.at[peer], store.inn.at[b], send.at[0], recv.at[0],
                     me.at_block(peer),
                 )
             )
+        seven = store.own.at[0:7]
+        all_seven = remote(seven, seven, send.at[0], recv.at[0], me.partner())
+        pend.later(all_seven)
 
         def wait():
-            for k in range(1, NBLK):
-                peer = me.other(k)
-                there = store.inn.at[peer]
-                remote(there, there, send.at[k], recv.at[peer], me.partner()).wait_recv()
+            all_seven.wait_recv()
             total = store.inn[0]
             for k in range(1, NBLK):
                 total = total + store.inn[k]
@@ -1378,16 +1491,19 @@
 
     wait_sm = to_owners(r.sm, r.aa.sm, 24)
 
+    for i in range(3):
+        g_wout.cross(i)
+    g_wout.finish()
     d_o = contract(r.dproj[...], r.w_out[cols(t), :], 1, 1).astype(BF16).astype(F32)
     for h in range(NQ):
         pair = h // 2
         dh_z = head_from_chunk(d_o[:, 128 * pair : 128 * (pair + 1)], h)
         den = r.den[h]
         r.dnz[h] = (dh_z / den).astype(BF16)
-        r.shift[h] = (
+        r.den[h] = (
             jnp.broadcast_to(jnp.sum(dh_z * r.oz[h], axis=1, keepdims=True), (TB, 128)) / den
         )
-        r.dq[h] = jnp.zeros((TB, 128), F32)
+        r.oz[h] = jnp.zeros((TB, 128), F32)
 
     def out_grads(n, carry):
         lanes = pl.ds(pl.multiple_of(n * 256, 256), 256)
@@ -1409,7 +1525,7 @@
             return remote(
                 self.part.at[rows(2 * i + (1 - c)), :],
                 self.core.at[i],
-                self.sems[0].at[i],
+                self.sems[0].at[0],
                 self.sems[1].at[i],
                 me.partner(),
             )
@@ -1428,8 +1544,9 @@
             self.drain_core()
 
         def drain_core(self):
-            for i in range(4):
-                self.core_copy(i).wait_send()
+            remote(
+                self.core, self.core, self.sems[0].at[0], self.sems[1].at[0], me.partner()
+            ).wait_send()
 
         def down(self):
             for i in range(4):
@@ -1466,10 +1583,12 @@
                 self.wait_slot(5)
                 acc[...] += self.line[5].astype(F32)
 
-    send_grads(1, (6, 3))
     red_out = Reduce(g_out_part, r.rd.go)
     red_out.start()
-
+    red_out.steps(z * (3 - z) == 0)
+
+    for j in range(4):
+        plane_relay(r.y, me.dest(j))
     def clear(i, carry):
         r.dkv[rows(i), :] = jnp.zeros((TB, 256), BF16)
         return carry
@@ -1482,16 +1601,18 @@
         mask = allowed(kb)
         dk = jnp.zeros((TB, 128), F32)
         dv = jnp.zeros((TB, 128), F32)
-        for h in range(NQ):
-            q = r.qz[h]
-            dn = r.dnz[h]
-            scores = contract(q, keys, 1, 1) * score_scale
-            e = jnp.where(mask, jnp.exp(scores), 0.0)
-            dp = contract(dn, values, 1, 1)
-            ds = (e * (dp - r.shift[h][:, 0:1])).astype(BF16)
-            r.dq[h] += jnp.dot(ds, keys, preferred_element_type=F32)
+        for g in range(2):
+            heads = pl.ds(3 * g, 3)
+            q = r.qz[heads].reshape(3 * TB, 128)
+            dn = r.dnz[heads].reshape(3 * TB, 128)
+            e = jnp.exp(contract(q, keys, 1, 1) * score_scale).reshape(3, TB, TB)
+            e = jnp.where(mask[None], e, 0.0)
+            dp = contract(dn, values, 1, 1).reshape(3, TB, TB)
+            ds = (e * (dp - r.den[heads][:, :, 0:1])).reshape(3 * TB, TB).astype(BF16)
+            e = e.reshape(3 * TB, TB).astype(BF16)
+            r.oz[heads] += jnp.dot(ds, keys, preferred_element_type=F32).reshape(3, TB, 128)
             dk = dk + contract(ds, q, 0, 0)
-            dv = dv + contract(e.astype(BF16), dn, 0, 0)
+            dv = dv + contract(e, dn, 0, 0)
         r.dkv[rows(kb), 0:128] = (dk * score_scale).astype(BF16)
         r.dkv[rows(kb), 128:256] = dv.astype(BF16)
         return carry
@@ -1501,7 +1622,7 @@
     red_kv.start()
     for pair in range(3):
         heads = [
-            jnp.where(half_mask(h // 3), r.dq[h] * score_scale, 0.0)
+            jnp.where(half_mask(h // 3), r.oz[h] * score_scale, 0.0)
             for h in (2 * pair, 2 * pair + 1)
         ]
         u = chunk_from_heads(heads[0], heads[1], pair).astype(BF16).astype(F32)
@@ -1509,10 +1630,17 @@
             u * cosine - swap_halves(u) * sine
         ).astype(BF16)
     red_kv.down()
-    send_grads(1, (5,))
-    for j in range(3):
-        red_out.step(j)
-    d_kv_acc = r.acc.at[:, 384:640]
+
+    def q_grads(n, carry):
+        lanes = pl.ds(pl.multiple_of(n * 256, 256), 256)
+        g_q_part[lanes, :] = contract(r.xn[:, lanes], r.dqkv[:, 0:TC], 0, 0).astype(BF16)
+        return carry
+
+    lax.fori_loop(0, DM // 256, q_grads, 0)
+    red_gq = Reduce(g_q_part, r.rd.gq)
+    red_gq.start()
+    red_gq.steps()
+    d_kv_acc = r.acc.at[:, 0:256]
     red_kv.down_total(d_kv_acc)
     d_kv = d_kv_acc[...].astype(BF16)
     u = d_kv[:, 0:128].astype(F32)
@@ -1522,51 +1650,30 @@
     for n in range(3):
         lanes = slice(512 * n, 512 * (n + 1))
         r.dx[:, lanes] = contract(r.dqkv[...], r.w_qkv[lanes, :], 1, 1).astype(BF16)
-    xs_send, xs_recv = r.pl.xs
-    dx_copies = [
-        remote(
-            r.dx.at[:, cols(me.peer_t(k))], r.dx_in.at[k - 1], xs_send.at[k - 1],
-            xs_recv.at[k - 1], me.plane(k),
-        )
-        for k in (3, 1, 2)
-    ]
-    for copy in dx_copies:
-        pend.start(copy)
-
-    def qkv_grads(n, carry):
+    wait_xs = to_plane(
+        r.pl.xs, lambda k: (r.dx.at[:, cols(me.peer_t(k))], r.dx_in.at[k - 1]), r.dx_in
+    )
+
+    def kv_grads(n, carry):
         lanes = pl.ds(pl.multiple_of(n * 256, 256), 256)
-        g_qkv_part[lanes, :] = contract(r.xn[:, lanes], r.dqkv[...], 0, 0).astype(BF16)
+        g_kv_part[lanes, :] = contract(r.xn[:, lanes], r.dqkv[:, TC:640], 0, 0).astype(BF16)
         return carry
 
-    lax.fori_loop(0, DM // 256, qkv_grads, 0)
-    red_qkv = Reduce(g_qkv_part, r.rd.gq)
-    red_qkv.start()
+    lax.fori_loop(0, DM // 256, kv_grads, 0)
+    red_gkv = Reduce(g_kv_part, r.rd.gkv)
+    red_gkv.start()
+    red_gq.total(r.acc.at[:, 0:TC])
+    r.g_qkv_sum[:, 0:TC] = r.acc[:, 0:TC].astype(BF16)
     for j in range(3):
-        red_qkv.step(j)
+        red_gkv.step(j)
+    red_out.steps(me.middle())
     send_grads(1, (4,))
-    for copy in dx_copies:
-        copy.wait_recv()
+    wait_xs()
     total = r.dx[:, cols(t)].astype(F32)
     for k in range(3):
         total = total + r.dx_in[k].astype(F32)
     r.dxn[:, cols(t)] = total.astype(BF16)
-    wait_dx = plane_gather(
-        r.pl.xg, r.dxn.at[:, cols(t)], lambda k: r.dxn.at[:, cols(me.peer_t(k))]
-    )
-    red_out.total(r.acc.at[:, 0:TC])
-    r.g_out_sum[...] = r.acc[:, 0:TC].astype(BF16)
-    go_send, go_recv = r.pl.go
-    own_go = pltpu.make_async_copy(r.g_out_sum, r.g_out_out.at[:, cols(t)], loc.at[0])
-    own_go.start()
-    for k in (3, 1, 2):
-        pend.start(
-            remote(
-                r.g_out_sum, r.g_out_out.at[:, cols(t)], go_send.at[k - 1], go_recv.at[k - 1],
-                me.plane(k),
-            )
-        )
-    for j in range(3):
-        chain_y.step(j)
+    wait_dx = plane_gather(r.pl.xg, r.dxn)
     wait_dx()
     r.flat[0:8, :] = jnp.zeros((8, DM), F32)
 
@@ -1581,43 +1688,55 @@
 
     row_chunks(norm_one_back)
     wait_sn = to_owners(r.sn, r.aa.sn, 8)
-    red_qkv.total(r.acc)
-    r.g_qkv_sum[...] = r.acc[...].astype(BF16)
-    gq_send, gq_recv = r.pl.gq
-    own_gq = pltpu.make_async_copy(r.g_qkv_sum, r.g_qkv_out.at[t], loc.at[1])
-    own_gq.start()
-    for k in (3, 1, 2):
-        pend.start(
-            remote(
-                r.g_qkv_sum, r.g_qkv_out.at[t], gq_send.at[k - 1], gq_recv.at[k - 1],
-                me.plane(k),
-            )
-        )
+    own_qkv, from_qkv = [], []
+
+    def give(n, start, width, target, sems, three):
+        def lanes(index):
+            return pl.ds(pl.multiple_of(width * index, 128), width)
+
+        piece = r.g_qkv_sum.at[:, start : start + width]
+        there = target.at[:, lanes(t)]
+        own = pltpu.make_async_copy(piece, there, loc.at[1 + n])
+        own.start()
+        own_qkv.append(own)
+        from_qkv.append(to_plane(sems, lambda k: (piece, there), three))
+
+    give(0, 0, TC, r.gq_out, r.pl.gq, r.dx_in)
+    red_gkv.total(r.acc.at[:, 0:256])
+    r.g_qkv_sum[:, TC:640] = r.acc[:, 0:256].astype(BF16)
+    give(1, 384, 128, r.gk_out, r.pl.gk, r.g_qkv_sum.at[:, 0:TC])
+    give(2, 512, 128, r.gv_out, r.pl.gv, r.g_qkv_sum.at[:, 0:TC])
+    red_out.total(r.acc.at[:, 0:TC])
+    r.g_out_sum[...] = r.acc[:, 0:TC].astype(BF16)
+    own_go = pltpu.make_async_copy(r.g_out_sum, r.g_out_out.at[:, cols(t)], loc.at[0])
+    own_go.start()
+    go_there = r.g_out_out.at[:, cols(t)]
+    wait_go = to_plane(r.pl.go, lambda k: (r.g_out_sum, go_there), r.dx_in)
+    chain_y.steps()
     chain_y.total(r.acc.at[:, 0:TC])
     r.block_out[...] = r.hidden[:, cols(t)] + residual_scale * r.acc[:, 0:TC]
     r.sm_out[...] = wait_sm()
     r.sn_out[...] = wait_sn()
 
-    for k in (1, 2, 3):
-        there = r.g_out_out.at[:, cols(me.peer_t(k))]
-        remote(there, there, go_send.at[k - 1], go_recv.at[k - 1], me.plane(k)).wait_recv()
-        there = r.g_qkv_out.at[me.peer_t(k)]
-        remote(there, there, gq_send.at[k - 1], gq_recv.at[k - 1], me.plane(k)).wait_recv()
+    wait_go()
+    for wait in from_qkv:
+        wait()
     own_go.wait()
-    own_gq.wait()
+    for copy in own_qkv:
+        copy.wait()
     for copy in own_grads:
         copy.wait()
-    for k in range(1, NBLK):
-        for e in range(2):
-            grads_copy(e, k).wait()
-            weights_from(e, k).wait_send()
+    for e in range(2):
+        seven_blocks(r.aa.gm[e]).wait()
+        seven_blocks(r.aa.wm[e]).wait_send()
     scatter_drain(r.h)
     scatter_drain(r.y)
     chain_h.drain()
     chain_y.drain()
     red_out.drain()
     red_kv.drain_core()
-    red_qkv.drain()
+    red_gq.drain()
+    red_gkv.drain()
     pend.drain()
 
 
@@ -1637,41 +1756,44 @@
     down_weight,
     grad_output,
 ):
-    block = 2 * lax.axis_index("fsdp") + lax.axis_index("heads")
-    start = block * TB
-    positions = start + jnp.arange(TB, dtype=jnp.int32)
     half = HEAD_DIM // 2
-    inverse = rope_base ** (-(jnp.arange(half, dtype=F32) * 2.0 / HEAD_DIM))
-    angles = positions[:, None].astype(F32) * inverse[None, :]
-    cosine, sine = jnp.cos(angles), jnp.sin(angles)
-    rope_c = jnp.concatenate([cosine] * 4, axis=1)
-    rope_s = jnp.concatenate([-sine, sine, -sine, sine], axis=1)
-    seg_rows = segments.reshape(NBLK, TB)
-    seg_k = jnp.pad(seg_rows, ((0, 0), (0, 256 - TB)))
-    seg_q = lax.dynamic_slice_in_dim(segments, start, TB, 0)[:, None]
-    mask_t = jnp.sum(
-        (routes.T[:, None, :] == jnp.arange(E, dtype=jnp.int32)[None, :, None]).astype(F32), axis=0
-    )
-    small = jnp.concatenate(
-        [router_weight.T, attn_gain[None], ffn_gain[None], jnp.zeros((14, TB), BF16)], axis=0
-    )
-    small = jnp.pad(small, ((0, 0), (0, 256 - TB)))
-    down_t = down_weight.transpose(0, 2, 1)
-
+    inverse = rope_base ** (-(np.arange(half, dtype=np.float64) * 2.0 / HEAD_DIM))
+    inverse = np.tile(inverse.astype(np.float32).astype(np.float64), 4)
+
+    def table(positions):
+        angles = positions[:, None] * inverse[None, :]
+        return np.stack([np.cos(angles), np.sin(angles)]).astype(np.float32)
+
+    vectors = (
+        jnp.pad(segments, (0, 512)).astype(F32)
+        + jnp.pad(attn_gain.astype(F32), (DM, 320))
+        + jnp.pad(ffn_gain.astype(F32), (DM + 256, 64))
+    ).reshape(16, 128)
     vmem, hbm = pl.BlockSpec(memory_space=pltpu.VMEM), pl.BlockSpec(memory_space=pl.ANY)
     ins = dict(
-        x=(block_input, vmem), gout=(grad_output, vmem), rope_c=(rope_c, vmem),
-        rope_s=(rope_s, vmem), seg_q=(seg_q, vmem), seg_k=(seg_k, vmem), mask_t=(mask_t, vmem),
-        small_own=(small, vmem), wq=(query_weight, hbm), wk=(key_matrix, hbm),
-        wv=(value_matrix, hbm), wo=(out_weight, hbm), gate=(gate_weight, hbm),
-        up=(up_weight, hbm), down_t=(down_t, hbm),
+        x=(block_input, vmem),
+        gout=(grad_output, vmem),
+        rope_block=(jnp.asarray(table(np.arange(NBLK) * TB)), vmem),
+        rope_row=(jnp.asarray(table(np.arange(TB))), vmem),
+        vectors=(vectors, vmem),
+        routes_t=(routes.T, vmem),
+        router_own=(router_weight.T, vmem),
+        wq=(query_weight, hbm),
+        wk=(key_matrix, hbm),
+        wv=(value_matrix, hbm),
+        wo=(out_weight, hbm),
+        gate=(gate_weight, hbm),
+        up=(up_weight, hbm),
+        down_t=(down_weight.transpose(0, 2, 1), hbm),
     )
     outs = dict(
         block_out=((TB, TC), F32, vmem),
         grad_in=((TB, DM), F32, vmem),
         sm_out=((24, 256), F32, vmem),
         sn_out=((8, 256), F32, vmem),
-        g_qkv_out=((4, TB, 640), BF16, hbm),
+        gq_out=((TB, DM), BF16, hbm),
+        gk_out=((TB, 512), BF16, hbm),
+        gv_out=((TB, 512), BF16, hbm),
         g_out_out=((TB, DM), BF16, hbm),
         gate_out=((E, TB, 128), BF16, hbm),
         up_out=((E, TB, 128), BF16, hbm),
@@ -1696,21 +1818,63 @@
         ),
     )(*[value for value, _ in ins.values()])
     res = Bag(zip(outs, results))
-    g_qkv = res.g_qkv_out.astype(F32).transpose(1, 0, 2)
+    wide = widen(
+        res.block_out, res.grad_in, res.gq_out, res.gk_out, res.gv_out, res.g_out_out,
+        res.gate_out, res.up_out, res.down_out, res.sm_out, res.sn_out,
+    )
+    block_output, grad_input, g_query, g_key, g_value, g_out, gate, up, down = wide[:9]
+    router, gain_two, gain_one = wide[9:]
     return (
-        res.block_out,
-        res.grad_in,
-        res.sn_out[0, :TB],
-        res.sm_out[16, :TB],
-        g_qkv[:, :, 0:384].reshape(TB, DM),
-        g_qkv[:, :, 384:512].reshape(TB, 512),
-        g_qkv[:, :, 512:640].reshape(TB, 512),
-        res.g_out_out.astype(F32),
-        res.sm_out[0:16, :TB].T,
-        res.gate_out.astype(F32),
-        res.up_out.astype(F32),
-        res.down_out.astype(F32).transpose(0, 2, 1),
-    )
+        block_output,
+        grad_input,
+        gain_one.reshape(TB),
+        gain_two.reshape(TB),
+        g_query,
+        g_key,
+        g_value,
+        g_out,
+        router.T,
+        gate,
+        up,
+        down.transpose(0, 2, 1),
+    )
+
+
+def widen(*arrays):
+    steps = 4
+
+    def spec(shape):
+        rest = (0,) * (len(shape) - 1)
+        return pl.BlockSpec((shape[0] // steps, *shape[1:]), lambda i: (i, *rest))
+
+    def entry(*refs):
+        count = len(arrays)
+        for source, target in zip(refs[: count - 2], refs[count:]):
+            target[...] = source[...].astype(F32)
+        sm, sn = refs[count - 2 : count]
+        router, gain_two, gain_one = refs[-3:]
+        router[...] = sm[0:16, 0:TB]
+        gain_two[...] = sm[16:17, 0:TB]
+        gain_one[...] = sn[0:1, 0:TB]
+
+    def whole(*shape):
+        return pl.BlockSpec(shape, lambda i: (0, 0))
+
+    specs = [spec(a.shape) for a in arrays[:-2]]
+    return pl.pallas_call(
+        entry,
+        name="widen",
+        grid=(steps,),
+        in_specs=[*specs, whole(24, 256), whole(8, 256)],
+        out_specs=[*specs, whole(16, TB), whole(1, TB), whole(1, TB)],
+        out_shape=[
+            *(jax.ShapeDtypeStruct(a.shape, F32) for a in arrays[:-2]),
+            jax.ShapeDtypeStruct((16, TB), F32),
+            jax.ShapeDtypeStruct((1, TB), F32),
+            jax.ShapeDtypeStruct((1, TB), F32),
+        ],
+        cost_estimate=pl.CostEstimate(flops=4_000_000, bytes_accessed=16_000_000, transcendentals=0),
+    )(*arrays)
 
 
 VMEM_BYTES = 67043328

time: 272 us -> 242 us (0.89)
  local copies, waits for them, and re-layouts: 12.7 us -> 0 us
  other arithmetic: 9.79 us -> 1.32 us
  Pallas kernels: 247 us -> 240 us
    pallas_call x1, Pallas kernels: 247 us -> 233 us  [fast_body(): pl.pallas_call(entry, name='layer', out_shape=[jax.ShapeDtypeStruct(shape...]
    pallas_call x0 -> x1, Pallas kernels: none -> 6.52 us  [widen(): pl.pallas_call(entry, name='widen', grid=(steps,), in_specs=[*specs, whol...]
    convert_element_type x4 -> x0, other arithmetic: 3.74 us -> none  [the longest x1 1.3 us: fast_body(): res.gate_out.astype(F32)]
    reshape x4 -> x0, local copies, waits for them, and re-layouts: 3.51 us -> none  [the longest x1 1.16 us: fast_body(): g_qkv[:, :, 0:384].reshape(TB, DM)]
where the time goes in v4:
time: 242 us
  Pallas kernels  240 us (99%)
    pallas_call x1, Pallas kernels, fast_body(): pl.pallas_call(entry, name='layer', out_shape=[jax.ShapeDtypeStruct(shape...  233 us
    pallas_call x1, Pallas kernels, widen(): pl.pallas_call(entry, name='widen', grid=(steps,), in_specs=[*specs, whol...  6.52 us

profile of v4, /device:TPU:16, one launch (start us, length us, event | category | flops | bytes accessed | tf_op | source)
XLA Modules:
  0.0 242.1 jit_solution(16176942282138745951)
XLA Ops:
  0.6 1.3 add_bitcast_fusion.refs_4_
  2.0 233.4 %layer.1 = (f32[192,384]{1,0:T(8,128)}, f32[192,1536]{1,0:T(8,128)}, f32[24,256]{1,0:T(8,128)}, f32[8,256]{1,0:T(8,128)}, bf16[192,1536]{1,0:T(8,128)(2,1)}, /*i...) custom-call(bf16[192,1536]{1,0:T(8,128)(2,1)} %refs_0_.1, ...), custom_call_target="tpu_custom_call" | custom-call | tf_op jit(solution)/shard_map/layer/pallas_call | solution.py:1809
  235.4 6.5 %widen.1 = (f32[192,384]{1,0:T(8,128)}, f32[192,1536]{1,0:T(8,128)}, f32[192,1536]{1,0:T(8,128)}, f32[192,512]{1,0:T(8,128)}, f32[192,512]{1,0:T(8,128)}, /*inde...) custom-call(f32[192,384]{1,0:T(8,128)} %get-tuple-element.35.refs_0_, ...), custom_call_target="tpu_custom_call" | custom-call | flops 4000000 | bytes 16000000 | tf_op jit(solution)/shard_map/widen/pallas_call | solution.py:1864

commit v5 on v4

--- a/solution.py
+++ b/solution.py
@@ -548,19 +548,30 @@
         return remote(ref, ref, send_sem.at[0], recv_sem.at[0], self.me.partner())
 
     def start(self):
+        self.send_own()
+        self.register()
+
+    def register(self):
+        me = self.me
+        for count, when in ((5, me.middle()), (1, me.z * (3 - me.z) == 0)):
+            self.pend.later(self.bytes_of(self.several_line(count), self.send, self.recv), when)
+        self.register_shares()
+
+    def send_own(self):
         me = self.me
         own = self.line_view(me.b)
         for dz, when in ((1, me.z < 3), (-1, me.z > 0)):
             self.pend.begin(
                 remote(own, own, self.send.at[0], self.recv.at[me.z], me.at_z(me.z + dz)), when
             )
-        for count, when in ((5, me.middle()), (1, me.z * (3 - me.z) == 0)):
-            self.pend.later(self.bytes_of(self.several_line(count), self.send, self.recv), when)
-        self.share_own()
+        self.share_block(me.b)
+
+    def register_shares(self):
+        self.pend.later(self.bytes_of(self.several(4), self.psend, self.precv))
 
     def share_own(self):
         self.share_block(self.me.b)
-        self.pend.later(self.bytes_of(self.several(4), self.psend, self.precv))
+        self.register_shares()
 
     def share_block(self, block):
         whole = self.view(block)
@@ -688,12 +699,15 @@
             self.me.plane(k),
         )
 
-    def spread(self, i):
+    def spread(self, i, last=True):
         for k in (1, 2):
             self.pend.begin(self.copy(self.piece(i, 0), i, 0, k))
-        if i == 2:
-            nine = self.buffer.at[0:864, 0:768]
-            self.pend.later(self.copy(nine, i, 0, 1))
+        if i == 2 and last:
+            self.register_spread()
+
+    def register_spread(self):
+        nine = self.buffer.at[0:864, 0:768]
+        self.pend.later(self.copy(nine, 2, 0, 1))
 
     def relay(self, i):
         self.copy(self.buffer.at[0 : 2 * TB, 0:TC], i, 0, 1).wait_recv()
@@ -893,13 +907,13 @@
         return LineGather(me, pend, view, view, several, several, sems)
 
     g_small = line(lambda k: r.small.at[k], lambda n: r.small.at[0:n], r.lg.s)
-    def half(h):
-        return lambda k: r.w_qkv.at[pl.ds(pl.multiple_of(TB * k + 96 * h, 96), 96), :]
-
-    g_qkv = [
-        line(half(h), lambda n: r.w_qkv.at[0 : 96 * n, :], sems)
-        for h, sems in enumerate((r.lg.w, r.lg.v))
-    ]
+    def columns(lanes, sems):
+        return line(
+            lambda k: r.w_qkv.at[rows(k), lanes], lambda n: r.w_qkv.at[0 : TB * n, lanes], sems
+        )
+
+    g_keys = columns(slice(TC, 640), r.lg.w)
+    g_query = columns(slice(0, TC), r.lg.v)
     g_kv = UpGather(me, pend, lambda k: r.kv.at[rows(k), :], r.lg.kv)
     g_comb = line(lambda k: r.comb.at[k], lambda n: r.comb.at[0:n], r.lg.c)
     early = Pending()
@@ -923,36 +937,32 @@
 
     end_chip = z * (3 - z) == 0
 
-    def send_weights_end(e, ks):
-        @pl.when(end_chip)
-        def _():
-            for k in ks:
-                send_weights_to(e, me.other(k))
-
-    def send_weights_inner(e, ks):
+    def send_weights(e, ks, middle):
         for k in ks:
             peer = me.other(k)
-
-            @pl.when(me.middle() & (peer // 2 + z != 3))
-            def _(peer=peer):
+            if middle:
+
+                @pl.when(peer // 2 + z != 3)
+                def _(peer=peer):
+                    send_weights_to(e, peer)
+
+            else:
                 send_weights_to(e, peer)
 
     def send_weights_middle(e):
-        @pl.when(me.middle())
-        def _():
-            for j in range(2):
-                peer = 6 - 2 * z + j
-                send_weights_to(e, peer)
+        for j in range(2):
+            send_weights_to(e, 6 - 2 * z + j)
 
     def seven_blocks(sems):
         whole = r.w_moe.at[0 : 7 * TB, 0:TC]
         return remote(whole, whole, sems[0].at[0], sems[1].at[0], me.partner())
 
     g_small.start()
-    for copy in local[:3]:
+    for copy in local[1:3]:
         copy.wait()
-    for g in g_qkv:
-        g.start()
+    g_keys.start()
+    local[0].wait()
+    g_query.start()
     local[3].wait()
     g_wcol.start()
 
@@ -964,13 +974,16 @@
     for i in range(3):
         g_small.arrive(i)
         g_small.share(i)
-        for g in g_qkv:
-            g.arrive(i)
-            g.share(i)
-        if i == 1:
-            g_wcol.arrive(0)
-            g_wcol.share(0)
-    send_weights_middle(0)
+        g_keys.arrive(i)
+        g_keys.share(i)
+        if i > 0:
+            g_query.arrive(i - 1)
+            g_query.share(i - 1)
+
+    @pl.when(me.middle())
+    def _():
+        send_weights_middle(0)
+
     g_small.finish()
     for k in range(NBLK):
         piece = r.small[k]
@@ -982,38 +995,52 @@
         r.xn[chunk, :] = (v * r.r_one[chunk, :] * r.gains[0:1, :]).astype(BF16)
 
     row_chunks(normalize_one)
-    for g in g_qkv:
-        g.finish()
-    qkv = jnp.dot(r.xn[...], r.w_qkv[...], preferred_element_type=F32)
+    g_keys.finish()
+    key_value = jnp.dot(r.xn[...], r.w_qkv[:, TC:640], preferred_element_type=F32)
     base_c, base_s = r.rope_block[0, pl.ds(b, 1), :], r.rope_block[1, pl.ds(b, 1), :]
     row_c, row_s = r.rope_row[0], r.rope_row[1]
     first_half = lax.broadcasted_iota(jnp.int32, (TB, 128), 1) % 64 < 32
     cosine = base_c * row_c - base_s * row_s
     sine = base_s * row_c + base_c * row_s
     sine = jnp.where(first_half, -sine, sine)
-    key = qkv[:, 384:512]
+    key = key_value[:, 0:128]
     r.kv[rows(b), 0:128] = (key * cosine + swap_halves(key) * sine).astype(BF16)
-    r.kv[rows(b), 128:256] = qkv[:, 512:640].astype(BF16)
+    r.kv[rows(b), 128:256] = key_value[:, 128:256].astype(BF16)
     g_kv.start()
-    g_dmoe.start()
+    g_dmoe.send_own()
+    g_query.arrive(2)
+    g_query.share(2)
+    g_wcol.arrive(0)
+    g_wcol.share(0)
+    g_kv.relay()
+    g_query.finish()
+    query = jnp.dot(r.xn[...], r.w_qkv[:, 0:TC], preferred_element_type=F32)
     for pair in range(3):
-        u = qkv[:, 128 * pair : 128 * (pair + 1)]
+        u = query[:, 128 * pair : 128 * (pair + 1)]
         u = (u * cosine + swap_halves(u) * sine).astype(BF16).astype(F32)
         r.qz[2 * pair] = head_from_chunk(u, 2 * pair).astype(BF16)
         r.qz[2 * pair + 1] = head_from_chunk(u, 2 * pair + 1).astype(BF16)
     for h in range(NQ):
         r.oz[h] = jnp.zeros((TB, 128), F32)
         r.den[h] = jnp.zeros((TB, 128), F32)
-    g_kv.relay()
-    send_weights_middle(1)
-    for i in (1, 2):
-        g_wcol.arrive(i)
-        g_wcol.share(i)
-    g_dmoe.arrive(0)
-    g_dmoe.spread(0)
-    send_weights_inner(0, (1, 7, 2))
-    send_weights_end(0, (1, 7, 2, 6))
-
+
+    @pl.when(me.middle())
+    def _():
+        g_wcol.arrive(1)
+        g_wcol.share(1)
+        g_wcol.arrive(2)
+        g_wcol.share(2)
+        g_dmoe.arrive(0)
+        g_dmoe.spread(0, False)
+        send_weights_middle(1)
+        send_weights(0, (1, 7, 2), True)
+
+    @pl.when(end_chip)
+    def _():
+        send_weights(0, (1, 7, 2, 6), False)
+
+    g_dmoe.register()
+    g_dmoe.register_spread()
     g_kv.finish()
 
     first_block = FIRST_DOC_BLOCKS * (b // FIRST_DOC_BLOCKS)
@@ -1066,8 +1093,21 @@
         return to_plane(sems, lambda k: (own, own), buffer.at[:, 0 : 3 * TC], pend)
 
     wait_o = plane_gather(r.pl.o, r.o_full)
-    send_weights_inner(0, (6, 3))
-    send_weights_end(0, (3, 5))
+
+    @pl.when(me.middle())
+    def _():
+        send_weights(0, (6, 3), True)
+
+    @pl.when(end_chip)
+    def _():
+        g_wcol.arrive(1)
+        g_wcol.share(1)
+        g_wcol.arrive(2)
+        g_wcol.share(2)
+        g_dmoe.arrive(0)
+        g_dmoe.spread(0, False)
+        send_weights(0, (3, 5), False)
+
     g_wcol.finish()
     wait_o()
 
@@ -1096,21 +1136,29 @@
     combine = weight / jnp.sum(weight, axis=0, keepdims=True)
     r.comb[b, :, 0:TB] = combine
     g_comb.start()
+    g_dmoe.arrive(1)
+    g_dmoe.spread(1, False)
+    g_dmoe.arrive(2)
+    g_dmoe.spread(2, False)
     g_dmoe.relay(0)
-    for i in (1, 2):
-        g_dmoe.arrive(i)
-        g_dmoe.spread(i)
     for i in range(3):
         g_hn.arrive(i)
         g_hn.spread(i)
         g_comb.arrive(i)
         g_comb.share(i)
-    send_weights_end(0, (4,))
-    send_weights_end(1, (4, 3, 5, 2, 6, 1, 7))
-    send_weights_inner(0, (5, 4))
-    send_weights_inner(1, (4, 3, 5, 2, 6, 1, 7))
-    for i in (1, 2):
-        g_dmoe.relay(i)
+
+    @pl.when(me.middle())
+    def _():
+        send_weights(0, (5, 4), True)
+        send_weights(1, (4, 3, 5, 2, 6, 1, 7), True)
+
+    @pl.when(end_chip)
+    def _():
+        send_weights(0, (4,), False)
+        send_weights(1, (4, 3, 5, 2, 6, 1, 7), False)
+
+    g_dmoe.relay(1)
+    g_dmoe.relay(2)
     for i in range(3):
         g_hn.relay(i)
     for i in range(3):
@@ -1429,10 +1477,22 @@
 
     dc_all.wait_recv()
     wait_dc = to_plane(r.pl.dc, lambda k: (r.dc_in, r.dc_plane.at[k - 1]), r.dc_plane)
-    send_grads(1, (1, 7, 2))
+
+    @pl.when(me.middle())
+    def _():
+        send_grads(1, (1, 7, 2))
+
+    @pl.when(end_chip)
+    def _():
+        send_grads(1, (4, 3, 5, 2, 6, 1, 7))
+
     chain_h.total(r.acc.at[:, 0:TC])
     r.dhn[:, cols(t)] = r.acc[:, 0:TC].astype(BF16)
-    send_grads(1, (6, 3, 5))
+
+    @pl.when(me.middle())
+    def _():
+        send_grads(1, (6, 3, 5, 4))
+
     wait_dh = plane_gather(r.pl.dh, r.dhn)
     for j in range(4):
         core_sum(r.y, me.dest(j))
@@ -1639,7 +1699,7 @@
     lax.fori_loop(0, DM // 256, q_grads, 0)
     red_gq = Reduce(g_q_part, r.rd.gq)
     red_gq.start()
-    red_gq.steps()
+    red_gq.steps(end_chip)
     d_kv_acc = r.acc.at[:, 0:256]
     red_kv.down_total(d_kv_acc)
     d_kv = d_kv_acc[...].astype(BF16)
@@ -1662,18 +1722,33 @@
     lax.fori_loop(0, DM // 256, kv_grads, 0)
     red_gkv = Reduce(g_kv_part, r.rd.gkv)
     red_gkv.start()
-    red_gq.total(r.acc.at[:, 0:TC])
-    r.g_qkv_sum[:, 0:TC] = r.acc[:, 0:TC].astype(BF16)
-    for j in range(3):
-        red_gkv.step(j)
-    red_out.steps(me.middle())
-    send_grads(1, (4,))
+    red_gq.steps(me.middle())
+    red_gkv.steps(end_chip)
+    chain_y.steps(end_chip)
     wait_xs()
     total = r.dx[:, cols(t)].astype(F32)
     for k in range(3):
         total = total + r.dx_in[k].astype(F32)
     r.dxn[:, cols(t)] = total.astype(BF16)
     wait_dx = plane_gather(r.pl.xg, r.dxn)
+    own_qkv, from_qkv = [], []
+
+    def give(n, start, width, target, sems, three):
+        def lanes(index):
+            return pl.ds(pl.multiple_of(width * index, 128), width)
+
+        piece = r.g_qkv_sum.at[:, start : start + width]
+        there = target.at[:, lanes(t)]
+        own = pltpu.make_async_copy(piece, there, loc.at[1 + n])
+        own.start()
+        own_qkv.append(own)
+        from_qkv.append(to_plane(sems, lambda k: (piece, there), three))
+
+    red_gkv.steps(me.middle())
+    red_gq.total(r.acc.at[:, 0:TC])
+    r.g_qkv_sum[:, 0:TC] = r.acc[:, 0:TC].astype(BF16)
+    give(0, 0, TC, r.gq_out, r.pl.gq, r.dx_in)
+    red_out.steps(me.middle())
     wait_dx()
     r.flat[0:8, :] = jnp.zeros((8, DM), F32)
 
@@ -1688,20 +1763,6 @@
 
     row_chunks(norm_one_back)
     wait_sn = to_owners(r.sn, r.aa.sn, 8)
-    own_qkv, from_qkv = [], []
-
-    def give(n, start, width, target, sems, three):
-        def lanes(index):
-            return pl.ds(pl.multiple_of(width * index, 128), width)
-
-        piece = r.g_qkv_sum.at[:, start : start + width]
-        there = target.at[:, lanes(t)]
-        own = pltpu.make_async_copy(piece, there, loc.at[1 + n])
-        own.start()
-        own_qkv.append(own)
-        from_qkv.append(to_plane(sems, lambda k: (piece, there), three))
-
-    give(0, 0, TC, r.gq_out, r.pl.gq, r.dx_in)
     red_gkv.total(r.acc.at[:, 0:256])
     r.g_qkv_sum[:, TC:640] = r.acc[:, 0:256].astype(BF16)
     give(1, 384, 128, r.gk_out, r.pl.gk, r.g_qkv_sum.at[:, 0:TC])
@@ -1712,7 +1773,7 @@
     own_go.start()
     go_there = r.g_out_out.at[:, cols(t)]
     wait_go = to_plane(r.pl.go, lambda k: (r.g_out_sum, go_there), r.dx_in)
-    chain_y.steps()
+    chain_y.steps(me.middle())
     chain_y.total(r.acc.at[:, 0:TC])
     r.block_out[...] = r.hidden[:, cols(t)] + residual_scale * r.acc[:, 0:TC]
     r.sm_out[...] = wait_sm()
@@ -1841,11 +1902,11 @@
 
 
 def widen(*arrays):
-    steps = 4
-
-    def spec(shape):
-        rest = (0,) * (len(shape) - 1)
-        return pl.BlockSpec((shape[0] // steps, *shape[1:]), lambda i: (i, *rest))
+    steps = 2
+
+    def spec(array):
+        rest = (0,) * (array.ndim - 1)
+        return pl.BlockSpec((array.shape[0] // steps, *array.shape[1:]), lambda i: (i, *rest))
 
     def entry(*refs):
         count = len(arrays)
@@ -1860,7 +1921,7 @@
     def whole(*shape):
         return pl.BlockSpec(shape, lambda i: (0, 0))
 
-    specs = [spec(a.shape) for a in arrays[:-2]]
+    specs = [spec(a) for a in arrays[:-2]]
     return pl.pallas_call(
         entry,
         name="widen",

time: 242 us -> 229 us (0.946); the launches traced: 242 us -> 224 us
  Pallas kernels: 240 us -> 222 us
    pallas_call x1, Pallas kernels: 233 us -> 216 us  [fast_body(): pl.pallas_call(entry, name='layer', out_shape=[jax.ShapeDtypeStruct(shape...]
where the time goes in v5:
time: 229 us; the launch traced here: 224 us
  Pallas kernels  222 us (97%)
    pallas_call x1, Pallas kernels, fast_body(): pl.pallas_call(entry, name='layer', out_shape=[jax.ShapeDtypeStruct(shape...  216 us
    pallas_call x1, Pallas kernels, widen(): pl.pallas_call(entry, name='widen', grid=(steps,), in_specs=[*specs, whol...  5.87 us

profile of v5, /device:TPU:16, one launch (start us, length us, event | category | flops | bytes accessed | tf_op | source)
XLA Modules:
  0.0 224.3 jit_solution(6647257974437144399)
XLA Ops:
  0.6 1.3 add_bitcast_fusion.refs_4_
  2.0 216.3 %layer.1 = (f32[192,384]{1,0:T(8,128)}, f32[192,1536]{1,0:T(8,128)}, f32[24,256]{1,0:T(8,128)}, f32[8,256]{1,0:T(8,128)}, bf16[192,1536]{1,0:T(8,128)(2,1)}, /*i...) custom-call(bf16[192,1536]{1,0:T(8,128)(2,1)} %refs_0_.1, ...), custom_call_target="tpu_custom_call" | custom-call | tf_op jit(solution)/shard_map/layer/pallas_call | solution.py:1870
  218.2 5.9 %widen.1 = (f32[192,384]{1,0:T(8,128)}, f32[192,1536]{1,0:T(8,128)}, f32[192,1536]{1,0:T(8,128)}, f32[192,512]{1,0:T(8,128)}, f32[192,512]{1,0:T(8,128)}, /*inde...) custom-call(f32[192,384]{1,0:T(8,128)} %get-tuple-element.35.refs_0_, ...), custom_call_target="tpu_custom_call" | custom-call | flops 4000000 | bytes 16000000 | tf_op jit(solution)/shard_map/widen/pallas_call | solution.py:1925

commit v6 on v5

--- a/solution.py
+++ b/solution.py
@@ -1457,6 +1457,8 @@
     pend.later(dc_all)
     r.dc_in[b] = r.dc_own[b]
 
+    for i in range(3):
+        g_wout.cross(i)
 
     @pl.when(me.middle())
     def _():
@@ -1491,7 +1493,7 @@
 
     @pl.when(me.middle())
     def _():
-        send_grads(1, (6, 3, 5, 4))
+        send_grads(1, (6, 3))
 
     wait_dh = plane_gather(r.pl.dh, r.dhn)
     for j in range(4):
@@ -1551,8 +1553,6 @@
 
     wait_sm = to_owners(r.sm, r.aa.sm, 24)
 
-    for i in range(3):
-        g_wout.cross(i)
     g_wout.finish()
     d_o = contract(r.dproj[...], r.w_out[cols(t), :], 1, 1).astype(BF16).astype(F32)
     for h in range(NQ):
@@ -1691,6 +1691,11 @@
         ).astype(BF16)
     red_kv.down()
 
+    @pl.when(me.middle())
+    def _():
+        send_grads(1, (5, 4))
+
+
     def q_grads(n, carry):
         lanes = pl.ds(pl.multiple_of(n * 256, 256), 256)
         g_q_part[lanes, :] = contract(r.xn[:, lanes], r.dqkv[:, 0:TC], 0, 0).astype(BF16)

time: 229 us -> 229 us (level)
  no operation moved by 1% of the time
where the time goes in v6:
time: 229 us; the launch traced here: 224 us
  Pallas kernels  222 us (97%)
    pallas_call x1, Pallas kernels, fast_body(): pl.pallas_call(entry, name='layer', out_shape=[jax.ShapeDtypeStruct(shape...  216 us
    pallas_call x1, Pallas kernels, widen(): pl.pallas_call(entry, name='widen', grid=(steps,), in_specs=[*specs, whol...  5.87 us

profile of v6, /device:TPU:16, one launch (start us, length us, event | category | flops | bytes accessed | tf_op | source)
XLA Modules:
  0.0 224.2 jit_solution(7171277686381785104)
XLA Ops:
  0.6 1.3 add_bitcast_fusion.refs_4_
  2.0 216.2 %layer.1 = (f32[192,384]{1,0:T(8,128)}, f32[192,1536]{1,0:T(8,128)}, f32[24,256]{1,0:T(8,128)}, f32[8,256]{1,0:T(8,128)}, bf16[192,1536]{1,0:T(8,128)(2,1)}, /*i...) custom-call(bf16[192,1536]{1,0:T(8,128)(2,1)} %refs_0_.1, ...), custom_call_target="tpu_custom_call" | custom-call | tf_op jit(solution)/shard_map/layer/pallas_call | solution.py:1875
  218.2 5.9 %widen.1 = (f32[192,384]{1,0:T(8,128)}, f32[192,1536]{1,0:T(8,128)}, f32[192,1536]{1,0:T(8,128)}, f32[192,512]{1,0:T(8,128)}, f32[192,512]{1,0:T(8,128)}, /*inde...) custom-call(f32[192,384]{1,0:T(8,128)} %get-tuple-element.35.refs_0_, ...), custom_call_target="tpu_custom_call" | custom-call | flops 4000000 | bytes 16000000 | tf_op jit(solution)/shard_map/widen/pallas_call | solution.py:1930
